TPU v7x, 32 devices: a whole 2x2x4 slice. The times are simulated.
32 devices in a mesh: dp: 2 (over core), row: 4 (over y, x), col: 4 (over z).
Axes of the slice: x: 2, y: 2, z: 4, core: 2. Of those that a mesh axis runs over, the one named last changes fastest.
Arguments:
- tokens: bfloat16 [4, 768, 2048], P('dp', 'row', 'col'), may hold values from -6 to 6
- segments: int32 [4, 2048], P('dp'), may hold values from 0 to 5, never falling along the last dimension, each value on 1 to 800 neighbouring positions
- labels: int32 [4, 6], P('dp'), may hold values from 0 to 13
- cotangent: bfloat16 [4, 768, 2048], P('dp', 'row', 'col'), may hold values from -6 to 6
- w_qkv: bfloat16 [768, 2304], P('row', 'col'), may hold values from -0.21875 to 0.21875
- b_qkv: float32 [2, 768], P(None, 'col'), may hold values from -0.75 to 0.75
- w_out: bfloat16 [768, 768], P('col', 'row'), may hold values from -2.5 to 2.5
- b_out: float32 [768], P('row'), may hold values from -4 to 4
- ln1_gain: float32 [768], P('row'), may hold values from 0.5 to 1.5
- ln1_bias: float32 [768], P('row'), may hold values from -4 to 4
- w_in: bfloat16 [768, 3072], P('row', 'col'), may hold values from -0.21875 to 0.21875
- b_in: float32 [3072], P('col'), may hold values from -4 to 4
- w_back: bfloat16 [768, 3072], P('row', 'col'), may hold values from -0.109375 to 0.109375
- b_back: float32 [768], P('row'), may hold values from -4 to 4
- ln2_gain: float32 [768], P('row'), may hold values from 0.5 to 1.5
- ln2_bias: float32 [768], P('row'), may hold values from -4 to 4
- s_proj: bfloat16 [768, 128], P('row'), may hold values from -0.21875 to 0.21875
- s_bias: float32 [128], replicated, may hold values from -4 to 4
- s_query: float32 [128], replicated, may hold values from -4 to 4
- s_mid: float32 [128, 128], replicated, may hold values from -0.5 to 0.5
- s_mid_bias: float32 [128], replicated, may hold values from -4 to 4
- s_cls: float32 [128, 14], replicated, may hold values from -0.5 to 0.5
- s_cls_bias: float32 [14], replicated, may hold values from -6 to 6
Outputs:
- out: bfloat16 [4, 768, 2048], P('dp', 'row', 'col')
- logits: float32 [4, 6, 14], P('dp')
- tokens_grad: float32 [4, 768, 2048], P('dp', 'row', 'col')
- w_qkv_grad: float32 [768, 2304], P('row', 'col')
- b_qkv_grad: float32 [2, 768], P(None, 'col')
- w_out_grad: float32 [768, 768], P('col', 'row')
- b_out_grad: float32 [768], P('row')
- ln1_gain_grad: float32 [768], P('row')
- ln1_bias_grad: float32 [768], P('row')
- w_in_grad: float32 [768, 3072], P('row', 'col')
- b_in_grad: float32 [3072], P('col')
- w_back_grad: float32 [768, 3072], P('row', 'col')
- b_back_grad: float32 [768], P('row')
- ln2_gain_grad: float32 [768], P('row')
- ln2_bias_grad: float32 [768], P('row')
- s_proj_grad: float32 [768, 128], P('row')
- s_bias_grad: float32 [128], replicated
- s_query_grad: float32 [128], replicated
- s_mid_grad: float32 [128, 128], replicated
- s_mid_bias_grad: float32 [128], replicated
- s_cls_grad: float32 [128, 14], replicated
- s_cls_bias_grad: float32 [14], replicated
Inputs may be any that keep to these rules, and one draw needn't show every extreme that they name: `segments`: in each sequence the ids never fall, every id from 0 to 5 is present, every document has 1 to 800 tokens, and some document has exactly 800.
All inputs are finite; a program needn't handle non-finite values.
Results may differ from a plain program's by a relative error of at most 0.015.
Values may be sent and summed in bfloat16 or wider, within the bound.
A program may use at most 192 MiB of HBM per device.

v0:
```python
import functools
import jax
import jax.numpy as jnp
from jax import lax
from jax.experimental import pallas as pl
from jax.experimental.pallas import tpu as pltpu
from jax.sharding import PartitionSpec as P

HD = 64
SH = 2
SHD = 64

norm_eps = 1e-06
masked_value = -1e30
highest = lax.Precision.HIGHEST
f32 = jnp.float32
bf16 = jnp.bfloat16
WORLD = ("col", "row", "dp")


def sizes(seqs_local):
    parts = lax.axis_size("dp")
    rows = lax.axis_size("row")
    seqs = seqs_local * parts
    return parts, rows, lax.axis_size("col"), seqs, rows // seqs


def row_groups(rows, sub):
    return [list(range(at, at + sub)) for at in range(0, rows, sub)]


def take_in(values):
    parts, rows, _, seqs, sub = sizes(values.shape[0])
    held = lax.all_to_all(values, "dp", 2, 0, tiled=True)
    feats, half = held.shape[1:]
    held = held.reshape(seqs, feats, sub, half // sub).transpose(0, 2, 1, 3)
    held = held.reshape(rows, feats, half // sub)
    held = lax.all_to_all(held, "row", 0, 0, tiled=True)
    return held.reshape(rows * feats, half // sub)


def give_back(values, seqs_local):
    parts, rows, _, seqs, sub = sizes(seqs_local)
    width, own = values.shape
    feats = width // rows
    held = lax.all_to_all(values.reshape(rows, feats, own), "row", 0, 0, tiled=True)
    held = held.reshape(seqs, sub, feats, own).transpose(0, 2, 1, 3).reshape(seqs, feats, sub * own)
    return lax.all_to_all(held, "dp", 0, 2, tiled=True)


def gather_world(shard):
    cols, rows = lax.axis_size("col"), lax.axis_size("row")
    out = lax.all_gather(shard, WORLD, axis=0, tiled=True)
    return out.reshape(cols, rows, -1, shard.shape[1])


def own_half(block):
    parts = lax.axis_size("dp")
    amount = block.shape[0] // parts
    return lax.dynamic_slice_in_dim(block, lax.axis_index("dp") * amount, amount)


def scatter_world(full):
    flat = full.reshape(-1, full.shape[-1])
    mine = lax.psum_scatter(flat, WORLD, scatter_dimension=0, tiled=True)
    return lax.all_gather(mine, "dp", axis=0, tiled=True)


def swap_cols(values):
    return lax.all_to_all(values, "col", 0, 0, tiled=True)


def gather_sequence(values, sub):
    cols, own, width = values.shape
    held = values[:, None]
    if sub > 1:
        groups = row_groups(lax.axis_size("row"), sub)
        held = lax.all_gather(held, "row", axis=1, tiled=True, axis_index_groups=groups)
    held = lax.all_gather(held[:, None], "dp", axis=1, tiled=True)
    return held.reshape(-1, width)


def scatter_sequence(values, cols, sub):
    parts = lax.axis_size("dp")
    width = values.shape[-1]
    held = values.reshape(cols, parts, sub, -1, width)
    held = lax.psum_scatter(held, "dp", scatter_dimension=1, tiled=True)[:, 0]
    if sub > 1:
        groups = row_groups(lax.axis_size("row"), sub)
        held = lax.psum_scatter(
            held, "row", scatter_dimension=1, tiled=True, axis_index_groups=groups
        )
    return held[:, 0]


def normalize(values):
    mean_v = jnp.mean(values, axis=-1, keepdims=True)
    center = values - mean_v
    inv_std = lax.rsqrt(jnp.mean(center * center, axis=-1, keepdims=True) + norm_eps)
    return center * inv_std, inv_std


def normalize_back(grad_hat, normed, inv_std):
    return inv_std * (
        grad_hat
        - jnp.mean(grad_hat, axis=-1, keepdims=True)
        - normed * jnp.mean(grad_hat * normed, axis=-1, keepdims=True)
    )


def gelu_exact(values):
    return jax.nn.gelu(values, approximate=False)


def mm(a, b, contract):
    return lax.dot_general(a, b, (contract, ((), ())), preferred_element_type=f32)


def combine_pool(part_one, part_two):
    top_a, total_a, sum_a = part_one
    top_b, total_b, sum_b = part_two
    row_top = jnp.maximum(top_a, top_b)
    factor_a = jnp.exp(top_a - row_top)
    factor_b = jnp.exp(top_b - row_top)
    return (
        row_top,
        total_a * factor_a + total_b * factor_b,
        sum_a * factor_a[:, :, None] + sum_b * factor_b[:, :, None],
    )


def attend(q, k, v, q_seg, k_seg, scale):
    scores = jnp.einsum("qhd,khd->hqk", q, k, preferred_element_type=f32) * scale
    scores = jnp.where((q_seg[:, None] == k_seg[None, :])[None], scores, masked_value)
    top = jnp.max(scores, axis=-1, keepdims=True)
    exp_scores = jnp.exp(scores - top)
    total = jnp.sum(exp_scores, axis=-1, keepdims=True)
    probs = exp_scores / total
    context = jnp.einsum("hqk,khd->qhd", probs.astype(bf16), v, preferred_element_type=f32)
    return context.astype(bf16), probs


def attend_back(q, k, v, probs, d_ctx, scale):
    d_probs = jnp.einsum("qhd,khd->hqk", d_ctx, v, preferred_element_type=f32)
    delta = jnp.sum(probs * d_probs, axis=-1, keepdims=True)
    d_scores = (probs * (d_probs - delta)).astype(bf16)
    d_q = jnp.einsum("hqk,khd->qhd", d_scores, k, preferred_element_type=f32) * scale
    d_k = jnp.einsum("hqk,qhd->khd", d_scores, q, preferred_element_type=f32) * scale
    d_v = jnp.einsum("hqk,qhd->khd", probs.astype(bf16), d_ctx, preferred_element_type=f32)
    return d_q, d_k, d_v


def general_local(
    tokens,
    segments,
    labels,
    cotangent,
    w_qkv,
    b_qkv,
    w_out,
    b_out,
    ln1_gain,
    ln1_bias,
    w_in,
    b_in,
    w_back,
    b_back,
    ln2_gain,
    ln2_bias,
    s_proj,
    s_bias,
    s_query,
    s_mid,
    s_mid_bias,
    s_cls,
    s_cls_bias,
):
    seqs_local, width_row, cols_local = tokens.shape
    parts, rows, cols, seqs, sub = sizes(seqs_local)
    width = width_row * rows
    own = cols_local // (parts * sub)
    width_col = b_qkv.shape[1]
    heads_dev = width_col // HD
    hidden_col = b_in.shape[0]
    docs_count = labels.shape[1]
    class_count = s_cls.shape[1]
    student_width = s_proj.shape[1]
    row_index = lax.axis_index("row")
    col_index = lax.axis_index("col")
    dp_index = lax.axis_index("dp")
    seq_index = row_index // sub
    sub_index = row_index % sub
    score_scale = HD ** (-0.5)
    pool_scale = SHD ** (-0.5)
    query_heads = s_query.reshape(SH, SHD)
    doc_ids = jnp.arange(docs_count, dtype=jnp.int32)
    class_ids = jnp.arange(class_count, dtype=jnp.int32)

    w_qkv_all = gather_world(own_half(w_qkv)).reshape(cols, width, 3 * width_col)
    x_t = take_in(tokens)
    rest = jnp.concatenate([own_half(w_in), own_half(w_back), own_half(w_out).reshape(-1, width_col)], axis=1)
    rest_all = gather_world(rest)
    w_in_all = rest_all[..., :hidden_col].reshape(cols, width, hidden_col)
    w_back_all = rest_all[..., hidden_col : 2 * hidden_col].reshape(cols, width, hidden_col)
    w_out_all = rest_all[..., 2 * hidden_col :].reshape(cols, rows, width_col, width_row)
    w_out_all = w_out_all.transpose(0, 2, 1, 3).reshape(width, width)
    row_vectors = lax.all_gather(
        jnp.stack([b_out, ln1_gain, ln1_bias, b_back, ln2_gain, ln2_bias]), "row", axis=1, tiled=True
    )
    b_out_a, gain_one, bias_one, b_back_a, gain_two, bias_two = [row_vectors[i] for i in range(6)]
    b_qkv_all = lax.all_gather(b_qkv, "col")
    b_in_all = lax.all_gather(b_in, "col")
    s_proj_all = lax.all_gather(s_proj, "row", axis=0, tiled=True)
    whole_ints = lax.all_gather(jnp.concatenate([segments, labels], axis=1), "dp", axis=0, tiled=True)
    ints = lax.dynamic_index_in_dim(whole_ints, seq_index, 0, False)
    seq_len = segments.shape[1]
    seg_all, label_seq = ints[:seq_len], ints[seq_len:]
    seg_blocks = seg_all.reshape(cols, parts, sub, own)
    seg_q = lax.dynamic_index_in_dim(seg_blocks, dp_index, 1, False)
    seg_q = lax.dynamic_index_in_dim(seg_q, sub_index, 1, False)
    seg_own = lax.dynamic_index_in_dim(seg_q, col_index, 0, False)
    seg_q = seg_q.reshape(-1)

    x = x_t.T
    offsets = jnp.stack([b_qkv_all[:, 0], jnp.zeros_like(b_qkv_all[:, 0]), b_qkv_all[:, 1]], axis=1)
    offsets = offsets.reshape(cols, 3, heads_dev, HD).transpose(0, 2, 1, 3).reshape(cols, 1, -1)
    qkv = jnp.einsum("td,cdn->ctn", x, w_qkv_all, preferred_element_type=f32) + offsets
    qkv = swap_cols(qkv.astype(bf16)).reshape(cols, own, heads_dev, 3, HD)
    queries = qkv[:, :, :, 0].reshape(cols * own, heads_dev, HD)
    kv = gather_sequence(qkv[:, :, :, 1:].reshape(cols, own, -1), sub)
    kv = kv.reshape(seq_len, heads_dev, 2, HD)
    key_rows, value_rows = kv[:, :, 0], kv[:, :, 1]
    context, probs = attend(queries, key_rows, value_rows, seg_q, seg_all, score_scale)
    ctx = swap_cols(context.reshape(cols, own, width_col))
    ctx = ctx.transpose(1, 0, 2).reshape(own, width)

    attn_out = mm(ctx, w_out_all, ((1,), (0,))) + b_out_a
    normed_one, inv_one = normalize(x.astype(f32) + attn_out)
    hidden_one = normed_one * gain_one + bias_one
    hidden_low = hidden_one.astype(bf16)
    pre_act = jnp.einsum("td,cdn->ctn", hidden_low, w_in_all, preferred_element_type=f32)
    pre_act = pre_act + b_in_all[:, None, :]
    act = gelu_exact(pre_act).astype(bf16)
    ffn_out = jnp.einsum("ctn,cdn->td", act, w_back_all, preferred_element_type=f32) + b_back_a
    normed_two, inv_two = normalize(hidden_one + ffn_out)
    layer_out = (normed_two * gain_two + bias_two).astype(bf16)
    out = give_back(layer_out.T, seqs_local)

    student_h = mm(layer_out, s_proj_all, ((1,), (0,))) + s_bias
    head_parts = student_h.reshape(own, SH, SHD)
    pool_logit = jnp.sum(head_parts * query_heads, axis=-1) * pool_scale
    member = (seg_own[:, None] == doc_ids[None, :])[:, :, None]
    masked = jnp.where(member, pool_logit[:, None, :], masked_value)
    local_top = jnp.max(masked, axis=0)
    local_exp = jnp.where(member, jnp.exp(masked - local_top[None]), 0.0)
    local_total = jnp.sum(local_exp, axis=0)
    local_sum = jnp.einsum("tdh,thk->dhk", local_exp, head_parts, precision=highest)
    stats = jnp.concatenate([local_top[..., None], local_total[..., None], local_sum], axis=-1)
    stats = lax.all_gather(stats, ("dp", "col"))
    if sub > 1:
        stats = lax.all_gather(stats, "row", axis=0, tiled=True, axis_index_groups=row_groups(rows, sub))
    tops, totals, sums = stats[..., 0], stats[..., 1], stats[..., 2:]
    doc_top = jnp.max(tops, axis=0)
    factors = jnp.exp(tops - doc_top[None])
    doc_total = jnp.sum(totals * factors, axis=0)
    pooled_heads = jnp.sum(sums * factors[..., None], axis=0) / doc_total[:, :, None]
    pooled = pooled_heads.reshape(docs_count, student_width)
    middle = jnp.tanh(jnp.dot(pooled, s_mid, precision=highest) + s_mid_bias)
    logit_rows = jnp.dot(middle, s_cls, precision=highest) + s_cls_bias
    logits = lax.all_gather(logit_rows, "row")[::sub]
    logits = lax.dynamic_slice_in_dim(logits, dp_index * seqs_local, seqs_local)
    logit_top = jnp.max(logit_rows, axis=-1, keepdims=True)
    logit_exp = jnp.exp(logit_rows - logit_top)
    one_hot = (label_seq[:, None] == class_ids[None, :]).astype(f32)
    d_logits = logit_exp / jnp.sum(logit_exp, axis=-1, keepdims=True) - one_hot
    g_cls = jnp.dot(middle.T, d_logits, precision=highest)
    g_cls_bias = jnp.sum(d_logits, axis=0)
    d_middle = jnp.dot(d_logits, s_cls.T, precision=highest) * (1.0 - middle * middle)
    g_mid = jnp.dot(pooled.T, d_middle, precision=highest)
    g_mid_bias = jnp.sum(d_middle, axis=0)
    d_pooled = jnp.dot(d_middle, s_mid.T, precision=highest).reshape(docs_count, SH, SHD)
    shares = jnp.where(member, jnp.exp(masked - doc_top[None]), 0.0) / doc_total[None]
    d_share = jnp.einsum("dhk,thk->tdh", d_pooled, head_parts, precision=highest)
    base_term = jnp.sum(d_pooled * pooled_heads, axis=-1)
    d_pool_logit = jnp.sum(shares * (d_share - base_term[None]), axis=1)
    d_heads = jnp.einsum("tdh,dhk->thk", shares, d_pooled, precision=highest)
    d_heads = d_heads + d_pool_logit[:, :, None] * query_heads[None] * pool_scale
    g_query = (jnp.sum(d_pool_logit[:, :, None] * head_parts, axis=0) * pool_scale).reshape(-1)
    d_student = d_heads.reshape(own, student_width)
    g_sbias = jnp.sum(d_student, axis=0)
    g_sproj = jnp.dot(layer_out.astype(f32).T, d_student, precision=highest)

    d_out = take_in(cotangent).T.astype(f32)
    g_ln2_gain = jnp.sum(d_out * normed_two, axis=0)
    g_ln2_bias = jnp.sum(d_out, axis=0)
    d_resid_two = normalize_back(d_out * gain_two, normed_two, inv_two)
    d_ffn = d_resid_two.astype(bf16)
    g_back_bias = jnp.sum(d_ffn.astype(f32), axis=0)
    g_back = jnp.einsum("td,ctn->cdn", d_ffn, act, preferred_element_type=f32)
    d_act = jnp.einsum("td,cdn->ctn", d_ffn, w_back_all, preferred_element_type=f32)
    _, gelu_fn = jax.vjp(gelu_exact, pre_act)
    d_pre = gelu_fn(d_act)[0].astype(bf16)
    g_in_bias = jnp.sum(d_pre.astype(f32), axis=1)
    g_in = jnp.einsum("td,ctn->cdn", hidden_low, d_pre, preferred_element_type=f32)
    d_hidden_one = d_resid_two + jnp.einsum(
        "ctn,cdn->td", d_pre, w_in_all, preferred_element_type=f32
    )
    g_ln1_gain = jnp.sum(d_hidden_one * normed_one, axis=0)
    g_ln1_bias = jnp.sum(d_hidden_one, axis=0)
    d_resid_one = normalize_back(d_hidden_one * gain_one, normed_one, inv_one)
    d_attn = d_resid_one.astype(bf16)
    g_out_bias = jnp.sum(d_attn.astype(f32), axis=0)
    g_out = mm(ctx, d_attn, ((0,), (0,)))
    d_ctx = mm(d_attn, w_out_all, ((1,), (1,))).astype(bf16)
    d_ctx = swap_cols(d_ctx.reshape(own, cols, width_col).transpose(1, 0, 2))
    d_ctx = d_ctx.reshape(cols * own, heads_dev, HD)
    d_q, d_k, d_v = attend_back(queries, key_rows, value_rows, probs, d_ctx, score_scale)
    d_kv = jnp.stack([d_k, d_v], axis=2).astype(bf16).reshape(seq_len, -1)
    d_kv = scatter_sequence(d_kv, cols, sub).reshape(cols, own, heads_dev, 2, HD)
    d_q = d_q.astype(bf16).reshape(cols, own, heads_dev, 1, HD)
    d_qkv = jnp.concatenate([d_q, d_kv], axis=3).reshape(cols, own, 3 * width_col)
    d_qkv = swap_cols(d_qkv)
    g_qkv_bias = jnp.sum(d_qkv.astype(f32), axis=1).reshape(cols, heads_dev, 3, HD)
    g_qkv = jnp.einsum("td,ctn->cdn", x, d_qkv, preferred_element_type=f32)
    d_tokens = d_resid_one + jnp.einsum("ctn,cdn->td", d_qkv, w_qkv_all, preferred_element_type=f32)
    grad_tokens = give_back(d_tokens.astype(bf16).T, seqs_local).astype(f32)

    g_out = g_out.reshape(cols, width_col, rows, width_row).transpose(0, 2, 1, 3)
    g_out = g_out.reshape(cols, rows, width_row, width_col)
    model = jnp.concatenate(
        [
            g_in.reshape(cols, rows, width_row, hidden_col).astype(bf16),
            g_back.reshape(cols, rows, width_row, hidden_col).astype(bf16),
            g_out.astype(bf16),
        ],
        axis=-1,
    )
    model = scatter_world(model).astype(f32)
    g_qkv = scatter_world(g_qkv.reshape(cols, rows, width_row, 3 * width_col).astype(bf16)).astype(f32)
    once = 1.0 / (parts * cols * sub)
    small = (
        g_qkv_bias[:, :, 0].reshape(cols, width_col),
        g_qkv_bias[:, :, 2].reshape(cols, width_col),
        g_in_bias,
        g_out_bias,
        g_ln1_gain,
        g_ln1_bias,
        g_back_bias,
        g_ln2_gain,
        g_ln2_bias,
        g_sproj,
        g_sbias,
        g_query,
        g_mid * once,
        g_mid_bias * once,
        g_cls * once,
        g_cls_bias * once,
    )
    small = lax.psum(small, WORLD)

    def at_col(part):
        return lax.dynamic_index_in_dim(part, col_index, 0, False)

    def at_row(part):
        return lax.dynamic_slice_in_dim(part, row_index * width_row, width_row)

    return (
        out,
        logits,
        grad_tokens,
        g_qkv,
        jnp.stack([at_col(small[0]), at_col(small[1])]),
        model[:, 2 * hidden_col :].reshape(width_col, width_row),
        at_row(small[3]),
        at_row(small[4]),
        at_row(small[5]),
        model[:, :hidden_col],
        at_col(small[2]),
        model[:, hidden_col : 2 * hidden_col],
        at_row(small[6]),
        at_row(small[7]),
        at_row(small[8]),
        at_row(small[9]),
        small[10],
        small[11],
        small[12],
        small[13],
        small[14],
        small[15],
    )


MESH = pl.DeviceIdType.MESH
HBM = pl.BlockSpec(memory_space=pl.ANY)


def place():
    return lax.axis_index("dp"), lax.axis_index("row"), lax.axis_index("col")


def greet(peers, guarded=()):
    barrier = pltpu.get_barrier_semaphore()
    for peer in peers:
        pl.semaphore_signal(barrier, inc=1, device_id=peer, device_id_type=MESH)
    for there, peer in guarded:

        @pl.when(there)
        def _():
            pl.semaphore_signal(barrier, inc=1, device_id=peer, device_id_type=MESH)

    amount = len(peers)
    for there, _ in guarded:
        amount = amount + there.astype(jnp.int32)
    pl.semaphore_wait(barrier, amount)


def rcopy(src, dst, send, recv, peer):
    return pltpu.make_async_remote_copy(
        src_ref=src, dst_ref=dst, send_sem=send, recv_sem=recv, device_id=peer, device_id_type=MESH
    )


def take_copies(src, out, local, send, recv):
    d, r, c = place()
    own = out.shape[2]
    moves = []
    for i in range(2):
        for far in range(2):
            row, core = 2 * d + i, d ^ far
            piece = src.at[i, :, pl.ds(pl.multiple_of(core * own, own), own)]
            here = (row == r) if far == 0 else None

            def start(piece=piece, row=row, core=core, slot=2 * i + far, here=here):
                def away():
                    rcopy(piece, out.at[r], send.at[slot], recv.at[r], (core, row, c)).start()

                if here is None:
                    away()
                else:
                    pl.when(jnp.logical_not(here))(away)

                    @pl.when(here)
                    def _():
                        pltpu.make_async_copy(piece, out.at[r], local).start()

            def wait(piece=piece, row=row, core=core, slot=2 * i + far, here=here):
                def away():
                    rcopy(piece, out.at[r], send.at[slot], recv.at[r], (core, row, c)).wait_send()

                if here is None:
                    away()
                else:
                    pl.when(jnp.logical_not(here))(away)

                    @pl.when(here)
                    def _():
                        pltpu.make_async_copy(piece, out.at[r], local).wait()

            moves.append((start, wait))
    for row in range(4):

        def arrive(row=row):
            @pl.when(jnp.logical_not((row == r) & (r // 2 == d)))
            def _():
                piece = src.at[0, :, pl.ds(0, own)]
                rcopy(piece, out.at[row], send.at[0], recv.at[row], (d, r, c)).wait_recv()

        moves.append((lambda: None, arrive))
    return moves


def gather_kernel(kinds, *refs):
    shards, refs = refs[:kinds], refs[kinds:]
    (tok, ints), refs = refs[:2], refs[2:]
    outs, refs = refs[:kinds], refs[kinds:]
    (tok_out, ints_out, q_out, kv_out, wo_out), refs = refs[:5], refs[5:]
    (x_nat, q_src, kv_src), refs = refs[:3], refs[3:]
    own_sem, zs, zr, xs, xr, ys, yr, cs, cr, ps, pr, tl, ts, tr, il, hs, hr, hps, hpr = refs
    d, r, c = place()
    cols = 4
    xn, yn, pn = (d, r ^ 1, c), (d, r ^ 2, c), (1 - d, r, c)
    up, down = (d, r, c + 1), (d, r, c - 1)
    has_up, has_down = c < cols - 1, c > 0
    greet(plane_peers() + [(d, r, c ^ j) for j in (1, 2, 3)])
    moves = take_copies(tok, tok_out, tl, ts, tr)
    for start, _ in moves:
        start()
    pltpu.make_async_copy(ints, ints_out.at[d], il.at[0]).start()
    rcopy(ints, ints_out.at[d], il.at[1], il.at[2], pn).start()
    halves = [shard.shape[0] // 2 for shard in shards]

    def z_send(k, at, way, hop):
        src = shards[k] if hop == 1 else outs[k].at[at, r, d]
        return rcopy(
            src, outs[k].at[at, r, d], zs.at[k, way, hop - 1], zr.at[k, way, hop - 1], up if way == 0 else down
        )

    def src_of(k, at, own):
        return shards[k] if own else outs[k].at[at, r, d]

    def to_x(k, at, own):
        return rcopy(src_of(k, at, own), outs[k].at[at, r, d], xs.at[k, at], xr.at[k, at], xn)

    def to_y(k, at, own):
        return rcopy(src_of(k, at, own), outs[k].at[at, r, d], ys.at[k, at], yr.at[k, at], yn)

    def to_p(k, at, own):
        return rcopy(src_of(k, at, own), outs[k].at[at, r, d], ps.at[k, at, 0], pr.at[k, at, 0], pn)

    def relay(k, at, which):
        row = r ^ 1 if which == 0 else r ^ 2
        ref = outs[k].at[at, row, d, pl.ds(which * halves[k], halves[k])]
        return rcopy(ref, ref, cs.at[k, at, which], cr.at[k, at, which], yn if which == 0 else xn)

    def pass_p(k, at, bit):
        ref = outs[k].at[at, r ^ bit, d]
        return rcopy(ref, ref, ps.at[k, at, bit], pr.at[k, at, bit], pn)

    def got_x(k, at):
        ref = outs[k].at[at, r ^ 1, d]
        rcopy(ref, ref, xs.at[k, at], xr.at[k, at], xn).wait_recv()

    def got_y(k, at):
        ref = outs[k].at[at, r ^ 2, d]
        rcopy(ref, ref, ys.at[k, at], yr.at[k, at], yn).wait_recv()

    def got_corner(k, at):
        for which in range(2):
            ref = outs[k].at[at, r ^ 3, d, pl.ds(which * halves[k], halves[k])]
            rcopy(ref, ref, cs.at[k, at, which], cr.at[k, at, which], xn).wait_recv()

    def got_p(k, at, bit):
        ref = outs[k].at[at, r ^ bit, 1 - d]
        rcopy(ref, ref, ps.at[k, at, bit], pr.at[k, at, bit], pn).wait_recv()

    for k in range(kinds):
        pltpu.make_async_copy(shards[k], outs[k].at[c, r, d], own_sem.at[k]).start()

        @pl.when(has_up)
        def _():
            z_send(k, c, 0, 1).start()

        @pl.when(has_down)
        def _():
            z_send(k, c, 1, 1).start()

    def spread(k, at, own):
        to_x(k, at, own).start()
        to_y(k, at, own).start()
        to_p(k, at, own).start()

    def onward(k, at):
        got_x(k, at)
        relay(k, at, 0).start()
        pass_p(k, at, 1).start()
        got_y(k, at)
        relay(k, at, 1).start()
        pass_p(k, at, 2).start()

    steps = [(0, 0)] + [(way, hop) for hop in (1, 2, 3) for way in (0, 1)]
    jobs = [(k, way, hop) for k in range(kinds) for way, hop in steps]

    def at_of(way, hop):
        return c - hop if way == 0 else c + hop

    def valid(way, hop):
        return c >= hop if way == 0 else c + hop < cols

    def guard(way, hop, body):
        if hop == 0:
            body()
        else:
            pl.when(valid(way, hop))(body)

    def first(k, way, hop):
        def body():
            at = at_of(way, hop)
            if hop:
                z_send(k, at, way, hop).wait_recv()
                if hop < 3:
                    can = has_up if way == 0 else has_down

                    @pl.when(can)
                    def _():
                        z_send(k, at, way, hop + 1).start()

            spread(k, at, hop == 0)

        guard(way, hop, body)

    def second(k, way, hop):
        guard(way, hop, lambda: onward(k, at_of(way, hop)))

    def third(k, way, hop):
        def body():
            at = at_of(way, hop)
            got_corner(k, at)
            pass_p(k, at, 3).start()

        guard(way, hop, body)

    def settle(k):
        pltpu.make_async_copy(shards[k], outs[k].at[c, r, d], own_sem.at[k]).wait()
        for way, hop in steps:

            def body():
                for bit in range(4):
                    got_p(k, at_of(way, hop), bit)

            guard(way, hop, body)

    def kv(j):
        return rcopy(kv_src.at[c ^ j], kv_out.at[c, d], hs.at[0, j], hr.at[0, j], (d, r, c ^ j))

    def q(j):
        return rcopy(q_src.at[c ^ j], q_out.at[c], hs.at[1, j], hr.at[1, j], (d, r, c ^ j))

    def pair(j):
        src = kv_src.at[c] if j == 0 else kv_out.at[c ^ j, d]
        return rcopy(src, kv_out.at[c ^ j, d], hps.at[j], hpr.at[j], pn)

    deep = kv_src.shape[1]
    out_cols = deep + q_src.shape[1]
    lanes = -(-out_cols // 128) * 128

    def prepare():
        for _, wait in moves:
            wait()
        feats = tok_out.shape[1]
        x_nat[...] = tok_out[...].reshape(4 * feats, -1).astype(f32).T.astype(bf16)

    def project(j):
        to = c ^ j
        weights = outs[0][to, :, :, :, :lanes].reshape(-1, lanes)
        bias = outs[1][to, r, 0, pl.ds(0, 8)]
        bias = jnp.concatenate([bias[i : i + 1] for i in range(lanes // 128)], axis=1)
        made = jnp.dot(x_nat[...], weights, preferred_element_type=f32) + bias
        made = made.T.astype(bf16)
        kv_src[to] = made[:deep]
        q_src[to] = made[deep:out_cols]
        if j:
            kv(j).start()
            q(j).start()
        else:
            pair(0).start()
            kv_out[c, d] = kv_src[c]
            q_out[c] = q_src[c]

    def spread_out(at):
        feats = tok_out.shape[1]
        for row in range(4):
            block = outs[0][at, row, :, :, out_cols:].reshape(-1, feats)
            wo_out[pl.ds(at * wide, wide), row * feats : (row + 1) * feats] = block

    wide = q_src.shape[1]
    lag = 3
    ready = 2 * len(steps) + 2 * lag
    for i in range(len(jobs) + 2 * lag):
        if i == ready:
            prepare()
            settle(0)
            settle(1)
        if ready <= i < ready + 4:
            project((3, 2, 1, 0)[i - ready])
        if ready + 4 <= i < ready + 8:
            spread_out(i - ready - 4)
        if i < len(jobs):
            first(*jobs[i])
        if 0 <= i - lag < len(jobs):
            second(*jobs[i - lag])
        if 0 <= i - 2 * lag < len(jobs):
            third(*jobs[i - 2 * lag])

    for j in (1, 2, 3):
        kv(j).wait_recv()
        pair(j).start()
    for k in range(kinds):
        if k > 1:
            settle(k)
        for way, hop in steps:

            def body():
                at = at_of(way, hop)
                own = hop == 0
                to_x(k, at, own).wait_send()
                to_y(k, at, own).wait_send()
                to_p(k, at, own).wait_send()
                for which in range(2):
                    relay(k, at, which).wait_send()
                for bit in (1, 2, 3):
                    pass_p(k, at, bit).wait_send()
                if hop < 3:
                    if own:

                        @pl.when(has_up)
                        def _():
                            z_send(k, c, 0, 1).wait_send()

                        @pl.when(has_down)
                        def _():
                            z_send(k, c, 1, 1).wait_send()
                    else:
                        can = has_up if way == 0 else has_down

                        @pl.when(can)
                        def _():
                            z_send(k, at, way, hop + 1).wait_send()

            guard(way, hop, body)
    for j in (1, 2, 3):
        q(j).wait()
        kv(j).wait_send()
    for j in range(4):
        pair(j).wait()
    pltpu.make_async_copy(ints, ints_out.at[d], il.at[0]).wait()
    rcopy(ints, ints_out.at[1 - d], il.at[1], il.at[2], pn).wait()


VM = pl.BlockSpec(memory_space=pltpu.VMEM)


def gather_fast(shards, tokens, ints, wide, cid):
    kinds = len(shards)
    dma = pltpu.SemaphoreType.DMA
    _, feats, cols = tokens.shape
    own = cols // 2
    piece = jax.ShapeDtypeStruct((4, wide, own), bf16)
    return pl.pallas_call(
        functools.partial(gather_kernel, kinds),
        out_shape=[jax.ShapeDtypeStruct((4, 4, 2) + s.shape, s.dtype) for s in shards]
        + [
            jax.ShapeDtypeStruct((4, feats, own), tokens.dtype),
            jax.ShapeDtypeStruct((2,) + ints.shape, ints.dtype),
            piece,
            jax.ShapeDtypeStruct((4, 2, 2 * wide, own), bf16),
            jax.ShapeDtypeStruct((4 * wide, 4 * feats), bf16),
        ],
        in_specs=[HBM] * (kinds + 2),
        out_specs=[VM, VM] + [HBM] * (kinds - 2) + [VM, HBM, VM, VM, VM],
        scratch_shapes=[
            pltpu.VMEM((own, 4 * feats), bf16),
            pltpu.VMEM((4, wide, own), bf16),
            pltpu.VMEM((4, 2 * wide, own), bf16),
            dma((kinds,)),
            dma((kinds, 2, 3)), dma((kinds, 2, 3)),
            dma((kinds, 4)), dma((kinds, 4)),
            dma((kinds, 4)), dma((kinds, 4)),
            dma((kinds, 4, 2)), dma((kinds, 4, 2)),
            dma((kinds, 4, 4)), dma((kinds, 4, 4)),
            dma, dma((4,)), dma((4,)), dma((3,)),
            dma((2, 4)), dma((2, 4)), dma((4,)), dma((4,)),
        ],
        compiler_params=pltpu.CompilerParams(
            collective_id=cid, has_side_effects=True, vmem_limit_bytes=40 * 1024 * 1024
        ),
        name="head",
    )(*shards, tokens, ints)


def scatter_core(grads, outs, scratch, begin, during, late=0):
    kinds = len(grads)
    (acc, precv, xr1, yr1, xr2, yr2, zup, zdn, fin) = scratch[:9]
    (ls, ps, pr, xs1, xm1, ys1, ym1, xs2, xm2, ys2, ym2, us, um, ds, dm, fs, fm, os) = scratch[9:]
    d, r, c = place()
    cols = 4
    chunks = kinds * cols
    xn, yn, pn = (d, r ^ 1, c), (d, r ^ 2, c), (1 - d, r, c)
    up, down = (d, r, c + 1), (d, r, c - 1)
    half = acc.shape[2] // 2
    first, last = pl.ds(0, half), pl.ds(half, half)

    def split(i):
        k = i // cols
        j = i - k * cols
        at = jnp.where(j == 0, 0, jnp.where(j == 1, 3, j - 1))
        return k, at

    def at_static(i):
        return i // cols, (0, 3, 1, 2)[i % cols]

    def load(i):
        k, at = at_static(i)
        return pltpu.make_async_copy(grads[k].at[at, :, d], acc.at[i], ls.at[i])

    def pair(i):
        k, at = at_static(i)
        return rcopy(grads[k].at[at, :, 1 - d], precv.at[i], ps.at[i], pr.at[i], pn)

    def launch(i):
        pair(i).start()
        load(i).start()

    for i in range((kinds - late) * cols):
        launch(i)
    begin()

    def x1(i, j):
        return rcopy(acc.at[i, r ^ 1 ^ (2 * j), first], xr1.at[i, j], xs1.at[i, j], xm1.at[i, j], xn)

    def y1(i, j):
        return rcopy(acc.at[i, r ^ 2 ^ j, last], yr1.at[i, j], ys1.at[i, j], ym1.at[i, j], yn)

    def y2(i):
        return rcopy(acc.at[i, r ^ 2, first], yr2.at[i], ys2.at[i], ym2.at[i], yn)

    def x2(i):
        return rcopy(acc.at[i, r ^ 1, last], xr2.at[i], xs2.at[i], xm2.at[i], xn)

    def to_up(i):
        return rcopy(acc.at[i, r], zup.at[i], us.at[i], um.at[i], up)

    def to_down(i):
        return rcopy(acc.at[i, r], zdn.at[i], ds.at[i], dm.at[i], down)

    def stage1(i):
        pltpu.make_async_copy(precv.at[i], acc.at[i], ls.at[i]).wait()
        rcopy(acc.at[i], precv.at[i], ps.at[i], pr.at[i], pn).wait_recv()

        @pl.loop(0, 4)
        def _(row):
            acc[i, row] = acc[i, row] + precv[i, row]

        x1(i, 1).start()
        y1(i, 1).start()
        x1(i, 0).start()
        y1(i, 0).start()

    def stage2(i):
        x1(i, 1).wait_recv()
        acc[i, r ^ 2, first] = acc[i, r ^ 2, first] + xr1[i, 1]
        y2(i).start()
        y1(i, 1).wait_recv()
        acc[i, r ^ 1, last] = acc[i, r ^ 1, last] + yr1[i, 1]
        x2(i).start()
        x1(i, 0).wait_recv()
        acc[i, r, first] = acc[i, r, first] + xr1[i, 0]
        y1(i, 0).wait_recv()
        acc[i, r, last] = acc[i, r, last] + yr1[i, 0]

    def stage3(i):
        y2(i).wait_recv()
        acc[i, r, first] = acc[i, r, first] + yr2[i]
        x2(i).wait_recv()
        acc[i, r, last] = acc[i, r, last] + xr2[i]

    def stage4(i, hops):
        k, at = split(i)

        @pl.when((at > c) & (c == hops))
        def _():
            @pl.when(c > 0)
            def _():
                to_up(i).wait_recv()
                acc[i, r] = acc[i, r] + zup[i]

            to_up(i).start()

        @pl.when((at < c) & (cols - 1 - c == hops))
        def _():
            @pl.when(c < cols - 1)
            def _():
                to_down(i).wait_recv()
                acc[i, r] = acc[i, r] + zdn[i]

            to_down(i).start()

        @pl.when((at == c) & (jnp.maximum(c, cols - 1 - c) == hops))
        def _():
            @pl.when(c > 0)
            def _():
                to_up(i).wait_recv()
                acc[i, r] = acc[i, r] + zup[i]

            @pl.when(c < cols - 1)
            def _():
                to_down(i).wait_recv()
                acc[i, r] = acc[i, r] + zdn[i]

            fin[k, d] = acc[i, r]
            rcopy(fin.at[k, d], fin.at[k, d], fs.at[k], fm.at[k], pn).start()

    stages = [(0, stage1), (2, stage2), (4, stage3)]
    stages += [(5 + h, functools.partial(lambda h, i: stage4(i, h), h)) for h in range(cols)]
    ending = stages[-1][0]

    assert len(during) <= chunks + ending

    @pl.loop(0, chunks + ending)
    def _(step):
        for i, extra in enumerate(during):
            pl.when(step == i)(functools.partial(extra, launch))

        for lag, stage in stages:

            @pl.when((step >= lag) & (step - lag < chunks))
            def _():
                stage(step - lag)

    @pl.loop(0, chunks)
    def _(i):
        k, at = split(i)
        rcopy(acc.at[i], precv.at[i], ps.at[i], pr.at[i], pn).wait_send()
        for j in range(2):
            x1(i, j).wait_send()
            y1(i, j).wait_send()
        y2(i).wait_send()
        x2(i).wait_send()

        @pl.when(at > c)
        def _():
            to_up(i).wait_send()

        @pl.when(at < c)
        def _():
            to_down(i).wait_send()

    for k in range(kinds):
        rcopy(fin.at[k, 1 - d], fin.at[k, 1 - d], fs.at[k], fm.at[k], pn).wait()
        pltpu.make_async_copy(fin.at[k], outs[k], os.at[k]).start()
    for k in range(kinds):
        pltpu.make_async_copy(fin.at[k], outs[k], os.at[k]).wait()

def scatter_scratch(kinds, n, w, dt):
    dma = pltpu.SemaphoreType.DMA
    chunks = kinds * 4
    return [
        pltpu.VMEM((chunks, 4, n, w), dt),
        pltpu.VMEM((chunks, 4, n, w), dt),
        pltpu.VMEM((chunks, 2, n // 2, w), dt),
        pltpu.VMEM((chunks, 2, n // 2, w), dt),
        pltpu.VMEM((chunks, n // 2, w), dt),
        pltpu.VMEM((chunks, n // 2, w), dt),
        pltpu.VMEM((chunks, n, w), dt),
        pltpu.VMEM((chunks, n, w), dt),
        pltpu.VMEM((kinds, 2, n, w), dt),
        dma((chunks,)), dma((chunks,)), dma((chunks,)),
        dma((chunks, 2)), dma((chunks, 2)), dma((chunks, 2)), dma((chunks, 2)),
        dma((chunks,)), dma((chunks,)), dma((chunks,)), dma((chunks,)),
        dma((chunks,)), dma((chunks,)), dma((chunks,)), dma((chunks,)),
        dma((kinds,)), dma((kinds,)), dma((kinds,)),
    ]


def give_moves(src_ref, out_ref, local, send, recv):
    d, r, c = place()
    own = src_ref.shape[2]
    home = r // 2

    def slot(i, core):
        return out_ref.at[i, :, pl.ds(pl.multiple_of(core * own, own), own)]

    def move(row):
        return rcopy(src_ref.at[row], slot(r % 2, d), send.at[row], recv.at[r % 2, d], (home, row, c))

    def stay():
        return pltpu.make_async_copy(src_ref.at[r], slot(r % 2, d), local)

    def start():
        for row in range(4):

            @pl.when(jnp.logical_not((row == r) & (home == d)))
            def _():
                move(row).start()

        @pl.when(home == d)
        def _():
            stay().start()

    def finish():
        for row in range(4):

            @pl.when(jnp.logical_not((row == r) & (home == d)))
            def _():
                move(row).wait_send()

        @pl.when(home == d)
        def _():
            stay().wait()

        for i in range(2):
            for core in range(2):

                @pl.when(jnp.logical_not((2 * d + i == r) & (core == d)))
                def _():
                    rcopy(src_ref.at[0], slot(i, core), send.at[0], recv.at[i, core], (d, r, c)).wait_recv()

    return start, finish


def plane_peers():
    d, r, c = place()
    return [(d ^ (j // 4), r ^ (j % 4), c) for j in range(1, 8)]


def line_peers():
    d, r, c = place()
    return [(d ^ (j // 4), r, c ^ (j % 4)) for j in range(1, 8)]


def swap_kernel(src, cot, out, cot_out, send, recv, tl, ts, tr):
    d, r, c = place()
    greet(plane_peers() + [(d, r, c ^ j) for j in (1, 2, 3)])

    def move(j):
        return rcopy(src.at[c ^ j], out.at[c], send.at[j], recv.at[j], (d, r, c ^ j))

    for j in (3, 2, 1):
        move(j).start()
    moves = take_copies(cot, cot_out, tl, ts, tr)
    for start, _ in moves:
        start()
    out[c] = src[c]
    for j in (1, 2, 3):
        move(j).wait()
    for _, wait in moves:
        wait()


def swap_fast(values, cotangent, cid):
    dma = pltpu.SemaphoreType.DMA
    _, feats, cols = cotangent.shape
    return pl.pallas_call(
        swap_kernel,
        out_shape=[
            jax.ShapeDtypeStruct(values.shape, values.dtype),
            jax.ShapeDtypeStruct((4, feats, cols // 2), cotangent.dtype),
        ],
        in_specs=[VM, HBM],
        out_specs=[VM, VM],
        scratch_shapes=[dma((4,)), dma((4,)), dma, dma((4,)), dma((4,))],
        compiler_params=pltpu.CompilerParams(collective_id=cid, has_side_effects=True),
        name="swap",
    )(values, cotangent)


def turn_kernel(ctx_ref, stats_ref, give_ref, ctx_out, stats_out, give_out, send, recv, ssend, srecv, gl, gs, gr):
    d, r, c = place()
    peers = line_peers()
    greet(plane_peers() + peers[:3] + peers[4:])

    def move(j):
        return rcopy(ctx_ref.at[c ^ j], ctx_out.at[c], send.at[j], recv.at[j], (d, r, c ^ j))

    def tell(j):
        return rcopy(stats_ref, stats_out.at[d, c], ssend.at[j - 1], srecv.at[j - 1], peers[j - 1])

    for j in range(1, 8):
        tell(j).start()
    for j in (3, 2, 1):
        move(j).start()
    start, finish = give_moves(give_ref, give_out, gl, gs, gr)
    start()
    ctx_out[c] = ctx_ref[c]
    stats_out[d, c] = stats_ref[...]
    for j in range(1, 8):
        tell(j).wait()
    for j in (1, 2, 3):
        move(j).wait()
    finish()


def turn_fast(d_ctx, stats, out_t, cid):
    width, own = out_t.shape
    dma = pltpu.SemaphoreType.DMA
    return pl.pallas_call(
        turn_kernel,
        out_shape=[
            jax.ShapeDtypeStruct(d_ctx.shape, d_ctx.dtype),
            jax.ShapeDtypeStruct((2, 4) + stats.shape, stats.dtype),
            jax.ShapeDtypeStruct((2, width // 4, 2 * own), out_t.dtype),
        ],
        in_specs=[VM, VM, HBM],
        out_specs=[VM, VM, HBM],
        scratch_shapes=[dma((4,)), dma((4,)), dma((7,)), dma((7,)), dma, dma((4,)), dma((2, 2))],
        compiler_params=pltpu.CompilerParams(collective_id=cid, has_side_effects=True),
        name="turn",
    )(d_ctx, stats, out_t.reshape(4, width // 4, own))


def sum_steps(src, total, parts, sems):
    d, r, c = place()
    peers = [(1 - d, r, c), (d, r ^ 1, c), (d, r ^ 2, c), (d, r, c ^ 1), (d, r, c ^ 2)]
    bits = [d, r % 2, r // 2, c % 2, c // 2]
    rs, rr, gs, gr = sems
    count = len(peers)
    size = [src.shape[0] >> (i + 1) for i in range(count)]
    offset = [jnp.int32(0)]
    for i in range(count):
        offset.append(offset[i] + bits[i] * size[i])

    def rows(at, amount):
        return pl.ds(pl.multiple_of(at, 8), amount)

    def down(i):
        other = offset[i] + (1 - bits[i]) * size[i]
        held = src if i == 0 else parts[i - 1]
        at = other if i == 0 else other - offset[i]
        return rcopy(held.at[rows(at, size[i])], parts[count + i], rs.at[i], rr.at[i], peers[i])

    def fold(i):
        down(i).wait_recv()
        held = src if i == 0 else parts[i - 1]
        at = offset[i + 1] if i == 0 else offset[i + 1] - offset[i]
        parts[i][...] = held[rows(at, size[i])] + parts[count + i][...]

    def back(i):
        spot = total.at[rows(offset[i + 1], size[i])]
        return rcopy(spot, spot, gs.at[i], gr.at[i], peers[i])

    def back_recv(i):
        spot = total.at[rows(offset[i] + (1 - bits[i]) * size[i], size[i])]
        rcopy(spot, spot, gs.at[i], gr.at[i], peers[i]).wait_recv()

    steps = [lambda: down(0).start()]
    for i in range(1, count):

        def step(i=i):
            fold(i - 1)
            down(i).start()

        steps.append(step)

    def middle():
        fold(count - 1)
        total[rows(offset[count], size[-1])] = parts[count - 1][...]
        back(count - 1).start()

    steps.append(middle)
    for i in range(count - 2, -1, -1):

        def step(i=i):
            back_recv(i + 1)
            back(i).start()

        steps.append(step)

    def end():
        back_recv(0)
        for i in range(count):
            down(i).wait_send()
            back(i).wait_send()

    return steps, end


def both(one, two):
    def run(launch):
        one()
        two(launch)

    return run


def tail_kernel(kinds, *refs):
    grads, refs = refs[:kinds], refs[kinds:]
    (q_ref, kv_ref, small_ref, x_ref, ctx_ref, resid_ref, w_ref), refs = refs[:7], refs[7:]
    outs, refs = refs[: kinds + 1], refs[kinds + 1 :]
    (give_out, small_out), refs = refs[:2], refs[2:]
    (total, theirs, dqkv, own_grads, dpad, weights, resid_t, give_src), refs = refs[:8], refs[8:]
    parts, refs = refs[:10], refs[10:]
    (send, recv, psend, precv), sems, (wl, gl, gs, gr), scratch = refs[:4], refs[4:8], refs[8:12], refs[12:]
    d, r, c = place()
    pn = (1 - d, r, c)
    deep, wide = kv_ref.shape[2], q_ref.shape[1]
    full = dqkv.shape[1]
    kv_rows, q_rows = pl.ds(0, deep), pl.ds(deep, wide)
    greet(plane_peers() + [(d, r, c ^ j) for j in (1, 2, 3)])

    def pair(j):
        return rcopy(kv_ref.at[c ^ j, 1 - d], theirs.at[c ^ j], psend.at[j], precv.at[j], pn)

    def kv(j):
        return rcopy(total.at[c ^ j], dqkv.at[c, kv_rows], send.at[0, j], recv.at[0, j], (d, r, c ^ j))

    def q(j):
        return rcopy(q_ref.at[c ^ j], dqkv.at[c, q_rows], send.at[1, j], recv.at[1, j], (d, r, c ^ j))

    for j in (3, 2, 1, 0):
        pair(j).start()
    for j in (3, 2, 1):
        q(j).start()
    load_w = pltpu.make_async_copy(w_ref, weights, wl)
    load_w.start()
    steps, end = sum_steps(small_ref, small_out, parts, sems)
    start, finish = give_moves(give_src, give_out, gl, gs, gr)

    def begin():
        for j in (3, 2, 1):
            pair(j).wait_recv()
            total[c ^ j] = kv_ref[c ^ j, d] + theirs[c ^ j]
            kv(j).start()
        pair(0).wait_recv()
        dqkv[c, kv_rows] = kv_ref[c, d] + theirs[c]
        dqkv[c, q_rows] = q_ref[c]
        spare = full - deep - wide
        for at in range(4):
            dqkv[at, pl.ds(deep + wide, spare)] = jnp.zeros((spare, dqkv.shape[2]), bf16)
        resid_t[...] = resid_ref[...].T
        feats = x_ref.shape[1]
        blank = dpad.shape[1] - feats
        for row in range(4):
            dpad[row, pl.ds(0, blank)] = jnp.zeros((blank, dpad.shape[2]), bf16)
            dpad[row, pl.ds(blank, feats)] = resid_t[pl.ds(row * feats, feats)].astype(bf16)

    across = (((1,), (1,)), ((), ()))

    def arrived():
        for j in (1, 2, 3):
            q(j).wait_recv()
            kv(j).wait_recv()

    def make(at):
        lead = full - dpad.shape[1]

        @pl.loop(0, 4)
        def _(row):
            one = lax.dot_general(x_ref[row], dqkv[at], across, preferred_element_type=f32)
            two = lax.dot_general(ctx_ref[at], dpad[row], across, preferred_element_type=f32)
            shape = own_grads.shape[2:4] + (-1,)
            own_grads[at, row, :, :, :lead] = one[:, :lead].astype(bf16).reshape(shape)
            own_grads[at, row, :, :, lead:] = (one[:, lead:] + two).astype(bf16).reshape(shape)

    def input_grad(launch):
        load_w.wait()
        feats = x_ref.shape[1]

        @pl.loop(0, 4)
        def _(row):
            rows = pl.ds(pl.multiple_of(row * feats, 8), feats)
            part = resid_t[rows]
            for at in range(4):
                w = weights[at, row].reshape(feats, full)
                part = part + jnp.dot(w, dqkv[at], preferred_element_type=f32)
            give_src[row] = part.astype(bf16)

        start()

    first = 4
    extras = [lambda launch: None] * first
    for j, at in enumerate((0, 3, 1, 2)):

        def extra(launch, j=j, at=at):
            if j == 0:
                arrived()
            make(at)
            launch(kinds * 4 + j)

        extras.append(extra)
    extras.append(input_grad)
    extras += [lambda launch: None] * (len(steps) - len(extras))
    during = [both(step, extra) for step, extra in zip(steps, extras)]
    scatter_core(list(grads) + [own_grads], outs, scratch, begin, during, late=1)
    end()
    finish()
    for j in range(4):
        pair(j).wait_send()
    for j in (1, 2, 3):
        q(j).wait_send()
        kv(j).wait_send()


def tail_fast(grads, q, kv, small, x_t, ctx_t, resid, w_attn, cid):
    kinds = len(grads)
    n, w = grads[0].shape[3:]
    dma = pltpu.SemaphoreType.DMA
    cols, _, wide, own = kv.shape
    feats = x_t.shape[1]
    parts = [pltpu.VMEM((small.shape[0] >> (i + 1), small.shape[1]), f32) for i in range(5)]
    return pl.pallas_call(
        functools.partial(tail_kernel, kinds),
        out_shape=[jax.ShapeDtypeStruct((2, n, w), bf16)] * (kinds + 1)
        + [
            jax.ShapeDtypeStruct((2, feats, 2 * own), bf16),
            jax.ShapeDtypeStruct(small.shape, f32),
        ],
        in_specs=[HBM] * kinds + [VM] * 6 + [HBM],
        out_specs=[HBM] * (kinds + 1) + [HBM, VM],
        scratch_shapes=[
            pltpu.VMEM((cols, wide, own), bf16),
            pltpu.VMEM((cols, wide, own), bf16),
            pltpu.VMEM((cols, w, own), bf16),
            pltpu.VMEM((4, 4, 2, n, w), bf16),
            pltpu.VMEM((4, 256, own), bf16),
            pltpu.VMEM((4, 4, 2, n, w), bf16),
            pltpu.VMEM((4 * feats, own), f32),
            pltpu.VMEM((4, feats, own), bf16),
        ]
        + parts * 2
        + [dma((2, 4)), dma((2, 4)), dma((4,)), dma((4,)), dma((5,)), dma((5,)), dma((5,)), dma((5,))]
        + [dma, dma, dma((4,)), dma((2, 2))]
        + scatter_scratch(kinds + 1, n, w, bf16),
        compiler_params=pltpu.CompilerParams(
            collective_id=cid, has_side_effects=True, vmem_limit_bytes=58 * 1024 * 1024
        ),
        name="tail",
    )(*grads, q, kv, small, x_t, ctx_t, resid, w_attn)


def dot(a, b, contract=((1,), (0,))):
    return lax.dot_general(a, b, (contract, ((), ())), preferred_element_type=f32)


def block_rows(ref, heads, scale, out):
    own = ref.shape[-1]
    for h in range(heads):
        for g in range(heads):
            spot = (pl.ds(h * HD, HD), pl.ds(g * own, own))
            if h == g:
                out[spot] = ref[0, pl.ds(h * HD, HD)] * jnp.asarray(scale, out.dtype)
            else:
                out[spot] = jnp.zeros((HD, own), out.dtype)


def attn_fwd_kernel(heads, scale, bounds, q_ref, kv_ref, qseg_ref, kseg_ref, ctx_ref, lse_ref, kn, q3, s_scr, o_scr):
    step = pl.program_id(0)
    tiles, _, tile = kv_ref.shape
    wide = heads * HD
    own = q_ref.shape[-1]

    @pl.when(step == 0)
    def _():
        @pl.loop(0, tiles)
        def _(j):
            kn[j] = kv_ref[j, pl.ds(0, wide)].astype(f32).T.astype(bf16)

    block_rows(q_ref, heads, scale, q3)
    low, high = bounds[step, 0], bounds[step, 1]
    qseg = jnp.concatenate([qseg_ref[0]] * heads, axis=1)

    def one(j, top):
        s = dot(kn[j], q3[...])
        s = jnp.where(kseg_ref[j] == qseg, s, masked_value)
        s_scr[j] = s
        return jnp.maximum(top, jnp.max(s, axis=0, keepdims=True))

    top = lax.fori_loop(low, high, one, jnp.full((1, heads * own), masked_value, f32))
    o_scr[...] = jnp.zeros_like(o_scr)

    def two(j, total):
        p = jnp.exp(s_scr[j] - top)
        low_p = p.astype(bf16)
        for h in range(heads):
            rows = pl.ds(h * HD, HD)
            v = kv_ref[j, pl.ds(wide + h * HD, HD)]
            o_scr[rows] += dot(v, low_p[:, h * own : (h + 1) * own])
        return total + jnp.sum(p, axis=0, keepdims=True)

    total = lax.fori_loop(low, high, two, jnp.zeros((1, heads * own), f32))
    for h in range(heads):
        rows = pl.ds(h * HD, HD)
        ctx_ref[0, rows] = (o_scr[rows] / total[:, h * own : (h + 1) * own]).astype(bf16)
    lse_ref[0] = top + jnp.log(total)


def attn_fwd(bounds, q, kv, qseg, kseg, scale):
    blocks, wide, own = q.shape
    tiles, _, tile = kv.shape
    heads = wide // HD
    return pl.pallas_call(
        functools.partial(attn_fwd_kernel, heads, scale),
        out_shape=[
            jax.ShapeDtypeStruct(q.shape, bf16),
            jax.ShapeDtypeStruct((blocks, 1, heads * own), f32),
        ],
        grid_spec=pltpu.PrefetchScalarGridSpec(
            num_scalar_prefetch=1,
            grid=(blocks,),
            in_specs=[
                pl.BlockSpec((1, wide, own), lambda i, b: (i, 0, 0)),
                pl.BlockSpec(kv.shape, lambda i, b: (0, 0, 0)),
                pl.BlockSpec((1, 1, own), lambda i, b: (i, 0, 0)),
                pl.BlockSpec(kseg.shape, lambda i, b: (0, 0, 0)),
            ],
            out_specs=[
                pl.BlockSpec((1, wide, own), lambda i, b: (i, 0, 0)),
                pl.BlockSpec((1, 1, heads * own), lambda i, b: (i, 0, 0)),
            ],
            scratch_shapes=[
                pltpu.VMEM((tiles, tile, wide), bf16),
                pltpu.VMEM((wide, heads * own), bf16),
                pltpu.VMEM((tiles, tile, heads * own), f32),
                pltpu.VMEM((wide, own), f32),
            ],
        ),
        compiler_params=pltpu.CompilerParams(
            dimension_semantics=("arbitrary",), vmem_limit_bytes=48 * 1024 * 1024
        ),
        name="attn_fwd",
    )(bounds, q, kv, qseg, kseg)


def attn_bwd_kernel(
    heads, scale, bounds, q_ref, kv_ref, qseg_ref, kseg_ref, lse_ref, ctx_ref, dctx_ref,
    dq_ref, dkv_ref, kn, vn, q3, dc3, dq_scr, dkv_scr,
):
    step = pl.program_id(0)
    tiles, _, tile = kv_ref.shape
    wide = heads * HD
    own = q_ref.shape[-1]

    @pl.when(step == 0)
    def _():
        @pl.loop(0, tiles)
        def _(j):
            kn[j] = kv_ref[j, pl.ds(0, wide)].astype(f32).T.astype(bf16)
            vn[j] = kv_ref[j, pl.ds(wide, wide)].astype(f32).T.astype(bf16)
            dkv_scr[j] = jnp.zeros((2 * wide, tile), f32)

    block_rows(q_ref, heads, scale, q3)
    block_rows(dctx_ref, heads, 1.0, dc3)
    low, high = bounds[step, 0], bounds[step, 1]
    qseg = jnp.concatenate([qseg_ref[0]] * heads, axis=1)
    lse = lse_ref[0]
    product = ctx_ref[0].astype(f32) * dctx_ref[0].astype(f32)
    delta = jnp.concatenate(
        [jnp.sum(product[h * HD : (h + 1) * HD], axis=0, keepdims=True) for h in range(heads)], axis=1
    )
    dq_scr[...] = jnp.zeros_like(dq_scr)

    @pl.loop(low, high)
    def _(j):
        s = dot(kn[j], q3[...])
        s = jnp.where(kseg_ref[j] == qseg, s, masked_value)
        p = jnp.exp(s - lse)
        d_p = dot(vn[j], dc3[...])
        d_s = (p * (d_p - delta)).astype(bf16)
        p = p.astype(bf16)
        for h in range(heads):
            rows, lanes = pl.ds(h * HD, HD), slice(h * own, (h + 1) * own)
            dq_scr[rows] += dot(kv_ref[j, rows], d_s[:, lanes])
            dkv_scr[j, rows] += dot(q3[rows, lanes], d_s[:, lanes], ((1,), (1,)))
            deep = pl.ds(wide + h * HD, HD)
            dkv_scr[j, deep] += dot(dctx_ref[0, rows], p[:, lanes], ((1,), (1,)))

    dq_ref[0] = (dq_scr[...] * scale).astype(bf16)

    @pl.when(step == pl.num_programs(0) - 1)
    def _():
        @pl.loop(0, tiles)
        def _(j):
            dkv_ref[j] = dkv_scr[j].astype(bf16)


def attn_bwd(bounds, q, kv, qseg, kseg, lse, ctx, dctx, scale):
    blocks, wide, own = q.shape
    tiles, _, tile = kv.shape
    heads = wide // HD
    rowed = pl.BlockSpec((1, wide, own), lambda i, b: (i, 0, 0))
    return pl.pallas_call(
        functools.partial(attn_bwd_kernel, heads, scale),
        out_shape=[jax.ShapeDtypeStruct(q.shape, bf16), jax.ShapeDtypeStruct(kv.shape, bf16)],
        grid_spec=pltpu.PrefetchScalarGridSpec(
            num_scalar_prefetch=1,
            grid=(blocks,),
            in_specs=[
                rowed,
                pl.BlockSpec(kv.shape, lambda i, b: (0, 0, 0)),
                pl.BlockSpec((1, 1, own), lambda i, b: (i, 0, 0)),
                pl.BlockSpec(kseg.shape, lambda i, b: (0, 0, 0)),
                pl.BlockSpec((1, 1, heads * own), lambda i, b: (i, 0, 0)),
                rowed,
                rowed,
            ],
            out_specs=[rowed, pl.BlockSpec(kv.shape, lambda i, b: (0, 0, 0))],
            scratch_shapes=[
                pltpu.VMEM((tiles, tile, wide), bf16),
                pltpu.VMEM((tiles, tile, wide), bf16),
                pltpu.VMEM((wide, heads * own), bf16),
                pltpu.VMEM((wide, heads * own), bf16),
                pltpu.VMEM((wide, own), f32),
                pltpu.VMEM((tiles, 2 * wide, tile), f32),
            ],
        ),
        compiler_params=pltpu.CompilerParams(
            dimension_semantics=("arbitrary",), vmem_limit_bytes=48 * 1024 * 1024
        ),
        name="attn_bwd",
    )(bounds, q, kv, qseg, kseg, lse, ctx, dctx)


def fast_local(
    tokens,
    segments,
    labels,
    cotangent,
    w_qkv,
    b_qkv,
    w_out,
    b_out,
    ln1_gain,
    ln1_bias,
    w_in,
    b_in,
    w_back,
    b_back,
    ln2_gain,
    ln2_bias,
    s_proj,
    s_bias,
    s_query,
    s_mid,
    s_mid_bias,
    s_cls,
    s_cls_bias,
):
    _, width_row, cols_local = tokens.shape
    parts, rows, cols, seqs, _ = sizes(tokens.shape[0])
    width = width_row * rows
    own = cols_local // parts
    width_col = b_qkv.shape[1]
    heads_dev = width_col // HD
    hidden_col = b_in.shape[0]
    docs_count = labels.shape[1]
    class_count = s_cls.shape[1]
    student_width = s_proj.shape[1]
    seq_len = segments.shape[1]
    row_index = lax.axis_index("row")
    col_index = lax.axis_index("col")
    dp_index = lax.axis_index("dp")
    score_scale = HD ** (-0.5)
    pool_scale = SHD ** (-0.5)
    query_heads = s_query.reshape(SH, SHD)
    doc_ids = jnp.arange(docs_count, dtype=jnp.int32)
    class_ids = jnp.arange(class_count, dtype=jnp.int32)

    w_three = w_qkv.reshape(width_row, heads_dev, 3, HD).transpose(0, 2, 1, 3)
    w_three = jnp.concatenate([w_three[:, 1], w_three[:, 2], w_three[:, 0]], axis=1)
    shard_attn = own_half(jnp.concatenate([w_three.reshape(width_row, -1), w_out], axis=1))
    proj_rows = width_row // cols
    lanes = -(-3 * width_col // 128) * 128
    offsets = jnp.concatenate([jnp.zeros_like(b_qkv[0]), b_qkv[1], b_qkv[0]])
    offsets = jnp.pad(offsets, (0, lanes - 3 * width_col))
    vectors = [offsets, b_out, ln1_gain, ln1_bias, b_back, ln2_gain, ln2_bias, b_in]
    vectors.append(lax.dynamic_slice_in_dim(s_proj, col_index * proj_rows, proj_rows).astype(f32).reshape(-1))
    flat = jnp.concatenate(vectors)
    flat = jnp.pad(flat, (0, 96 * 128 - flat.shape[0])).reshape(96, 128)
    w_attn, vec, w_in_all, w_back_all, x_parts, ints, queries, kv, w_out_all = gather_fast(
        [shard_attn, own_half(flat), own_half(w_in), own_half(w_back)],
        tokens,
        jnp.concatenate([segments, labels], axis=1),
        width_col,
        1,
    )
    w_in_all = w_in_all.reshape(cols, width, hidden_col)
    w_back_all = w_back_all.reshape(cols, width, hidden_col)
    vec = vec.reshape(cols, rows, -1)
    at = lanes + 6 * width_row
    row_vectors = vec[0, :, lanes:at].reshape(rows, 6, width_row).transpose(1, 0, 2).reshape(6, width)
    b_out_a, gain_one, bias_one, b_back_a, gain_two, bias_two = [row_vectors[i] for i in range(6)]
    b_in_all = vec[:, 0, at : at + hidden_col]
    at += hidden_col
    s_proj_all = vec[:, :, at : at + proj_rows * student_width].astype(bf16)
    s_proj_all = s_proj_all.reshape(cols, rows, proj_rows, student_width).transpose(1, 0, 2, 3)
    s_proj_all = s_proj_all.reshape(width, student_width)
    x_t = x_parts.reshape(width, own)
    ints = lax.dynamic_index_in_dim(ints.reshape(seqs, -1), row_index, 0, False)
    seg_all, label_seq = ints[:seq_len], ints[seq_len:]
    seg_blocks = seg_all.reshape(cols, parts, own)
    seg_q = lax.dynamic_index_in_dim(seg_blocks, dp_index, 1, False)
    seg_own = lax.dynamic_index_in_dim(seg_q, col_index, 0, False)
    lows = jnp.sum(seg_all[None, :] < seg_q[:, :1], axis=1) // own
    highs = (jnp.sum(seg_all[None, :] <= seg_q[:, -1:], axis=1) + own - 1) // own
    bounds = jnp.stack([lows, highs], axis=1).astype(jnp.int32)

    kv = kv.reshape(cols * parts, 2 * width_col, own)
    q_rows, k_rows = seg_q[:, None, :], seg_all.reshape(cols * parts, own, 1)
    context, lse = attn_fwd(bounds, queries, kv, q_rows, k_rows, score_scale)
    ctx_t, c_parts = swap_fast(context, cotangent, 3)
    ctx_parts, ctx_t = ctx_t, ctx_t.reshape(width, own)

    x = x_t.T
    attn_out = mm(ctx_t, w_out_all, ((0,), (0,))) + b_out_a
    normed_one, inv_one = normalize(x.astype(f32) + attn_out)
    hidden_one = normed_one * gain_one + bias_one
    hidden_low = hidden_one.astype(bf16)
    pre_act = jnp.einsum("td,cdn->ctn", hidden_low, w_in_all, preferred_element_type=f32)
    pre_act = pre_act + b_in_all[:, None, :]
    act = gelu_exact(pre_act).astype(bf16)
    ffn_out = jnp.einsum("ctn,cdn->td", act, w_back_all, preferred_element_type=f32) + b_back_a
    normed_two, inv_two = normalize(hidden_one + ffn_out)
    layer_out = (normed_two * gain_two + bias_two).astype(bf16)

    student_h = mm(layer_out, s_proj_all, ((1,), (0,))) + s_bias
    head_parts = student_h.reshape(own, SH, SHD)
    pool_logit = jnp.sum(head_parts * query_heads, axis=-1) * pool_scale
    member = (seg_own[:, None] == doc_ids[None, :])[:, :, None]
    masked = jnp.where(member, pool_logit[:, None, :], masked_value)
    local_top = jnp.max(masked, axis=0)
    local_exp = jnp.where(member, jnp.exp(masked - local_top[None]), 0.0)
    local_total = jnp.sum(local_exp, axis=0)
    local_sum = jnp.einsum("tdh,thk->dhk", local_exp, head_parts, precision=highest)
    stats = jnp.concatenate([local_top[..., None], local_total[..., None], local_sum], axis=-1)
    stats = jnp.pad(stats.reshape(-1), (0, 8 * 128 - stats.size)).reshape(8, 128)

    d_out = c_parts.reshape(width, own).T.astype(f32)
    g_ln2_gain = jnp.sum(d_out * normed_two, axis=0)
    g_ln2_bias = jnp.sum(d_out, axis=0)
    d_resid_two = normalize_back(d_out * gain_two, normed_two, inv_two)
    d_ffn = d_resid_two.astype(bf16)
    g_back_bias = jnp.sum(d_ffn.astype(f32), axis=0)
    g_back = jnp.einsum("td,ctn->cdn", d_ffn, act, preferred_element_type=f32)
    d_act = jnp.einsum("td,cdn->ctn", d_ffn, w_back_all, preferred_element_type=f32)
    _, gelu_fn = jax.vjp(gelu_exact, pre_act)
    d_pre = gelu_fn(d_act)[0].astype(bf16)
    g_in_bias = jnp.sum(d_pre.astype(f32), axis=1)
    g_in = jnp.einsum("td,ctn->cdn", hidden_low, d_pre, preferred_element_type=f32)
    d_hidden_one = d_resid_two + jnp.einsum(
        "ctn,cdn->td", d_pre, w_in_all, preferred_element_type=f32
    )
    g_ln1_gain = jnp.sum(d_hidden_one * normed_one, axis=0)
    g_ln1_bias = jnp.sum(d_hidden_one, axis=0)
    d_resid_one = normalize_back(d_hidden_one * gain_one, normed_one, inv_one)
    d_attn = d_resid_one.astype(bf16)
    g_out_bias = jnp.sum(d_attn.astype(f32), axis=0)
    d_ctx = mm(w_out_all, d_attn, ((1,), (1,))).astype(bf16)
    d_ctx, stats, out = turn_fast(d_ctx.reshape(cols, width_col, own), stats, layer_out.T, 4)

    stats = stats.reshape(cols * parts, -1)[:, : docs_count * SH * (SHD + 2)]
    stats = stats.reshape(cols * parts, docs_count, SH, SHD + 2)
    tops, totals, sums = stats[..., 0], stats[..., 1], stats[..., 2:]
    doc_top = jnp.max(tops, axis=0)
    factors = jnp.exp(tops - doc_top[None])
    doc_total = jnp.sum(totals * factors, axis=0)
    pooled_heads = jnp.sum(sums * factors[..., None], axis=0) / doc_total[:, :, None]
    pooled = pooled_heads.reshape(docs_count, student_width)
    middle = jnp.tanh(jnp.dot(pooled, s_mid, precision=highest) + s_mid_bias)
    logit_rows = jnp.dot(middle, s_cls, precision=highest) + s_cls_bias
    logit_top = jnp.max(logit_rows, axis=-1, keepdims=True)
    logit_exp = jnp.exp(logit_rows - logit_top)
    one_hot = (label_seq[:, None] == class_ids[None, :]).astype(f32)
    d_logits = logit_exp / jnp.sum(logit_exp, axis=-1, keepdims=True) - one_hot
    g_cls = jnp.dot(middle.T, d_logits, precision=highest)
    g_cls_bias = jnp.sum(d_logits, axis=0)
    d_middle = jnp.dot(d_logits, s_cls.T, precision=highest) * (1.0 - middle * middle)
    g_mid = jnp.dot(pooled.T, d_middle, precision=highest)
    g_mid_bias = jnp.sum(d_middle, axis=0)
    d_pooled = jnp.dot(d_middle, s_mid.T, precision=highest).reshape(docs_count, SH, SHD)
    shares = jnp.where(member, jnp.exp(masked - doc_top[None]), 0.0) / doc_total[None]
    d_share = jnp.einsum("dhk,thk->tdh", d_pooled, head_parts, precision=highest)
    base_term = jnp.sum(d_pooled * pooled_heads, axis=-1)
    d_pool_logit = jnp.sum(shares * (d_share - base_term[None]), axis=1)
    d_heads = jnp.einsum("tdh,dhk->thk", shares, d_pooled, precision=highest)
    d_heads = d_heads + d_pool_logit[:, :, None] * query_heads[None] * pool_scale
    g_query = (jnp.sum(d_pool_logit[:, :, None] * head_parts, axis=0) * pool_scale).reshape(-1)
    d_student = d_heads.reshape(own, student_width)
    g_sbias = jnp.sum(d_student, axis=0)
    g_sproj = jnp.dot(layer_out.astype(f32).T, d_student, precision=highest)

    d_q, d_kv = attn_bwd(bounds, queries, kv, q_rows, k_rows, lse, context, d_ctx, score_scale)
    at_seq = (jnp.arange(seqs) == row_index).astype(f32)[:, None]
    at_heads = (jnp.arange(cols) == col_index).astype(f32)[:, None, None]
    g_q_bias = jnp.sum(d_q.astype(f32), axis=(0, 2))
    g_v_bias = jnp.sum(d_kv[:, width_col:].astype(f32), axis=(0, 2))
    once = 1.0 / (parts * cols)
    small = (
        g_sproj,
        jnp.stack([g_q_bias, g_v_bias])[None] * at_heads,
        g_in_bias,
        g_out_bias,
        g_ln1_gain,
        g_ln1_bias,
        g_back_bias,
        g_ln2_gain,
        g_ln2_bias,
        g_sbias,
        g_query,
        g_mid * once,
        g_mid_bias * once,
        g_cls * once,
        logit_rows.reshape(1, -1) * (at_seq * once),
        g_cls_bias * once,
    )
    flat = jnp.concatenate([part.reshape(-1) for part in small])
    tall = -(-flat.shape[0] // (128 * 256)) * 256
    flat = jnp.pad(flat, (0, tall * 128 - flat.shape[0])).reshape(tall, 128)
    blocked = (cols, rows, parts, width_row // parts, -1)
    g_in, g_back, g_attn, grad_tokens, flat = tail_fast(
        [g_in.astype(bf16).reshape(blocked), g_back.astype(bf16).reshape(blocked)],
        d_q,
        d_kv.reshape(cols, parts, 2 * width_col, own),
        flat,
        x_parts,
        ctx_parts,
        d_resid_one,
        w_attn,
        5,
    )
    flat = flat.reshape(-1)
    sums_all, at = [], 0
    for part in small:
        sums_all.append(flat[at : at + part.size].reshape(part.shape))
        at += part.size
    g_in, g_back, g_attn = [part.reshape(width_row, -1).astype(f32) for part in (g_in, g_back, g_attn)]
    g_qkv = g_attn[:, : 3 * width_col].reshape(width_row, 3, heads_dev, HD)
    g_qkv = jnp.stack([g_qkv[:, 2], g_qkv[:, 0], g_qkv[:, 1]], axis=2).reshape(width_row, -1)

    def at_col(part):
        return lax.dynamic_index_in_dim(part, col_index, 0, False)

    def at_row(part):
        return lax.dynamic_slice_in_dim(part, row_index * width_row, width_row)

    (
        g_sproj, g_qkv_bias, g_in_bias, g_out_bias, g_ln1_gain, g_ln1_bias, g_back_bias, g_ln2_gain,
        g_ln2_bias, g_sbias, g_query, g_mid, g_mid_bias, g_cls, logits, g_cls_bias,
    ) = sums_all
    logits = lax.dynamic_slice_in_dim(logits, dp_index * (seqs // parts), seqs // parts)
    return (
        out,
        logits.reshape(seqs // parts, docs_count, class_count),
        grad_tokens.astype(f32),
        g_qkv,
        at_col(g_qkv_bias),
        g_attn[:, 3 * width_col :],
        at_row(g_out_bias),
        at_row(g_ln1_gain),
        at_row(g_ln1_bias),
        g_in,
        at_col(g_in_bias),
        g_back,
        at_row(g_back_bias),
        at_row(g_ln2_gain),
        at_row(g_ln2_bias),
        at_row(g_sproj),
        g_sbias,
        g_query,
        g_mid,
        g_mid_bias,
        g_cls,
        g_cls_bias,
    )


def solution(mesh):
    row, col = P("row"), P("col")
    grid, whole = P("row", "col"), P("dp", "row", "col")
    placed = (
        (whole, P("dp", None), P("dp", None), whole, grid, P(None, "col"), P("col", "row"))
        + (row, row, row, grid, col, grid, row, row, row, P("row", None))
        + (P(),) * 6
    )
    results = (
        (whole, P("dp", None, None), whole, grid, P(None, "col"), P("col", "row"))
        + (row, row, row, grid, col, grid, row, row, row, P("row", None))
        + (P(),) * 6
    )
    quick = dict(mesh.shape) == {"dp": 2, "row": 4, "col": 4}
    local = fast_local if quick else general_local
    return jax.shard_map(local, mesh=mesh, in_specs=placed, out_specs=results, check_vma=False)
```

profile of v0, /device:TPU:0, one launch (start us, length us, event | category | flops | bytes accessed | tf_op | source)
XLA Modules:
  0.0 367.3 jit_solution(1605860234068271571)
XLA Ops:
  1.7 0.7 mul.350
  2.5 0.8 fusion.97
  3.3 0.7 pad_add_fusion.refs_5_
  4.8 0.9 concatenate.24
  6.3 1.6 constant_dynamic-slice_fusion.7.refs_3_
  7.9 1.1 copy.226
  9.5 0.9 copy-done.10
  10.4 1.0 copy-done.12
  11.4 92.1 %head.1 = (bf16[4,4,2,96,768]{4,3,2,1,0:T(8,128)(2,1)S(1)}, f32[4,4,2,48,128]{4,3,2,1,0:T(8,128)S(1)}, bf16[4,4,2,96,768]{4,3,2,1,0:T(8,128)(2,1)}, bf16[4,4,2,9...) custom-call(bf16[96,768]{1,0:T(8,128)(2,1)S(1)} %fusion.47.refs_0_, ...), custom_call_target="tpu_custom_call" | custom-call | tf_op jit(solution)/shard_map/head/pallas_call | solution.py:728
  103.4 1.0 copy-done.2
  104.5 2.1 copy-done.3
  109.2 1.2 reshape.450
  110.5 0.8 slice.235
  111.3 0.7 slice.231
  112.0 1.1 slice.280
  114.6 1.1 copy.230
  115.8 0.9 reshape.494.kseg_ref
  116.7 9.1 %attn_fwd.1 = (bf16[4,192,256]{2,1,0:T(8,128)(2,1)S(1)}, f32[4,1,768]{2,1,0:T(1,128)S(1)}) custom-call(s32[4,2]{1,0:T(4,128)S(1)} %pad_add_fusion.1.bounds, bf16[4,192,256]{2,1,0:T(8,128)(2,1)S(1)} %get-tuple-element.48.q_ref, bf16[8,384,256]{2,1,0:T(8,128)(2,1)S(1)} %bitcast.316, s32[4,1,256]{2,1,0:T(1,128)S(1)} %constant_dynamic-slice_fusion.6.qseg_ref, ...), custom_call_target="tpu_custom_call" | custom-call | tf_op jit(solution)/shard_map/attn_fwd/pallas_call | solution.py:1359
  125.8 0.7 copy-done.5
  126.5 14.4 %swap.1 = (bf16[4,192,256]{2,1,0:T(8,128)(2,1)}, bf16[4,192,256]{2,1,0:T(8,128)(2,1)}) custom-call(bf16[4,192,256]{2,1,0:T(8,128)(2,1)} %copy-done.5, bf16[2,192,512]{2,1,0:T(8,128)(2,1)} %cot.1), custom_call_target="tpu_custom_call" | custom-call | tf_op jit(solution)/shard_map/swap/pallas_call | solution.py:1022
  140.9 1.2 convert_reduce_fusion.5
  142.7 2.0 copy.240
  144.8 2.3 fusion.94
  147.4 11.6 %fusion.9 = (bf16[4,256,768]{2,1,0:T(8,128)(2,1)S(1)}, f32[4,256,768]{2,1,0:T(8,128)}, f32[4,768,256]{1,2,0:T(8,128)}) fusion(f32[4,768]{1,0:T(4,128)S(1)} %bitcast.342, bf16[4,768,768]{2,1,0:T(8,128)(2,1)} %bitcast.351, f32[256,768]{1,0:T(8,128)S(1)} %get-tuple-element.226, f32[768]{0:T(1024)S(1)} %add.216, f32[768]{0:T(1024)S(1)} %mul.319, ...), kind=kOutput, calls=%fused_computation.18 | convolution fusion | flops 1260847104 | bytes 13389824 | tf_op jit(solution)/shard_map/td,cdn->ctn/dot_general | solution.py:1576
  159.1 1.5 fusion.91
  160.6 1.0 copy-done.19
  161.8 1.2 fusion.34
  163.1 1.9 copy.246
  165.0 2.6 fusion.39
  168.2 0.9 convert_reduce_fusion.2
  169.1 6.2 %convert_reduce_fusion = (f32[4,768]{1,0:T(4,128)S(1)}, bf16[4,256,768]{2,1,0:T(8,128)(2,1)S(1)}) fusion(f32[4,256,768]{2,1,0:T(8,128)S(1)} %copy-done.47, bf16[4,768,768]{2,1,0:T(8,128)(2,1)} %bitcast.355, f32[256,768]{1,0:T(8,128)S(1)} %get-tuple-element.218, f32[4,768,256]{1,2,0:T(8,128)} %get-tuple-element.251, f32[4,768]{1,0:T(4,128)S(1)} %bitcast.343), kind=kOutput, calls=%fused_computation.19 | convolution fusion | flops 1221522432 | bytes 13393920 | tf_op jit(solution)/shard_map/td,cdn->ctn/dot_general | solution.py:1602
  175.4 3.0 multiply_reduce_fusion
  179.1 2.2 convert_reduce_fusion.3
  181.3 0.9 copy-done.16
  182.2 2.5 convolution_convert_fusion.2
  186.0 15.2 %turn.1 = (bf16[4,192,256]{2,1,0:T(8,128)(2,1)}, f32[2,4,8,128]{3,2,1,0:T(8,128)}, bf16[2,192,512]{2,1,0:T(8,128)(2,1)}) custom-call(bf16[4,192,256]{2,1,0:T(8,128)(2,1)} %bitcast.324, f32[8,128]{1,0:T(8,128)} %pad_bitcast_fusion.2.stats_ref, bf16[4,192,256]{2,1,0:T(8,128)(2,1)} %bitcast.323), custom_call_target="tpu_custom_call" | custom-call | tf_op jit(solution)/shard_map/turn/pallas_call | solution.py:1065
  201.1 1.0 copy-done.6
  202.1 1.0 copy-done.11
  203.1 12.5 %attn_bwd.1 = (bf16[4,192,256]{2,1,0:T(8,128)(2,1)S(1)}, bf16[8,384,256]{2,1,0:T(8,128)(2,1)S(1)}) custom-call(s32[4,2]{1,0:T(4,128)S(1)} %pad_add_fusion.1.bounds, bf16[4,192,256]{2,1,0:T(8,128)(2,1)S(1)} %get-tuple-element.48.q_ref, bf16[8,384,256]{2,1,0:T(8,128)(2,1)S(1)} %bitcast.317, s32[4,1,256]{2,1,0:T(1,128)S(1)} %constant_dynamic-slice_fusion.6.qseg_ref, ...), custom_call_target="tpu_custom_call" | custom-call | tf_op jit(solution)/shard_map/attn_bwd/pallas_call | solution.py:1449
  215.8 0.9 copy-done.4
  217.7 0.8 copy.288
  220.0 0.8 fusion.29
  220.8 1.0 fusion.98
  222.0 0.8 fusion.87
  224.1 0.9 fusion.100
  225.1 0.9 convolution_multiply_fusion.1
  227.1 0.9 fusion.28
  229.7 7.9 %concatenate.27 = f32[126430]{0:T(1024)S(1)} concatenate(f32[98304]{0:T(1024)S(1)} %convolution_bitcast_fusion, f32[1536]{0:T(1024)} %mul.378, f32[3072]{0:T(1024)} %reshape.468, f32[768]{0:T(1024)} %get-tuple-element.219, f32[768]{0:T(1024)} %get-tuple-element.202, f32[768]{0:T(1024)} %get-tuple-element.206, f32[768]{0:T(1024)} %get-tuple-element.217, f32[768]{0:T(1024)} %get-tuple-element.200, ...), dimensions={0} | concatenate | bytes 1011440 | tf_op jit(solution)/shard_map/concatenate | solution.py:1673
  237.6 0.8 pad_bitcast_fusion.refs_4_
  238.4 4.6 %convolution_convert_fusion.1 = bf16[4,768,768]{1,2,0:T(8,128)(2,1)} fusion(bf16[4,256,768]{2,1,0:T(8,128)(2,1)S(1)} %copy-done.28, f32[256,768]{1,0:T(8,128)S(1)} %copy-done.15, f32[768]{0:T(1024)} %copy-done.36, f32[768]{0:T(1024)} %copy-done.35, f32[256]{0:T(256)} %copy-done.42, f32[256]{0:T(256)} %copy-done.41), kind=kOutput, calls=%fused_computation.34 | convolution fusion | flops 1211301888 | bytes 7086080 | tf_op jit(solution)/shard_map/td,ctn->cdn/dot_general | solution.py:1606
  243.0 3.7 %convolution_convert_fusion = bf16[4,768,768]{1,2,0:T(8,128)(2,1)} fusion(bf16[4,256,768]{2,1,0:T(8,128)(2,1)S(1)} %copy-done.26, f32[256,768]{1,0:T(8,128)S(1)} %copy-done.24), kind=kOutput, calls=%fused_computation.33 | convolution fusion | flops 1210515456 | bytes 7077888 | tf_op jit(solution)/shard_map/td,ctn->cdn/dot_general | solution.py:1601
  246.7 96.9 %tail.1 = (bf16[2,96,768]{2,1,0:T(8,128)(2,1)}, bf16[2,96,768]{2,1,0:T(8,128)(2,1)}, bf16[2,96,768]{2,1,0:T(8,128)(2,1)}, bf16[2,192,512]{2,1,0:T(8,128)(2,1)}, f32[1024,128]{1,0:T(8,128)}) custom-call(bf16[4,4,2,96,768]{4,3,2,1,0:T(8,128)(2,1)} %bitcast.319, bf16[4,4,2,96,768]{4,3,2,1,0:T(8,128)(2,1)} %bitcast.320, bf16[4,192,256]{2,1,0:T(8,128)(2,1)} %copy-done.7, ...), custom_call_target="tpu_custom_call" | custom-call | tf_op jit(solution)/shard_map/tail/pallas_call | solution.py:1269
  343.6 1.3 slice.250
  344.9 1.3 slice_bitcast_fusion.12
  351.0 0.8 slice_bitcast_fusion.6
  356.4 1.5 slice.221
  357.9 1.0 slice.216
  359.6 2.0 convert_element_type.151
  361.6 1.0 bitcast_convert_fusion.3
  362.6 0.8 slice.249
  363.8 1.0 copy.263
  364.8 0.9 bitcast_convert_fusion.2
  365.7 0.9 bitcast_convert_fusion.1
  366.6 0.7 copy.292
  (221 shorter events, 28.2 us)
Async XLA Ops:
  0.7 5.0 %copy-start = (bf16[192,768]{1,0:T(8,128)(2,1)S(1)}, bf16[192,768]{1,0:T(8,128)(2,1)}, u32[]{:S(2)}) copy-start(bf16[192,768]{1,0:T(8,128)(2,1)} %param.33) | copy-start | bytes 884740
  0.7 8.7 %copy-start.34 = (bf16[192,192]{1,0:T(8,128)(2,1)S(1)}, bf16[192,192]{1,0:T(8,128)(2,1)}, u32[]{:S(2)}) copy-start(bf16[192,192]{1,0:T(8,128)(2,1)} %param.29) | copy-start | bytes 221188
  2.5 165.1 %copy-start.43 = (f32[2,64]{1,0:T(2,128)}, f32[2,64]{1,0:T(2,128)S(1)}, u32[]{:S(2)}) copy-start(f32[2,64]{1,0:T(2,128)S(1)} %mul.350) | copy-start | bytes 1540
  6.3 3.1 copy-start.9
  9.4 0.9 copy-start.10
  10.4 1.0 copy-start.12
  103.4 1.0 copy-start.2
  104.5 2.1 copy-start.3
  106.6 8.0 %copy-start.8 = (bf16[4,192,256]{2,1,0:T(8,128)(2,1)}, bf16[4,192,256]{2,1,0:T(8,128)(2,1)S(1)}, u32[]{:S(2)}) copy-start(bf16[4,192,256]{2,1,0:T(8,128)(2,1)S(1)} %get-tuple-element.46.refs_5_) | copy-start | bytes 1179652
  108.5 76.4 %copy-start.37 = (pred[256,6]{0,1:T(8,128)(4,1)}, pred[256,6]{0,1:T(8,128)(4,1)S(1)}, u32[]{:S(2)}) copy-start(pred[256,6]{0,1:T(8,128)(4,1)S(1)} %iota_compare_fusion) | copy-start | bytes 4612
  114.2 64.8 %copy-start.35 = (f32[768]{0:T(1024)}, f32[768]{0:T(1024)S(1)}, u32[]{:S(2)}) copy-start(f32[768]{0:T(1024)S(1)} %mul.319) | copy-start | bytes 9220
  114.3 47.5 %copy-start.36 = (f32[768]{0:T(1024)}, f32[768]{0:T(1024)S(1)}, u32[]{:S(2)}) copy-start(f32[768]{0:T(1024)S(1)} %add.216) | copy-start | bytes 9220
  125.7 0.7 copy-start.5
  144.8 14.2 %slice-start.2 = ((s8[4718592]{0:T(1024)(128)(4,1)}), s8[4194304]{0:T(1024)(128)(4,1)S(1)}, s32[]{:S(2)}) async-start(s8[4718592]{0:T(1024)(128)(4,1)} %bitcast.356), calls=%async_computation.2 | async-start | bytes 8388608
  147.1 11.9 %copy-start.13 = (f32[256,768]{1,0:T(8,128)}, f32[256,768]{1,0:T(8,128)S(1)}, u32[]{:S(2)}) copy-start(f32[256,768]{1,0:T(8,128)S(1)} %get-tuple-element.226) | copy-start | bytes 2359300
  147.2 31.9 %copy-start.41 = (f32[256]{0:T(256)}, f32[256]{0:T(256)S(1)}, u32[]{:S(2)}) copy-start(f32[256]{0:T(256)S(1)} %broadcast_multiply_fusion.8) | copy-start | bytes 3076
  147.4 31.6 %copy-start.42 = (f32[256]{0:T(256)}, f32[256]{0:T(256)S(1)}, u32[]{:S(2)}) copy-start(f32[256]{0:T(256)S(1)} %add_rsqrt_fusion.1) | copy-start | bytes 3076
  147.4 11.6 %slice-start.3 = ((s8[4718592]{0:T(1024)(128)(4,1)}), s8[524288]{0:T(1024)(128)(4,1)S(1)}, s32[]{:S(2)}) async-start(s8[4718592]{0:T(1024)(128)(4,1)} %bitcast.356), calls=%async_computation.3 | async-start | bytes 1048576
  159.0 1.6 copy-start.25
  159.1 2.8 copy-start.17
  160.6 1.0 copy-start.19
  161.6 6.0 %copy-start.29 = (bf16[4,4,48,128]{3,2,0,1:T(8,128)(2,1)S(1)}, bf16[4,4,48,128]{3,2,0,1:T(8,128)(2,1)}, u32[]{:S(2)}) copy-start(bf16[4,4,48,128]{3,2,0,1:T(8,128)(2,1)} %copy.267) | copy-start | bytes 589828
  161.6 6.0 %copy-start.45 = (f32[128]{0:T(128)S(1)}, f32[128]{0:T(128)}, u32[]{:S(2)}) copy-start(f32[128]{0:T(128)} %param.40) | copy-start | bytes 1540
  165.0 3.2 copy-start.18
  165.0 3.2 copy-start.20
  165.0 4.1 %copy-start.47 = (f32[4,256,768]{2,1,0:T(8,128)S(1)}, f32[4,256,768]{2,1,0:T(8,128)}, u32[]{:S(2)}) copy-start(f32[4,256,768]{2,1,0:T(8,128)} %get-tuple-element.224) | copy-start | bytes 9437188
  167.6 1.5 copy-start.21
  167.9 17.0 %copy-start.39 = (f32[256,2]{0,1:T(2,128)}, f32[256,2]{0,1:T(2,128)S(1)}, u32[]{:S(2)}) copy-start(f32[256,2]{0,1:T(2,128)S(1)} %broadcast_multiply_fusion.2) | copy-start | bytes 6148
  168.2 7.1 %slice-start = ((s8[4718592]{0:T(1024)(128)(4,1)}), s8[4194304]{0:T(1024)(128)(4,1)S(1)}, s32[]{:S(2)}) async-start(s8[4718592]{0:T(1024)(128)(4,1)} %bitcast.352), calls=%async_computation | async-start | bytes 8388608
  169.1 6.2 %copy-start.23 = (f32[256,768]{1,0:T(8,128)}, f32[256,768]{1,0:T(8,128)S(1)}, u32[]{:S(2)}) copy-start(f32[256,768]{1,0:T(8,128)S(1)} %get-tuple-element.218) | copy-start | bytes 2359300
  169.1 6.2 %copy-start.14 = (f32[256,768]{1,0:T(8,128)S(1)}, f32[256,768]{1,0:T(8,128)}, u32[]{:S(2)}) copy-start(f32[256,768]{1,0:T(8,128)} %copy-done.13) | copy-start | bytes 2359300
  169.1 6.2 %slice-start.1 = ((s8[4718592]{0:T(1024)(128)(4,1)}), s8[524288]{0:T(1024)(128)(4,1)S(1)}, s32[]{:S(2)}) async-start(s8[4718592]{0:T(1024)(128)(4,1)} %bitcast.352), calls=%async_computation.1 | async-start | bytes 1048576
  175.3 3.1 copy-start.27
  181.3 0.9 copy-start.16
  184.7 32.3 %copy-start.46 = (f32[4]{0:T(128)S(1)}, f32[4]{0:T(128)}, u32[]{:S(2)}) copy-start(f32[4]{0:T(128)} %compare_convert_fusion) | copy-start | bytes 52
  186.0 34.0 %copy-start.33 = (f32[128,128]{1,0:T(8,128)S(1)}, f32[128,128]{1,0:T(8,128)}, u32[]{:S(2)}) copy-start(f32[128,128]{1,0:T(8,128)} %param.42) | copy-start | bytes 196612
  201.1 1.0 copy-start.6
  202.1 1.0 copy-start.11
  215.6 1.1 copy-start.4
  215.6 1.3 copy-start.7
  215.6 13.0 %copy-start.38 = (pred[256,6]{0,1:T(8,128)(4,1)S(1)}, pred[256,6]{0,1:T(8,128)(4,1)}, u32[]{:S(2)}) copy-start(pred[256,6]{0,1:T(8,128)(4,1)} %copy-done.37) | copy-start | bytes 4612
  215.7 13.0 %copy-start.40 = (f32[256,2]{0,1:T(2,128)S(1)}, f32[256,2]{0,1:T(2,128)}, u32[]{:S(2)}) copy-start(f32[256,2]{0,1:T(2,128)} %copy-done.39) | copy-start | bytes 6148
  215.7 13.0 %copy-start.44 = (f32[2,64]{1,0:T(2,128)S(1)}, f32[2,64]{1,0:T(2,128)}, u32[]{:S(2)}) copy-start(f32[2,64]{1,0:T(2,128)} %copy-done.43) | copy-start | bytes 1540
  215.7 13.5 %copy-start.22 = (bf16[256,768]{1,0:T(8,128)(2,1)S(1)}, bf16[256,768]{1,0:T(8,128)(2,1)}, u32[]{:S(2)}) copy-start(bf16[256,768]{1,0:T(8,128)(2,1)} %copy-done.21) | copy-start | bytes 1179652
  215.7 22.7 %copy-start.15 = (f32[256,768]{1,0:T(8,128)S(1)}, f32[256,768]{1,0:T(8,128)}, u32[]{:S(2)}) copy-start(f32[256,768]{1,0:T(8,128)} %copy-done.13) | copy-start | bytes 2359300
  215.7 22.7 %copy-start.28 = (bf16[4,256,768]{2,1,0:T(8,128)(2,1)S(1)}, bf16[4,256,768]{2,1,0:T(8,128)(2,1)}, u32[]{:S(2)}) copy-start(bf16[4,256,768]{2,1,0:T(8,128)(2,1)} %copy-done.27) | copy-start | bytes 4718596
  238.4 4.6 %copy-start.24 = (f32[256,768]{1,0:T(8,128)S(1)}, f32[256,768]{1,0:T(8,128)}, u32[]{:S(2)}) copy-start(f32[256,768]{1,0:T(8,128)} %copy-done.23) | copy-start | bytes 2359300
  238.4 4.6 %copy-start.26 = (bf16[4,256,768]{2,1,0:T(8,128)(2,1)S(1)}, bf16[4,256,768]{2,1,0:T(8,128)(2,1)}, u32[]{:S(2)}) copy-start(bf16[4,256,768]{2,1,0:T(8,128)(2,1)} %copy-done.25) | copy-start | bytes 4718596
  363.4 1.4 copy-start.32
  363.4 2.3 copy-start.31
  363.6 2.9 copy-start.30
  363.7 3.7 copy-start.1
where the time goes:
time: 371 us; the launch traced here: 367 us
  Pallas kernels  240 us (65%)
  local copies, waits for them, and re-layouts  62.8 us (17%)
  matrix products  42 us (11%)
  other arithmetic  21 us (6%)
    pallas_call x1, Pallas kernels, tail_fast(): pl.pallas_call(functools.partial(tail_kernel, kinds), out_shape=[jax.Shap...  96.9 us
    pallas_call x1, Pallas kernels, gather_fast(): pl.pallas_call(functools.partial(gather_kernel, kinds), out_shape=[jax.Sh...  92.1 us
    unnamed x114, local copies, waits for them, and re-layouts  16 us
    pallas_call x1, Pallas kernels, turn_fast(): pl.pallas_call(turn_kernel, out_shape=[jax.ShapeDtypeStruct(d_ctx.shape,...  15.2 us
    pallas_call x1, Pallas kernels, swap_fast(): pl.pallas_call(swap_kernel, out_shape=[jax.ShapeDtypeStruct(values.shape,...  14.4 us
    pallas_call x1, Pallas kernels, attn_bwd(): pl.pallas_call(functools.partial(attn_bwd_kernel, heads, scale), out_shap...  12.5 us
    dot_general x1, matrix products, fast_local(): jnp.einsum('td,cdn->ctn', hidden_low, w_in_all, preferred_element_type=f32)  11.6 us
    pallas_call x1, Pallas kernels, attn_fwd(): pl.pallas_call(functools.partial(attn_fwd_kernel, heads, scale), out_shap...  9.07 us

commit v1 on v0

--- a/solution.py
+++ b/solution.py
@@ -757,7 +757,7 @@
     )(*shards, tokens, ints)
 
 
-def scatter_core(grads, outs, scratch, begin, during, late=0):
+def scatter_core(grads, outs, scratch, begin, during, late=0, gap=0):
     kinds = len(grads)
     (acc, precv, xr1, yr1, xr2, yr2, zup, zdn, fin) = scratch[:9]
     (ls, ps, pr, xs1, xm1, ys1, ym1, xs2, xm2, ys2, ym2, us, um, ds, dm, fs, fm, os) = scratch[9:]
@@ -883,18 +883,22 @@
     stages += [(5 + h, functools.partial(lambda h, i: stage4(i, h), h)) for h in range(cols)]
     ending = stages[-1][0]
 
-    assert len(during) <= chunks + ending
-
-    @pl.loop(0, chunks + ending)
+    assert len(during) <= chunks + gap + ending
+    early = (kinds - late) * cols
+
+    @pl.loop(0, chunks + gap + ending)
     def _(step):
         for i, extra in enumerate(during):
             pl.when(step == i)(functools.partial(extra, launch))
 
         for lag, stage in stages:
 
-            @pl.when((step >= lag) & (step - lag < chunks))
+            spot = step - lag
+            there = (spot >= 0) & (spot < early) | (spot >= early + gap) & (spot < chunks + gap)
+
+            @pl.when(there)
             def _():
-                stage(step - lag)
+                stage(jnp.where(spot < early, spot, spot - gap))
 
     @pl.loop(0, chunks)
     def _(i):
@@ -1033,50 +1037,6 @@
     )(values, cotangent)
 
 
-def turn_kernel(ctx_ref, stats_ref, give_ref, ctx_out, stats_out, give_out, send, recv, ssend, srecv, gl, gs, gr):
-    d, r, c = place()
-    peers = line_peers()
-    greet(plane_peers() + peers[:3] + peers[4:])
-
-    def move(j):
-        return rcopy(ctx_ref.at[c ^ j], ctx_out.at[c], send.at[j], recv.at[j], (d, r, c ^ j))
-
-    def tell(j):
-        return rcopy(stats_ref, stats_out.at[d, c], ssend.at[j - 1], srecv.at[j - 1], peers[j - 1])
-
-    for j in range(1, 8):
-        tell(j).start()
-    for j in (3, 2, 1):
-        move(j).start()
-    start, finish = give_moves(give_ref, give_out, gl, gs, gr)
-    start()
-    ctx_out[c] = ctx_ref[c]
-    stats_out[d, c] = stats_ref[...]
-    for j in range(1, 8):
-        tell(j).wait()
-    for j in (1, 2, 3):
-        move(j).wait()
-    finish()
-
-
-def turn_fast(d_ctx, stats, out_t, cid):
-    width, own = out_t.shape
-    dma = pltpu.SemaphoreType.DMA
-    return pl.pallas_call(
-        turn_kernel,
-        out_shape=[
-            jax.ShapeDtypeStruct(d_ctx.shape, d_ctx.dtype),
-            jax.ShapeDtypeStruct((2, 4) + stats.shape, stats.dtype),
-            jax.ShapeDtypeStruct((2, width // 4, 2 * own), out_t.dtype),
-        ],
-        in_specs=[VM, VM, HBM],
-        out_specs=[VM, VM, HBM],
-        scratch_shapes=[dma((4,)), dma((4,)), dma((7,)), dma((7,)), dma, dma((4,)), dma((2, 2))],
-        compiler_params=pltpu.CompilerParams(collective_id=cid, has_side_effects=True),
-        name="turn",
-    )(d_ctx, stats, out_t.reshape(4, width // 4, own))
-
-
 def sum_steps(src, total, parts, sems):
     d, r, c = place()
     peers = [(1 - d, r, c), (d, r ^ 1, c), (d, r ^ 2, c), (d, r, c ^ 1), (d, r, c ^ 2)]
@@ -1143,71 +1103,245 @@
     return steps, end
 
 
-def both(one, two):
-    def run(launch):
-        one()
-        two(launch)
-
-    return run
-
-
-def tail_kernel(kinds, *refs):
+highest = lax.Precision.HIGHEST
+
+
+def fine(a, b, contract=((1,), (0,))):
+    return lax.dot_general(a, b, (contract, ((), ())), precision=highest, preferred_element_type=f32)
+
+
+def same_head(size, part):
+    one = lax.broadcasted_iota(jnp.int32, (size, size), 0) // part
+    two = lax.broadcasted_iota(jnp.int32, (size, size), 1) // part
+    return (one == two).astype(f32)
+
+
+def student_stats(docs, scale, out_ref, seg_ref, proj_ref, vec_ref, hidden, logit, stats):
+    width = hidden.shape[1]
+    h = jnp.dot(out_ref[...], proj_ref[...], preferred_element_type=f32) + vec_ref[0:1]
+    pool = fine(h * vec_ref[1:2], same_head(width, SHD)) * scale
+    hidden[...] = h
+    logit[...] = pool
+    stats[0:8] = jnp.zeros((8, width), f32)
+    stats[8:16] = jnp.zeros((8, width), f32)
+    stats[16:24] = jnp.ones((8, width), f32)
+    for doc in range(docs):
+        mine = seg_ref[...] == doc
+        top = jnp.max(jnp.where(mine, pool, masked_value), axis=0, keepdims=True)
+        weight = jnp.where(mine, jnp.exp(pool - top), 0.0)
+        stats[doc : doc + 1] = jnp.sum(weight * h, axis=0, keepdims=True)
+        stats[8 + doc : 9 + doc] = top
+        stats[16 + doc : 17 + doc] = jnp.sum(weight, axis=0, keepdims=True)
+
+
+def student_grads(docs, classes, scale, once, row, out_ref, seg_ref, label_ref, vec_ref, mid_ref, cls_ref, hidden, logit, stats, small):
+    width = hidden.shape[1]
+    every = [stats[i, j] for i in range(stats.shape[0]) for j in range(stats.shape[1])]
+    top = every[0][8:16]
+    for one in every[1:]:
+        top = jnp.maximum(top, one[8:16])
+    total = jnp.zeros_like(top)
+    pooled = jnp.zeros_like(top)
+    for one in every:
+        factor = jnp.exp(one[8:16] - top)
+        total = total + one[16:24] * factor
+        pooled = pooled + one[0:8] * factor
+    pooled = pooled / total
+    middle = jnp.tanh(fine(pooled, mid_ref[...]) + vec_ref[2:3])
+    logits = fine(middle, cls_ref[...]) + vec_ref[3:4]
+    lane = lax.broadcasted_iota(jnp.int32, logits.shape, 1)
+    doc = lax.broadcasted_iota(jnp.int32, logits.shape, 0)
+    real = lane < classes
+    peak = jnp.max(jnp.where(real, logits, masked_value), axis=1, keepdims=True)
+    share = jnp.where(real, jnp.exp(logits - peak), 0.0)
+    share = share / jnp.sum(share, axis=1, keepdims=True)
+    d_logits = jnp.where(doc < docs, share - (label_ref[...] == lane).astype(f32), 0.0)
+    d_middle = fine(d_logits, cls_ref[...], ((1,), (1,))) * (1.0 - middle * middle)
+    d_pooled = fine(d_middle, mid_ref[...], ((1,), (1,)))
+    zeros = jnp.zeros((1, width), f32)
+    small[768:896] = fine(pooled, d_middle, ((0,), (0,))) * once
+    small[896:912] = fine(d_logits, middle, ((0,), (0,)))[0:16] * once
+    small[912:913] = jnp.sum(d_middle, axis=0, keepdims=True) * once
+    small[913:914] = jnp.sum(d_logits, axis=0, keepdims=True) * once
+    for at in range(4):
+        small[920 + 8 * at : 928 + 8 * at] = jnp.where(row == at, logits * once, 0.0)
+
+    heads = same_head(width, SHD)
+    base = fine(d_pooled * pooled, heads)
+    h, pool = hidden[...], logit[...]
+    top_t, total_t = jnp.zeros_like(h), jnp.ones_like(h)
+    back_t, base_t = jnp.zeros_like(h), jnp.zeros_like(h)
+    for doc in range(docs):
+        mine = seg_ref[...] == doc
+        top_t = jnp.where(mine, top[doc : doc + 1], top_t)
+        total_t = jnp.where(mine, total[doc : doc + 1], total_t)
+        back_t = jnp.where(mine, d_pooled[doc : doc + 1], back_t)
+        base_t = jnp.where(mine, base[doc : doc + 1], base_t)
+    share = jnp.exp(pool - top_t) / total_t
+    d_pool = share * (fine(back_t * h, heads) - base_t)
+    d_h = share * back_t + d_pool * vec_ref[1:2] * scale
+    small[914:915] = jnp.sum(d_h, axis=0, keepdims=True)
+    small[915:916] = jnp.sum(d_pool * h, axis=0, keepdims=True) * scale
+    for i in range(916, 920):
+        small[i : i + 1] = zeros
+    small[0:768] = fine(out_ref[...].astype(f32), d_h, ((0,), (0,)))
+
+
+def tail_kernel(docs, classes, scale, *refs):
+    kinds = 2
     grads, refs = refs[:kinds], refs[kinds:]
-    (q_ref, kv_ref, small_ref, x_ref, ctx_ref, resid_ref, w_ref), refs = refs[:7], refs[7:]
+    (q_ref, kv_ref, lse_ref, ctx_ref, dctx_ref, qseg_ref, kseg_ref), refs = refs[:7], refs[7:]
+    (out_ref, seg_ref, label_ref, proj_ref, svec_ref, mid_ref, cls_ref), refs = refs[:7], refs[7:]
+    vec_refs, refs = refs[:7], refs[7:]
+    (x_ref, ctx_all_ref, resid_ref, out_t_ref, w_ref), refs = refs[:5], refs[5:]
     outs, refs = refs[: kinds + 1], refs[kinds + 1 :]
-    (give_out, small_out), refs = refs[:2], refs[2:]
+    (give_out, out_out, small_out), refs = refs[:3], refs[3:]
     (total, theirs, dqkv, own_grads, dpad, weights, resid_t, give_src), refs = refs[:8], refs[8:]
+    (dctx, dq, dkv, kn, vn, q3, dc3, dq_scr, dkv_scr, bias_scr), refs = refs[:10], refs[10:]
+    (hidden, logit, stats, stats_all, small), refs = refs[:5], refs[5:]
     parts, refs = refs[:10], refs[10:]
-    (send, recv, psend, precv), sems, (wl, gl, gs, gr), scratch = refs[:4], refs[4:8], refs[8:12], refs[12:]
+    (send, recv, psend, precv), sems, (wl, gl, gs, gr), refs = refs[:4], refs[4:8], refs[8:12], refs[12:]
+    (dsend, drecv, ssend, srecv, ol, osend, orecv), scratch = refs[:7], refs[7:]
     d, r, c = place()
     pn = (1 - d, r, c)
-    deep, wide = kv_ref.shape[2], q_ref.shape[1]
+    tiles, deep, tile = kv_ref.shape
+    wide = deep // 2
+    heads = wide // HD
     full = dqkv.shape[1]
+    own = q_ref.shape[2]
     kv_rows, q_rows = pl.ds(0, deep), pl.ds(deep, wide)
-    greet(plane_peers() + [(d, r, c ^ j) for j in (1, 2, 3)])
-
-    def pair(j):
-        return rcopy(kv_ref.at[c ^ j, 1 - d], theirs.at[c ^ j], psend.at[j], precv.at[j], pn)
-
-    def kv(j):
-        return rcopy(total.at[c ^ j], dqkv.at[c, kv_rows], send.at[0, j], recv.at[0, j], (d, r, c ^ j))
-
-    def q(j):
-        return rcopy(q_ref.at[c ^ j], dqkv.at[c, q_rows], send.at[1, j], recv.at[1, j], (d, r, c ^ j))
-
-    for j in (3, 2, 1, 0):
-        pair(j).start()
+    peers = line_peers()
+    greet(plane_peers() + peers[:3] + peers[4:])
+
+    def to_heads(j):
+        return rcopy(dctx_ref.at[c ^ j], dctx.at[c], dsend.at[j], drecv.at[j], (d, r, c ^ j))
+
     for j in (3, 2, 1):
-        q(j).start()
+        to_heads(j).start()
+    dctx[c] = dctx_ref[c]
     load_w = pltpu.make_async_copy(w_ref, weights, wl)
     load_w.start()
-    steps, end = sum_steps(small_ref, small_out, parts, sems)
+
+    def tell(j):
+        return rcopy(stats, stats_all.at[d, c], ssend.at[j - 1], srecv.at[j - 1], peers[j - 1])
+
+    out_start, out_finish = give_moves(out_t_ref, out_out, ol, osend, orecv)
     start, finish = give_moves(give_src, give_out, gl, gs, gr)
+    steps, end = sum_steps(small, small_out, parts, sems)
+    pool_scale = SHD ** (-0.5)
 
     def begin():
-        for j in (3, 2, 1):
-            pair(j).wait_recv()
-            total[c ^ j] = kv_ref[c ^ j, d] + theirs[c ^ j]
-            kv(j).start()
-        pair(0).wait_recv()
-        dqkv[c, kv_rows] = kv_ref[c, d] + theirs[c]
-        dqkv[c, q_rows] = q_ref[c]
+        out_start()
+        student_stats(docs, pool_scale, out_ref, seg_ref, proj_ref, svec_ref, hidden, logit, stats)
+        for j in range(1, 8):
+            tell(j).start()
+        stats_all[d, c] = stats[...]
         spare = full - deep - wide
         for at in range(4):
-            dqkv[at, pl.ds(deep + wide, spare)] = jnp.zeros((spare, dqkv.shape[2]), bf16)
+            dqkv[at, pl.ds(deep + wide, spare)] = jnp.zeros((spare, own), bf16)
         resid_t[...] = resid_ref[...].T
         feats = x_ref.shape[1]
         blank = dpad.shape[1] - feats
         for row in range(4):
-            dpad[row, pl.ds(0, blank)] = jnp.zeros((blank, dpad.shape[2]), bf16)
+            dpad[row, pl.ds(0, blank)] = jnp.zeros((blank, own), bf16)
             dpad[row, pl.ds(blank, feats)] = resid_t[pl.ds(row * feats, feats)].astype(bf16)
-
+        at = 952
+        for ref in vec_refs:
+            for i in range(ref.shape[0]):
+                for j in range(ref.shape[1] // 128):
+                    small[at : at + 1] = ref[i : i + 1, j * 128 : (j + 1) * 128]
+                    at += 1
+        for i in range(at, small.shape[0]):
+            small[i : i + 1] = jnp.zeros((1, 128), f32)
+
+    def student(_):
+        for j in range(1, 8):
+            tell(j).wait_recv()
+        once = 1.0 / 8
+        student_grads(
+            docs, classes, pool_scale, once, r, out_ref, seg_ref, label_ref, svec_ref, mid_ref, cls_ref, hidden, logit,
+            stats_all, small,
+        )
+
+    def prepare(_):
+        @pl.loop(0, tiles)
+        def _(j):
+            kn[j] = kv_ref[j, pl.ds(0, wide)].astype(f32).T.astype(bf16)
+            vn[j] = kv_ref[j, pl.ds(wide, wide)].astype(f32).T.astype(bf16)
+            dkv_scr[j] = jnp.zeros((deep, tile), f32)
+
+        bias_scr[...] = jnp.zeros_like(bias_scr)
+        for j in (1, 2, 3):
+            to_heads(j).wait_recv()
+
+    ones = jnp.ones((8, own), bf16)
     across = (((1,), (1,)), ((), ()))
 
-    def arrived():
-        for j in (1, 2, 3):
-            q(j).wait_recv()
-            kv(j).wait_recv()
+    def attend_block(block, _):
+        q_at, dc_at = q_ref.at[pl.ds(block, 1)], dctx.at[pl.ds(block, 1)]
+        block_rows(q_at, heads, scale, q3)
+        block_rows(dc_at, heads, 1.0, dc3)
+        qseg = jnp.concatenate([qseg_ref[block]] * heads, axis=1)
+        lse = lse_ref[block]
+        product = ctx_ref[block].astype(f32) * dctx[block].astype(f32)
+        delta = jnp.concatenate(
+            [jnp.sum(product[h * HD : (h + 1) * HD], axis=0, keepdims=True) for h in range(heads)], axis=1
+        )
+        dq_scr[...] = jnp.zeros_like(dq_scr)
+        here = 2 * block + d
+
+        @pl.loop(jnp.maximum(here - 4, 0), jnp.minimum(here + 5, tiles))
+        def _(j):
+            s = jnp.dot(kn[j], q3[...], preferred_element_type=f32)
+            s = jnp.where(kseg_ref[j] == qseg, s, masked_value)
+            p = jnp.exp(s - lse)
+            d_p = jnp.dot(vn[j], dc3[...], preferred_element_type=f32)
+            d_s = (p * (d_p - delta)).astype(bf16)
+            p = p.astype(bf16)
+            for h in range(heads):
+                rows, lanes = pl.ds(h * HD, HD), slice(h * own, (h + 1) * own)
+                dq_scr[rows] += jnp.dot(kv_ref[j, rows], d_s[:, lanes], preferred_element_type=f32)
+                dkv_scr[j, rows] += lax.dot_general(q3[rows, lanes], d_s[:, lanes], across, preferred_element_type=f32)
+                low = pl.ds(wide + h * HD, HD)
+                dkv_scr[j, low] += lax.dot_general(dctx[block, rows], p[:, lanes], across, preferred_element_type=f32)
+
+        made = (dq_scr[...] * scale).astype(bf16)
+        dq[block] = made
+        bias_scr[:, :wide] += lax.dot_general(ones, made, across, preferred_element_type=f32)
+
+    def pair(j):
+        return rcopy(dkv.at[c ^ j, 1 - d], theirs.at[c ^ j], psend.at[j], precv.at[j], pn)
+
+    def kv(j):
+        return rcopy(total.at[c ^ j], dqkv.at[c, kv_rows], send.at[0, j], recv.at[0, j], (d, r, c ^ j))
+
+    def q(j):
+        return rcopy(dq.at[c ^ j], dqkv.at[c, q_rows], send.at[1, j], recv.at[1, j], (d, r, c ^ j))
+
+    def leave(_):
+        for j in (3, 2, 1, 0):
+            for core in range(2):
+                tile_at = 2 * (c ^ j) + core
+                dkv[c ^ j, core] = dkv_scr[tile_at].astype(bf16)
+            pair(j).start()
+            if j:
+                q(j).start()
+        dqkv[c, q_rows] = dq[c]
+        for j in (3, 2, 1):
+            pair(j).wait_recv()
+            total[c ^ j] = dkv[c ^ j, d] + theirs[c ^ j]
+            kv(j).start()
+        pair(0).wait_recv()
+        dqkv[c, kv_rows] = dkv[c, d] + theirs[c]
+
+        @pl.loop(0, 4)
+        def _(at):
+            for core in range(2):
+                some = dkv[at, core, pl.ds(wide, wide)]
+                bias_scr[:, wide:] += lax.dot_general(ones, some, across, preferred_element_type=f32)
+
+        for i in range(3):
+            small[pl.ds(1012 + 3 * c + i, 1)] = bias_scr[0:1, i * 128 : (i + 1) * 128]
 
     def make(at):
         lead = full - dpad.shape[1]
@@ -1215,19 +1349,26 @@
         @pl.loop(0, 4)
         def _(row):
             one = lax.dot_general(x_ref[row], dqkv[at], across, preferred_element_type=f32)
-            two = lax.dot_general(ctx_ref[at], dpad[row], across, preferred_element_type=f32)
+            two = lax.dot_general(ctx_all_ref[at], dpad[row], across, preferred_element_type=f32)
             shape = own_grads.shape[2:4] + (-1,)
             own_grads[at, row, :, :, :lead] = one[:, :lead].astype(bf16).reshape(shape)
             own_grads[at, row, :, :, lead:] = (one[:, lead:] + two).astype(bf16).reshape(shape)
 
-    def input_grad(launch):
+    def make_chunk(j, launch):
+        if j == 0:
+            for far in (1, 2, 3):
+                q(far).wait_recv()
+                kv(far).wait_recv()
+        make((0, 3, 1, 2)[j])
+        launch(kinds * 4 + j)
+
+    def input_grad(_):
         load_w.wait()
         feats = x_ref.shape[1]
 
         @pl.loop(0, 4)
         def _(row):
-            rows = pl.ds(pl.multiple_of(row * feats, 8), feats)
-            part = resid_t[rows]
+            part = resid_t[pl.ds(pl.multiple_of(row * feats, 8), feats)]
             for at in range(4):
                 w = weights[at, row].reshape(feats, full)
                 part = part + jnp.dot(w, dqkv[at], preferred_element_type=f32)
@@ -1235,65 +1376,90 @@
 
         start()
 
-    first = 4
-    extras = [lambda launch: None] * first
-    for j, at in enumerate((0, 3, 1, 2)):
-
-        def extra(launch, j=j, at=at):
-            if j == 0:
-                arrived()
-            make(at)
-            launch(kinds * 4 + j)
-
-        extras.append(extra)
-    extras.append(input_grad)
-    extras += [lambda launch: None] * (len(steps) - len(extras))
-    during = [both(step, extra) for step, extra in zip(steps, extras)]
-    scatter_core(list(grads) + [own_grads], outs, scratch, begin, during, late=1)
+    gap = 6
+    hooks = [[] for _ in range(8 + gap + 5)]
+    hooks[1].append(student)
+    hooks[2].append(prepare)
+    for block in range(4):
+        hooks[3 + block].append(functools.partial(attend_block, block))
+    hooks[7].append(leave)
+    for i, step in enumerate(steps):
+        hooks[8 + i].append(lambda launch, step=step: step())
+    for j in range(4):
+        hooks[7 + gap + j].append(functools.partial(make_chunk, j))
+    hooks[11 + gap].append(input_grad)
+
+    def run(todo, launch):
+        for one in todo:
+            one(launch)
+
+    during = [functools.partial(run, todo) for todo in hooks]
+    scatter_core(list(grads) + [own_grads], outs, scratch, begin, during, late=1, gap=gap)
     end()
     finish()
+    out_finish()
+    for j in range(1, 8):
+        tell(j).wait_send()
     for j in range(4):
         pair(j).wait_send()
     for j in (1, 2, 3):
+        to_heads(j).wait_send()
         q(j).wait_send()
         kv(j).wait_send()
 
 
-def tail_fast(grads, q, kv, small, x_t, ctx_t, resid, w_attn, cid):
-    kinds = len(grads)
+def tail_fast(docs, classes, scale, grads, attention, student, vectors, rest, out_t, w_attn, cid):
     n, w = grads[0].shape[3:]
+    q, kv = attention[:2]
     dma = pltpu.SemaphoreType.DMA
-    cols, _, wide, own = kv.shape
-    feats = x_t.shape[1]
-    parts = [pltpu.VMEM((small.shape[0] >> (i + 1), small.shape[1]), f32) for i in range(5)]
+    tiles, deep, own = kv.shape
+    wide = deep // 2
+    cols = tiles // 2
+    feats = rest[0].shape[1]
+    student_width = student[3].shape[1]
+    tall = 1024
+    parts = [pltpu.VMEM((tall >> (i + 1), 128), f32) for i in range(5)]
+    home = jax.ShapeDtypeStruct((2, feats, 2 * own), bf16)
     return pl.pallas_call(
-        functools.partial(tail_kernel, kinds),
-        out_shape=[jax.ShapeDtypeStruct((2, n, w), bf16)] * (kinds + 1)
-        + [
-            jax.ShapeDtypeStruct((2, feats, 2 * own), bf16),
-            jax.ShapeDtypeStruct(small.shape, f32),
-        ],
-        in_specs=[HBM] * kinds + [VM] * 6 + [HBM],
-        out_specs=[HBM] * (kinds + 1) + [HBM, VM],
+        functools.partial(tail_kernel, docs, classes, scale),
+        out_shape=[jax.ShapeDtypeStruct((2, n, w), bf16)] * 3 + [home, home, jax.ShapeDtypeStruct((tall, 128), f32)],
+        in_specs=[HBM] * 2 + [VM] * (len(attention) + len(student) + len(vectors) + len(rest)) + [HBM] * 2,
+        out_specs=[HBM] * 5 + [VM],
         scratch_shapes=[
-            pltpu.VMEM((cols, wide, own), bf16),
-            pltpu.VMEM((cols, wide, own), bf16),
+            pltpu.VMEM((cols, deep, own), bf16),
+            pltpu.VMEM((cols, deep, own), bf16),
             pltpu.VMEM((cols, w, own), bf16),
             pltpu.VMEM((4, 4, 2, n, w), bf16),
             pltpu.VMEM((4, 256, own), bf16),
             pltpu.VMEM((4, 4, 2, n, w), bf16),
             pltpu.VMEM((4 * feats, own), f32),
             pltpu.VMEM((4, feats, own), bf16),
+            pltpu.VMEM((cols, wide, own), bf16),
+            pltpu.VMEM((cols, wide, own), bf16),
+            pltpu.VMEM((cols, 2, deep, own), bf16),
+            pltpu.VMEM((tiles, own, wide), bf16),
+            pltpu.VMEM((tiles, own, wide), bf16),
+            pltpu.VMEM((wide, wide // HD * own), bf16),
+            pltpu.VMEM((wide, wide // HD * own), bf16),
+            pltpu.VMEM((wide, own), f32),
+            pltpu.VMEM((tiles, deep, own), f32),
+            pltpu.VMEM((8, deep), f32),
+            pltpu.VMEM((own, student_width), f32),
+            pltpu.VMEM((own, student_width), f32),
+            pltpu.VMEM((24, student_width), f32),
+            pltpu.VMEM((2, 4, 24, student_width), f32),
+            pltpu.VMEM((tall, 128), f32),
         ]
         + parts * 2
         + [dma((2, 4)), dma((2, 4)), dma((4,)), dma((4,)), dma((5,)), dma((5,)), dma((5,)), dma((5,))]
         + [dma, dma, dma((4,)), dma((2, 2))]
-        + scatter_scratch(kinds + 1, n, w, bf16),
+        + [dma((4,)), dma((4,)), dma((7,)), dma((7,)), dma, dma((4,)), dma((2, 2))]
+        + scatter_scratch(3, n, w, bf16),
         compiler_params=pltpu.CompilerParams(
-            collective_id=cid, has_side_effects=True, vmem_limit_bytes=58 * 1024 * 1024
+            collective_id=cid, has_side_effects=True, vmem_limit_bytes=60 * 1024 * 1024
         ),
         name="tail",
-    )(*grads, q, kv, small, x_t, ctx_t, resid, w_attn)
+    )(*grads, *attention, *student, *vectors, *rest, out_t.reshape(4, feats, own), w_attn)
 
 
 def dot(a, b, contract=((1,), (0,))):
@@ -1387,95 +1553,6 @@
         ),
         name="attn_fwd",
     )(bounds, q, kv, qseg, kseg)
-
-
-def attn_bwd_kernel(
-    heads, scale, bounds, q_ref, kv_ref, qseg_ref, kseg_ref, lse_ref, ctx_ref, dctx_ref,
-    dq_ref, dkv_ref, kn, vn, q3, dc3, dq_scr, dkv_scr,
-):
-    step = pl.program_id(0)
-    tiles, _, tile = kv_ref.shape
-    wide = heads * HD
-    own = q_ref.shape[-1]
-
-    @pl.when(step == 0)
-    def _():
-        @pl.loop(0, tiles)
-        def _(j):
-            kn[j] = kv_ref[j, pl.ds(0, wide)].astype(f32).T.astype(bf16)
-            vn[j] = kv_ref[j, pl.ds(wide, wide)].astype(f32).T.astype(bf16)
-            dkv_scr[j] = jnp.zeros((2 * wide, tile), f32)
-
-    block_rows(q_ref, heads, scale, q3)
-    block_rows(dctx_ref, heads, 1.0, dc3)
-    low, high = bounds[step, 0], bounds[step, 1]
-    qseg = jnp.concatenate([qseg_ref[0]] * heads, axis=1)
-    lse = lse_ref[0]
-    product = ctx_ref[0].astype(f32) * dctx_ref[0].astype(f32)
-    delta = jnp.concatenate(
-        [jnp.sum(product[h * HD : (h + 1) * HD], axis=0, keepdims=True) for h in range(heads)], axis=1
-    )
-    dq_scr[...] = jnp.zeros_like(dq_scr)
-
-    @pl.loop(low, high)
-    def _(j):
-        s = dot(kn[j], q3[...])
-        s = jnp.where(kseg_ref[j] == qseg, s, masked_value)
-        p = jnp.exp(s - lse)
-        d_p = dot(vn[j], dc3[...])
-        d_s = (p * (d_p - delta)).astype(bf16)
-        p = p.astype(bf16)
-        for h in range(heads):
-            rows, lanes = pl.ds(h * HD, HD), slice(h * own, (h + 1) * own)
-            dq_scr[rows] += dot(kv_ref[j, rows], d_s[:, lanes])
-            dkv_scr[j, rows] += dot(q3[rows, lanes], d_s[:, lanes], ((1,), (1,)))
-            deep = pl.ds(wide + h * HD, HD)
-            dkv_scr[j, deep] += dot(dctx_ref[0, rows], p[:, lanes], ((1,), (1,)))
-
-    dq_ref[0] = (dq_scr[...] * scale).astype(bf16)
-
-    @pl.when(step == pl.num_programs(0) - 1)
-    def _():
-        @pl.loop(0, tiles)
-        def _(j):
-            dkv_ref[j] = dkv_scr[j].astype(bf16)
-
-
-def attn_bwd(bounds, q, kv, qseg, kseg, lse, ctx, dctx, scale):
-    blocks, wide, own = q.shape
-    tiles, _, tile = kv.shape
-    heads = wide // HD
-    rowed = pl.BlockSpec((1, wide, own), lambda i, b: (i, 0, 0))
-    return pl.pallas_call(
-        functools.partial(attn_bwd_kernel, heads, scale),
-        out_shape=[jax.ShapeDtypeStruct(q.shape, bf16), jax.ShapeDtypeStruct(kv.shape, bf16)],
-        grid_spec=pltpu.PrefetchScalarGridSpec(
-            num_scalar_prefetch=1,
-            grid=(blocks,),
-            in_specs=[
-                rowed,
-                pl.BlockSpec(kv.shape, lambda i, b: (0, 0, 0)),
-                pl.BlockSpec((1, 1, own), lambda i, b: (i, 0, 0)),
-                pl.BlockSpec(kseg.shape, lambda i, b: (0, 0, 0)),
-                pl.BlockSpec((1, 1, heads * own), lambda i, b: (i, 0, 0)),
-                rowed,
-                rowed,
-            ],
-            out_specs=[rowed, pl.BlockSpec(kv.shape, lambda i, b: (0, 0, 0))],
-            scratch_shapes=[
-                pltpu.VMEM((tiles, tile, wide), bf16),
-                pltpu.VMEM((tiles, tile, wide), bf16),
-                pltpu.VMEM((wide, heads * own), bf16),
-                pltpu.VMEM((wide, heads * own), bf16),
-                pltpu.VMEM((wide, own), f32),
-                pltpu.VMEM((tiles, 2 * wide, tile), f32),
-            ],
-        ),
-        compiler_params=pltpu.CompilerParams(
-            dimension_semantics=("arbitrary",), vmem_limit_bytes=48 * 1024 * 1024
-        ),
-        name="attn_bwd",
-    )(bounds, q, kv, qseg, kseg, lse, ctx, dctx)
 
 
 def fast_local(
@@ -1580,18 +1657,6 @@
     normed_two, inv_two = normalize(hidden_one + ffn_out)
     layer_out = (normed_two * gain_two + bias_two).astype(bf16)
 
-    student_h = mm(layer_out, s_proj_all, ((1,), (0,))) + s_bias
-    head_parts = student_h.reshape(own, SH, SHD)
-    pool_logit = jnp.sum(head_parts * query_heads, axis=-1) * pool_scale
-    member = (seg_own[:, None] == doc_ids[None, :])[:, :, None]
-    masked = jnp.where(member, pool_logit[:, None, :], masked_value)
-    local_top = jnp.max(masked, axis=0)
-    local_exp = jnp.where(member, jnp.exp(masked - local_top[None]), 0.0)
-    local_total = jnp.sum(local_exp, axis=0)
-    local_sum = jnp.einsum("tdh,thk->dhk", local_exp, head_parts, precision=highest)
-    stats = jnp.concatenate([local_top[..., None], local_total[..., None], local_sum], axis=-1)
-    stats = jnp.pad(stats.reshape(-1), (0, 8 * 128 - stats.size)).reshape(8, 128)
-
     d_out = c_parts.reshape(width, own).T.astype(f32)
     g_ln2_gain = jnp.sum(d_out * normed_two, axis=0)
     g_ln2_bias = jnp.sum(d_out, axis=0)
@@ -1613,83 +1678,32 @@
     d_attn = d_resid_one.astype(bf16)
     g_out_bias = jnp.sum(d_attn.astype(f32), axis=0)
     d_ctx = mm(w_out_all, d_attn, ((1,), (1,))).astype(bf16)
-    d_ctx, stats, out = turn_fast(d_ctx.reshape(cols, width_col, own), stats, layer_out.T, 4)
-
-    stats = stats.reshape(cols * parts, -1)[:, : docs_count * SH * (SHD + 2)]
-    stats = stats.reshape(cols * parts, docs_count, SH, SHD + 2)
-    tops, totals, sums = stats[..., 0], stats[..., 1], stats[..., 2:]
-    doc_top = jnp.max(tops, axis=0)
-    factors = jnp.exp(tops - doc_top[None])
-    doc_total = jnp.sum(totals * factors, axis=0)
-    pooled_heads = jnp.sum(sums * factors[..., None], axis=0) / doc_total[:, :, None]
-    pooled = pooled_heads.reshape(docs_count, student_width)
-    middle = jnp.tanh(jnp.dot(pooled, s_mid, precision=highest) + s_mid_bias)
-    logit_rows = jnp.dot(middle, s_cls, precision=highest) + s_cls_bias
-    logit_top = jnp.max(logit_rows, axis=-1, keepdims=True)
-    logit_exp = jnp.exp(logit_rows - logit_top)
-    one_hot = (label_seq[:, None] == class_ids[None, :]).astype(f32)
-    d_logits = logit_exp / jnp.sum(logit_exp, axis=-1, keepdims=True) - one_hot
-    g_cls = jnp.dot(middle.T, d_logits, precision=highest)
-    g_cls_bias = jnp.sum(d_logits, axis=0)
-    d_middle = jnp.dot(d_logits, s_cls.T, precision=highest) * (1.0 - middle * middle)
-    g_mid = jnp.dot(pooled.T, d_middle, precision=highest)
-    g_mid_bias = jnp.sum(d_middle, axis=0)
-    d_pooled = jnp.dot(d_middle, s_mid.T, precision=highest).reshape(docs_count, SH, SHD)
-    shares = jnp.where(member, jnp.exp(masked - doc_top[None]), 0.0) / doc_total[None]
-    d_share = jnp.einsum("dhk,thk->tdh", d_pooled, head_parts, precision=highest)
-    base_term = jnp.sum(d_pooled * pooled_heads, axis=-1)
-    d_pool_logit = jnp.sum(shares * (d_share - base_term[None]), axis=1)
-    d_heads = jnp.einsum("tdh,dhk->thk", shares, d_pooled, precision=highest)
-    d_heads = d_heads + d_pool_logit[:, :, None] * query_heads[None] * pool_scale
-    g_query = (jnp.sum(d_pool_logit[:, :, None] * head_parts, axis=0) * pool_scale).reshape(-1)
-    d_student = d_heads.reshape(own, student_width)
-    g_sbias = jnp.sum(d_student, axis=0)
-    g_sproj = jnp.dot(layer_out.astype(f32).T, d_student, precision=highest)
-
-    d_q, d_kv = attn_bwd(bounds, queries, kv, q_rows, k_rows, lse, context, d_ctx, score_scale)
-    at_seq = (jnp.arange(seqs) == row_index).astype(f32)[:, None]
-    at_heads = (jnp.arange(cols) == col_index).astype(f32)[:, None, None]
-    g_q_bias = jnp.sum(d_q.astype(f32), axis=(0, 2))
-    g_v_bias = jnp.sum(d_kv[:, width_col:].astype(f32), axis=(0, 2))
-    once = 1.0 / (parts * cols)
-    small = (
-        g_sproj,
-        jnp.stack([g_q_bias, g_v_bias])[None] * at_heads,
-        g_in_bias,
-        g_out_bias,
-        g_ln1_gain,
-        g_ln1_bias,
-        g_back_bias,
-        g_ln2_gain,
-        g_ln2_bias,
-        g_sbias,
-        g_query,
-        g_mid * once,
-        g_mid_bias * once,
-        g_cls * once,
-        logit_rows.reshape(1, -1) * (at_seq * once),
-        g_cls_bias * once,
+    blocked = (cols, rows, parts, width_row // parts, -1)
+    lane_pad = ((0, 0), (0, 128 - class_count))
+    student_vectors = jnp.stack([s_bias, s_query, s_mid_bias, jnp.pad(s_cls_bias, (0, 128 - class_count))])
+    student_vectors = jnp.pad(student_vectors, ((0, 4), (0, 0)))
+    g_in, g_back, g_attn, grad_tokens, out, small = tail_fast(
+        docs_count,
+        class_count,
+        score_scale,
+        [g_in.astype(bf16).reshape(blocked), g_back.astype(bf16).reshape(blocked)],
+        [queries, kv, lse, context, d_ctx.reshape(cols, width_col, own), q_rows, k_rows],
+        [
+            layer_out,
+            seg_own[:, None],
+            jnp.pad(label_seq, (0, 8 - docs_count))[:, None],
+            s_proj_all,
+            student_vectors,
+            s_mid,
+            jnp.pad(s_cls, lane_pad),
+        ],
+        [g_in_bias]
+        + [v[None] for v in (g_out_bias, g_ln1_gain, g_ln1_bias, g_back_bias, g_ln2_gain, g_ln2_bias)],
+        [x_parts, ctx_parts, d_resid_one],
+        layer_out.T,
+        w_attn,
+        4,
     )
-    flat = jnp.concatenate([part.reshape(-1) for part in small])
-    tall = -(-flat.shape[0] // (128 * 256)) * 256
-    flat = jnp.pad(flat, (0, tall * 128 - flat.shape[0])).reshape(tall, 128)
-    blocked = (cols, rows, parts, width_row // parts, -1)
-    g_in, g_back, g_attn, grad_tokens, flat = tail_fast(
-        [g_in.astype(bf16).reshape(blocked), g_back.astype(bf16).reshape(blocked)],
-        d_q,
-        d_kv.reshape(cols, parts, 2 * width_col, own),
-        flat,
-        x_parts,
-        ctx_parts,
-        d_resid_one,
-        w_attn,
-        5,
-    )
-    flat = flat.reshape(-1)
-    sums_all, at = [], 0
-    for part in small:
-        sums_all.append(flat[at : at + part.size].reshape(part.shape))
-        at += part.size
     g_in, g_back, g_attn = [part.reshape(width_row, -1).astype(f32) for part in (g_in, g_back, g_attn)]
     g_qkv = g_attn[:, : 3 * width_col].reshape(width_row, 3, heads_dev, HD)
     g_qkv = jnp.stack([g_qkv[:, 2], g_qkv[:, 0], g_qkv[:, 1]], axis=2).reshape(width_row, -1)
@@ -1700,14 +1714,17 @@
     def at_row(part):
         return lax.dynamic_slice_in_dim(part, row_index * width_row, width_row)
 
-    (
-        g_sproj, g_qkv_bias, g_in_bias, g_out_bias, g_ln1_gain, g_ln1_bias, g_back_bias, g_ln2_gain,
-        g_ln2_bias, g_sbias, g_query, g_mid, g_mid_bias, g_cls, logits, g_cls_bias,
-    ) = sums_all
+    g_sproj, g_mid, g_cls = small[:width], small[width : width + 128], small[width + 128 : width + 144].T
+    g_mid_bias, g_cls_bias, g_sbias, g_query = [small[width + 144 + i] for i in range(4)]
+    logits = small[width + 152 : width + 184].reshape(seqs, 8, 128)[:, :docs_count, :class_count]
+    g_in_bias = small[width + 184 : width + 208].reshape(cols, hidden_col)
+    vector_sums = small[width + 208 : width + 244].reshape(6, width)
+    g_out_bias, g_ln1_gain, g_ln1_bias, g_back_bias, g_ln2_gain, g_ln2_bias = [vector_sums[i] for i in range(6)]
+    g_qkv_bias = small[width + 244 :].reshape(cols, 2, width_col)
     logits = lax.dynamic_slice_in_dim(logits, dp_index * (seqs // parts), seqs // parts)
     return (
         out,
-        logits.reshape(seqs // parts, docs_count, class_count),
+        logits,
         grad_tokens.astype(f32),
         g_qkv,
         at_col(g_qkv_bias),
@@ -1726,8 +1743,8 @@
         g_query,
         g_mid,
         g_mid_bias,
-        g_cls,
-        g_cls_bias,
+        g_cls[:, :class_count],
+        g_cls_bias[:class_count],
     )
 
 

time: 371 us -> 354 us (0.954)
  Pallas kernels: 240 us -> 254 us
  matrix products: 42 us -> 31.1 us
  local copies, waits for them, and re-layouts: 62.8 us -> 52.1 us
  other arithmetic: 21 us -> 14.7 us
    pallas_call x3 -> x1, Pallas kernels: 125 us -> 138 us  [tail_fast(): pl.pallas_call(functools.partial(tail_kernel, docs, classes, scale), out_...]
    concatenate x2 -> x0, local copies, waits for them, and re-layouts: 7.87 us -> none  [the longest x1 7.86 us: fast_local(): flat = jnp.concatenate([part.reshape(-1) for part in small])]
    dot_general x10 -> x0, matrix products: 6.23 us -> none  [the longest x1 0.96 us: fast_local(): logit_rows = jnp.dot(middle, s_cls, precision=highest) + s_cls_bias]
    broadcast_in_dim x2 -> x10, local copies, waits for them, and re-layouts: 0.2 us -> 5.11 us  [the longest x6 3.62 us: fast_local(): v[None]]
    slice x11 -> x5, local copies, waits for them, and re-layouts: 8.82 us -> 5.09 us  [the longest x1 1.47 us: fast_local(): small[width:width + 128]]
    unnamed x114 -> x70, local copies, waits for them, and re-layouts: 16 us -> 12.9 us
where the time goes in v1:
time: 354 us; the launch traced here: 353 us
  Pallas kernels  254 us (72%)
  local copies, waits for them, and re-layouts  52.1 us (15%)
  matrix products  31.1 us (9%)
  other arithmetic  14.7 us (4%)
    pallas_call x1, Pallas kernels, tail_fast(): pl.pallas_call(functools.partial(tail_kernel, docs, classes, scale), out_...  138 us
    pallas_call x1, Pallas kernels, gather_fast(): pl.pallas_call(functools.partial(gather_kernel, kinds), out_shape=[jax.Sh...  92.1 us
    pallas_call x1, Pallas kernels, swap_fast(): pl.pallas_call(swap_kernel, out_shape=[jax.ShapeDtypeStruct(values.shape,...  14.6 us
    unnamed x70, local copies, waits for them, and re-layouts  12.9 us
    dot_general x1, matrix products, fast_local(): jnp.einsum('td,cdn->ctn', hidden_low, w_in_all, preferred_element_type=f32)  10.1 us
    pallas_call x1, Pallas kernels, attn_fwd(): pl.pallas_call(functools.partial(attn_fwd_kernel, heads, scale), out_shap...  9.07 us

profile of v1, /device:TPU:0, one launch (start us, length us, event | category | flops | bytes accessed | tf_op | source)
XLA Modules:
  0.0 352.7 jit_solution(3765217771316326731)
XLA Ops:
  0.7 0.7 pad_bitcast_fusion.1
  1.4 0.8 fusion.59
  2.2 1.3 select_maximum_fusion.refs_13_
  3.5 0.7 pad_add_fusion.refs_5_
  4.3 0.7 bitcast_convert_fusion.4
  5.0 0.9 concatenate.18
  5.9 0.8 copy.140
  6.7 0.6 pad.29.refs_15_
  7.3 0.7 constant_dynamic-slice_fusion.8.refs_2_
  8.0 1.6 constant_dynamic-slice_fusion.7.refs_3_
  9.6 1.1 copy.122
  11.1 0.9 copy-done.9
  12.0 0.9 copy-done.10
  12.9 1.0 copy-done.11
  13.9 92.1 %head.1 = (bf16[4,4,2,96,768]{4,3,2,1,0:T(8,128)(2,1)S(1)}, f32[4,4,2,48,128]{4,3,2,1,0:T(8,128)S(1)}, bf16[4,4,2,96,768]{4,3,2,1,0:T(8,128)(2,1)}, bf16[4,4,2,9...) custom-call(bf16[96,768]{1,0:T(8,128)(2,1)S(1)} %fusion.41.refs_0_, ...), custom_call_target="tpu_custom_call" | custom-call | tf_op jit(solution)/shard_map/head/pallas_call | solution.py:728
  106.0 1.0 copy-done.3
  107.0 2.1 copy-done.5
  110.4 1.4 fusion.58
  111.9 0.7 copy.145.refs_11_
  113.3 0.8 copy.144.refs_10_
  114.1 1.2 reshape.323
  115.3 0.8 slice.204
  116.1 0.7 slice.200
  116.9 1.1 slice.243
  118.1 0.7 copy.139
  119.5 1.1 copy.126
  120.6 0.9 reshape.349.kseg_ref.refs_8_
  121.6 9.1 %attn_fwd.1 = (bf16[4,192,256]{2,1,0:T(8,128)(2,1)S(1)}, f32[4,1,768]{2,1,0:T(1,128)S(1)}) custom-call(s32[4,2]{1,0:T(4,128)S(1)} %pad_add_fusion.1.bounds, bf16[4,192,256]{2,1,0:T(8,128)(2,1)S(1)} %get-tuple-element.44.q_ref.refs_2_, bf16[8,384,256]{2,1,0:T(8,128)(2,1)S(1)} %bitcast.264, s32[4,1,256]{2,1,0:T(1,128)S(1)} %constant_dynamic-slice_fusion.6.qseg_ref.refs_7_, ...), custom_call_target="tpu_custom_call" | custom-call | tf_op jit(solution)/shard_map/attn_fwd/pallas_call | solution.py:1525
  130.6 0.7 copy-done.7
  132.0 14.6 %swap.1 = (bf16[4,192,256]{2,1,0:T(8,128)(2,1)}, bf16[4,192,256]{2,1,0:T(8,128)(2,1)}) custom-call(bf16[4,192,256]{2,1,0:T(8,128)(2,1)} %copy-done.7, bf16[2,192,512]{2,1,0:T(8,128)(2,1)} %cot.1), custom_call_target="tpu_custom_call" | custom-call | tf_op jit(solution)/shard_map/swap/pallas_call | solution.py:1026
  146.6 1.2 convert_reduce_fusion.3
  147.8 0.7 broadcast_in_dim.46.refs_22_
  148.5 2.1 copy.136
  150.6 2.0 fusion.57
  153.3 10.1 %fusion.9 = (bf16[4,256,768]{2,1,0:T(8,128)(2,1)S(1)}, f32[4,256,768]{2,1,0:T(8,128)}, f32[4,768,256]{1,2,0:T(8,128)}) fusion(f32[4,768]{1,0:T(4,128)S(1)} %bitcast.282, bf16[4,768,768]{2,1,0:T(8,128)(2,1)S(1)} %bitcast.291, f32[256,768]{1,0:T(8,128)S(1)} %get-tuple-element.152, f32[768]{0:T(1024)S(1)} %add.193, f32[768]{0:T(1024)S(1)} %mul.181, ...), kind=kOutput, calls=%fused_computation.17 | convolution fusion | flops 1260847104 | bytes 13389824 | tf_op jit(solution)/shard_map/td,cdn->ctn/dot_general | solution.py:1653
  163.4 2.4 fusion.54
  165.8 1.4 multiply_reduce_fusion.3
  167.6 0.9 copy.142
  168.5 2.4 fusion.33
  171.6 1.6 convert_reduce_fusion.1
  173.2 6.2 %convert_reduce_fusion = (f32[4,768]{1,0:T(4,128)}, bf16[4,256,768]{2,1,0:T(8,128)(2,1)S(1)}) fusion(f32[4,256,768]{2,1,0:T(8,128)S(1)} %copy-done.26, bf16[4,768,768]{2,1,0:T(8,128)(2,1)} %bitcast.295, f32[256,768]{1,0:T(8,128)S(1)} %get-tuple-element.144, f32[4,768,256]{1,2,0:T(8,128)} %get-tuple-element.174, f32[4,768]{1,0:T(4,128)S(1)} %bitcast.283), kind=kOutput, calls=%fused_computation.18 | convolution fusion | flops 1221522432 | bytes 13393920 | tf_op jit(solution)/shard_map/td,cdn->ctn/dot_general | solution.py:1667
  180.0 1.7 multiply_reduce_fusion
  182.6 1.3 convolution_convert_fusion.2
  185.0 3.8 %convolution_convert_fusion.1 = bf16[4,768,768]{1,2,0:T(8,128)(2,1)} fusion(bf16[4,256,768]{2,1,0:T(8,128)(2,1)S(1)} %get-tuple-element.178, f32[256,768]{1,0:T(8,128)S(1)} %get-tuple-element.152, f32[768]{0:T(1024)S(1)} %add.193, f32[768]{0:T(1024)S(1)} %mul.181, f32[256]{0:T(256)S(1)} %add_rsqrt_fusion.1, f32[256]{0:T(256)S(1)} %broadcast_multiply_fusion.5), kind=kOutput, calls=%fused_computation.33 | convolution fusion | flops 1211301888 | bytes 7086080 | tf_op jit(solution)/shard_map/td,ctn->cdn/dot_general | solution.py:1671
  188.8 3.7 %convolution_convert_fusion = bf16[4,768,768]{1,2,0:T(8,128)(2,1)} fusion(bf16[4,256,768]{2,1,0:T(8,128)(2,1)S(1)} %copy-done.18, f32[256,768]{1,0:T(8,128)S(1)} %get-tuple-element.144), kind=kOutput, calls=%fused_computation.32 | convolution fusion | flops 1210515456 | bytes 7077888 | tf_op jit(solution)/shard_map/td,ctn->cdn/dot_general | solution.py:1666
  192.5 137.9 %tail.1 = (bf16[2,96,768]{2,1,0:T(8,128)(2,1)}, bf16[2,96,768]{2,1,0:T(8,128)(2,1)}, bf16[2,96,768]{2,1,0:T(8,128)(2,1)}, bf16[2,192,512]{2,1,0:T(8,128)(2,1)}, ...) custom-call(bf16[4,4,2,96,768]{4,3,2,1,0:T(8,128)(2,1)} %bitcast.266, bf16[4,4,2,96,768]{4,3,2,1,0:T(8,128)(2,1)} %bitcast.267, ...), custom_call_target="tpu_custom_call" | custom-call | tf_op jit(solution)/shard_map/tail/pallas_call | solution.py:1423
  330.4 1.2 slice_bitcast_fusion.14
  331.6 1.3 slice_bitcast_fusion.15
  332.9 1.3 slice_bitcast_fusion.7
  334.2 0.7 slice.177
  335.6 0.7 slice.182
  336.9 0.7 slice_bitcast_fusion.6
  338.2 0.8 slice_bitcast_fusion.8
  339.0 0.6 dynamic_slice.75
  342.8 1.5 slice.189
  344.3 1.0 slice.186
  345.3 0.7 constant_dynamic-slice_fusion.1
  346.0 1.0 bitcast_convert_fusion.3
  347.0 0.8 slice.214
  348.2 1.0 copy.149
  349.2 0.9 bitcast_convert_fusion.2
  350.1 0.9 bitcast_convert_fusion.1
  351.0 1.0 convert_element_type.129
  351.9 0.7 copy.166
  (124 shorter events, 13.7 us)
Async XLA Ops:
  0.7 6.7 %copy-start = (bf16[192,768]{1,0:T(8,128)(2,1)S(1)}, bf16[192,768]{1,0:T(8,128)(2,1)}, u32[]{:S(2)}) copy-start(bf16[192,768]{1,0:T(8,128)(2,1)} %param.33) | copy-start | bytes 884740
  0.7 10.3 %copy-start.23 = (bf16[192,192]{1,0:T(8,128)(2,1)S(1)}, bf16[192,192]{1,0:T(8,128)(2,1)}, u32[]{:S(2)}) copy-start(bf16[192,192]{1,0:T(8,128)(2,1)} %param.29) | copy-start | bytes 221188
  11.0 0.9 copy-start.9
  12.0 0.9 copy-start.10
  12.9 1.0 copy-start.11
  106.0 1.0 copy-start.3
  107.0 2.1 copy-start.5
  109.1 10.4 %copy-start.8 = (bf16[4,192,256]{2,1,0:T(8,128)(2,1)}, bf16[4,192,256]{2,1,0:T(8,128)(2,1)S(1)}, u32[]{:S(2)}) copy-start(bf16[4,192,256]{2,1,0:T(8,128)(2,1)S(1)} %get-tuple-element.42.refs_23_) | copy-start | bytes 1179652
  109.1 12.4 %copy-start.2 = (bf16[4,2,384,256]{3,2,1,0:T(8,128)(2,1)}, bf16[4,2,384,256]{3,2,1,0:T(8,128)(2,1)S(1)}, u32[]{:S(2)}) copy-start(bf16[4,2,384,256]{3,2,1,0:T(8,128)(2,1)S(1)} %get-tuple-element.45) | copy-start | bytes 4718596
  109.1 12.4 %copy-start.6 = (bf16[4,192,256]{2,1,0:T(8,128)(2,1)}, bf16[4,192,256]{2,1,0:T(8,128)(2,1)S(1)}, u32[]{:S(2)}) copy-start(bf16[4,192,256]{2,1,0:T(8,128)(2,1)S(1)} %get-tuple-element.44.q_ref.refs_2_) | copy-start | bytes 1179652
  109.1 0.7 copy-start.24
  111.9 9.6 %copy-start.12 = (s32[4,1,256]{2,1,0:T(1,128)}, s32[4,1,256]{2,1,0:T(1,128)S(1)}, u32[]{:S(2)}) copy-start(s32[4,1,256]{2,1,0:T(1,128)S(1)} %constant_dynamic-slice_fusion.6.qseg_ref.refs_7_) | copy-start | bytes 12292
  121.5 31.0 %copy-start.1 = (s32[8,256,1]{2,1,0:T(8,128)}, s32[8,256,1]{2,1,0:T(8,128)S(1)}, u32[]{:S(2)}) copy-start(s32[8,256,1]{2,1,0:T(8,128)S(1)} %reshape.349.kseg_ref.refs_8_) | copy-start | bytes 24580
  130.6 0.7 copy-start.7
  131.4 0.6 copy-start.13
  132.0 18.6 %copy-start.4 = (bf16[768,768]{1,0:T(8,128)(2,1)S(1)}, bf16[768,768]{1,0:T(8,128)(2,1)}, u32[]{:S(2)}) copy-start(bf16[768,768]{1,0:T(8,128)(2,1)} %copy-done.3) | copy-start | bytes 3538948
  150.6 2.7 copy-start.25
  150.6 12.8 %slice-start.2 = ((s8[4718592]{0:T(1024)(128)(4,1)}), s8[4194304]{0:T(1024)(128)(4,1)S(1)}, s32[]{:S(2)}) async-start(s8[4718592]{0:T(1024)(128)(4,1)} %bitcast.296), calls=%async_computation.2 | async-start | bytes 8388608
  153.3 10.1 %slice-start.3 = ((s8[4718592]{0:T(1024)(128)(4,1)}), s8[524288]{0:T(1024)(128)(4,1)S(1)}, s32[]{:S(2)}) async-start(s8[4718592]{0:T(1024)(128)(4,1)} %bitcast.296), calls=%async_computation.3 | async-start | bytes 1048576
  163.3 2.5 copy-start.17
  163.4 3.9 %copy-start.14 = (f32[768,256]{0,1:T(8,128)S(1)}, f32[768,256]{0,1:T(8,128)}, u32[]{:S(2)}) copy-start(f32[768,256]{0,1:T(8,128)} %copy.126) | copy-start | bytes 2359300
  165.8 2.7 copy-start.15
  168.5 4.6 %copy-start.26 = (f32[4,256,768]{2,1,0:T(8,128)S(1)}, f32[4,256,768]{2,1,0:T(8,128)}, u32[]{:S(2)}) copy-start(f32[4,256,768]{2,1,0:T(8,128)} %get-tuple-element.150) | copy-start | bytes 9437188
  171.6 8.4 %slice-start = ((s8[4718592]{0:T(1024)(128)(4,1)}), s8[4194304]{0:T(1024)(128)(4,1)S(1)}, s32[]{:S(2)}) async-start(s8[4718592]{0:T(1024)(128)(4,1)} %bitcast.292), calls=%async_computation | async-start | bytes 8388608
  173.1 6.8 %slice-start.1 = ((s8[4718592]{0:T(1024)(128)(4,1)}), s8[524288]{0:T(1024)(128)(4,1)S(1)}, s32[]{:S(2)}) async-start(s8[4718592]{0:T(1024)(128)(4,1)} %bitcast.292), calls=%async_computation.1 | async-start | bytes 1048576
  182.6 6.2 %copy-start.16 = (f32[256,768]{1,0:T(8,128)}, f32[256,768]{1,0:T(8,128)S(1)}, u32[]{:S(2)}) copy-start(f32[256,768]{1,0:T(8,128)S(1)} %get-tuple-element.146.refs_25_) | copy-start | bytes 2359300
  185.0 3.8 %copy-start.18 = (bf16[4,256,768]{2,1,0:T(8,128)(2,1)S(1)}, bf16[4,256,768]{2,1,0:T(8,128)(2,1)}, u32[]{:S(2)}) copy-start(bf16[4,256,768]{2,1,0:T(8,128)(2,1)} %copy-done.17) | copy-start | bytes 4718596
  347.8 1.4 copy-start.22
  347.8 2.3 copy-start.21
  348.0 2.9 copy-start.20
  348.1 3.8 %copy-start.19 = (bf16[2,192,512]{2,1,0:T(8,128)(2,1)S(1)}, bf16[2,192,512]{2,1,0:T(8,128)(2,1)}, u32[]{:S(2)}) copy-start(bf16[2,192,512]{2,1,0:T(8,128)(2,1)} %get-tuple-element.203) | copy-start | bytes 1179652

commit v2 on v1

--- a/solution.py
+++ b/solution.py
@@ -469,25 +469,63 @@
     return moves
 
 
-def gather_kernel(kinds, *refs):
-    shards, refs = refs[:kinds], refs[kinds:]
-    (tok, ints), refs = refs[:2], refs[2:]
-    outs, refs = refs[:kinds], refs[kinds:]
-    (tok_out, ints_out, q_out, kv_out, wo_out), refs = refs[:5], refs[5:]
-    (x_nat, q_src, kv_src), refs = refs[:3], refs[3:]
-    own_sem, zs, zr, xs, xr, ys, yr, cs, cr, ps, pr, tl, ts, tr, il, hs, hr, hps, hpr = refs
+VM = pl.BlockSpec(memory_space=pltpu.VMEM)
+
+
+def head_kernel(scale, *refs):
+    (w_qkv_ref, w_out_ref, w_in_ref, w_back_ref, tok, cot, ints), refs = refs[:7], refs[7:]
+    (b_qkv_ref, b_in_ref, proj_ref), row_vecs, refs = refs[:3], refs[3:9], refs[9:]
+    (a_out, b_out, c_out, tok_out, cot_out, ints_out, q_out, kv_out), refs = refs[:8], refs[8:]
+    (wo_out, vec_all, b_in_all, proj_all, ctx_own, lse_ref, ctx_out), refs = refs[:7], refs[7:]
+    (shard_a, shard_v, vec_out, x_nat, q_src, kv_src, kn, q3, s_scr, o_scr, kcol), refs = refs[:11], refs[11:]
+    own_sem, zs, zr, xs, xr, ys, yr, cs, cr, ps, pr, tl, ts, tr, il, hs, hr, hps, hpr, xl, xs2, xr2, vs, vr = refs
     d, r, c = place()
+    kinds = 4
+    part = w_in_ref.shape[0] // 2
+    mine = pl.ds(pl.multiple_of(d * part, 16), part)
+    feats = tok_out.shape[1]
+    shards = [shard_a.at[mine], shard_v.at[pl.ds(pl.multiple_of(d * 48, 8), 48)], w_in_ref.at[mine], w_back_ref.at[mine]]
+    outs = [a_out, vec_out, b_out, c_out]
     cols = 4
     xn, yn, pn = (d, r ^ 1, c), (d, r ^ 2, c), (1 - d, r, c)
     up, down = (d, r, c + 1), (d, r, c - 1)
     has_up, has_down = c < cols - 1, c > 0
+    columns = w_qkv_ref.shape[1]
+    shard_a[:, :columns] = w_qkv_ref[...]
+    shard_a[:, columns:] = w_out_ref[...]
+    heads = columns // (3 * HD)
+    pieces = []
+    for h in range(heads):
+        spot = slice(h * HD, (h + 1) * HD)
+        pieces += [b_qkv_ref[0:1, spot], jnp.zeros((1, HD), f32), b_qkv_ref[1:2, spot]]
+    bias_lanes = -(-columns // 128) * 128
+    pieces.append(jnp.zeros((1, bias_lanes - columns), f32))
+    line = jnp.concatenate(pieces, axis=1)
+    at = 0
+    for i in range(bias_lanes // 128):
+        shard_v[at : at + 1] = line[:, i * 128 : (i + 1) * 128]
+        at += 1
+    for ref in row_vecs:
+        line = jnp.concatenate([ref[...], jnp.zeros((1, 256 - feats), f32)], axis=1)
+        for i in range(2):
+            shard_v[at : at + 1] = line[:, i * 128 : (i + 1) * 128]
+            at += 1
+    for i in range(b_in_ref.shape[1] // 128):
+        shard_v[at : at + 1] = b_in_ref[:, i * 128 : (i + 1) * 128]
+        at += 1
+    proj_at, proj_rows = 48, feats // 4
+    for i in range(at, proj_at):
+        shard_v[i : i + 1] = jnp.zeros((1, 128), f32)
+    shard_v[proj_at:] = proj_ref[pl.ds(pl.multiple_of(c * proj_rows, 16), proj_rows)].astype(f32)
+
     greet(plane_peers() + [(d, r, c ^ j) for j in (1, 2, 3)])
     moves = take_copies(tok, tok_out, tl, ts, tr)
     for start, _ in moves:
         start()
+    late_moves = take_copies(cot, cot_out, xl, xs2, xr2)
     pltpu.make_async_copy(ints, ints_out.at[d], il.at[0]).start()
     rcopy(ints, ints_out.at[d], il.at[1], il.at[2], pn).start()
-    halves = [shard.shape[0] // 2 for shard in shards]
+    halves = [part // 2, 24, part // 2, part // 2]
 
     def z_send(k, at, way, hop):
         src = shards[k] if hop == 1 else outs[k].at[at, r, d]
@@ -619,25 +657,25 @@
         src = kv_src.at[c] if j == 0 else kv_out.at[c ^ j, d]
         return rcopy(src, kv_out.at[c ^ j, d], hps.at[j], hpr.at[j], pn)
 
-    deep = kv_src.shape[1]
-    out_cols = deep + q_src.shape[1]
-    lanes = -(-out_cols // 128) * 128
+    lanes = bias_lanes
 
     def prepare():
         for _, wait in moves:
             wait()
-        feats = tok_out.shape[1]
         x_nat[...] = tok_out[...].reshape(4 * feats, -1).astype(f32).T.astype(bf16)
 
     def project(j):
         to = c ^ j
-        weights = outs[0][to, :, :, :, :lanes].reshape(-1, lanes)
-        bias = outs[1][to, r, 0, pl.ds(0, 8)]
+        weights = a_out[to, :, :, :, :lanes].reshape(-1, lanes)
+        bias = vec_out[to, r, 0, pl.ds(0, 8)]
         bias = jnp.concatenate([bias[i : i + 1] for i in range(lanes // 128)], axis=1)
         made = jnp.dot(x_nat[...], weights, preferred_element_type=f32) + bias
         made = made.T.astype(bf16)
-        kv_src[to] = made[:deep]
-        q_src[to] = made[deep:out_cols]
+        for h in range(heads):
+            rows = pl.ds(h * HD, HD)
+            q_src[to, rows] = made[3 * h * HD : (3 * h + 1) * HD]
+            kv_src[to, rows] = made[(3 * h + 1) * HD : (3 * h + 2) * HD]
+            kv_src[to, pl.ds(wide + h * HD, HD)] = made[(3 * h + 2) * HD : (3 * h + 3) * HD]
         if j:
             kv(j).start()
             q(j).start()
@@ -647,14 +685,95 @@
             q_out[c] = q_src[c]
 
     def spread_out(at):
-        feats = tok_out.shape[1]
         for row in range(4):
-            block = outs[0][at, row, :, :, out_cols:].reshape(-1, feats)
+            block = a_out[at, row, :, :, columns:].reshape(-1, feats)
             wo_out[pl.ds(at * wide, wide), row * feats : (row + 1) * feats] = block
+
+    def unpack():
+        first = bias_lanes // 128
+        for i in range(6):
+            for row in range(4):
+                line = vec_out[0, row, 0, pl.ds(first + 2 * i, 2)]
+                line = jnp.concatenate([line[0:1], line[1:2]], axis=1)
+                vec_all[i : i + 1, row * feats : (row + 1) * feats] = line[:, :feats]
+        vec_all[6:8] = jnp.zeros((2, 4 * feats), f32)
+        first += 12
+        for at in range(4):
+            for i in range(b_in_all.shape[1] // 128):
+                b_in_all[at : at + 1, i * 128 : (i + 1) * 128] = vec_out[at, 0, 0, pl.ds(first + i, 1)]
+            for row in range(4):
+                rows = pl.ds(row * feats + at * proj_rows, proj_rows)
+                proj_all[rows] = vec_out[at, row, 1].astype(bf16)
+
+    tiles = 8
+    own = x_nat.shape[0]
+
+    def segment(tile):
+        return ints_out[r // 2, r % 2, pl.ds(tile, 1)].astype(f32)
+
+    def collect():
+        for j in (1, 2, 3):
+            kv(j).wait_recv()
+            pair(j).start()
+        pltpu.make_async_copy(ints, ints_out.at[d], il.at[0]).wait()
+        rcopy(ints, ints_out.at[1 - d], il.at[1], il.at[2], pn).wait()
+        for tile in range(tiles):
+            kcol[tile] = jnp.broadcast_to(segment(tile), (128, own)).T
+        for j in (1, 2, 3):
+            q(j).wait_recv()
+        for j in range(4):
+            pair(j).wait_recv()
+
+        @pl.loop(0, 4)
+        def _(at):
+            for core in range(2):
+                kn[2 * at + core] = kv_out[at, core, pl.ds(0, wide)].astype(f32).T.astype(bf16)
+
+    def attend_block(block):
+        block_rows(q_out.at[pl.ds(block, 1)], heads, scale, q3)
+        here = 2 * block + d
+        low, high = jnp.maximum(here - 4, 0), jnp.minimum(here + 5, tiles)
+        qseg = jnp.concatenate([segment(here)] * heads, axis=1)
+
+        def one(j, top):
+            s = jnp.dot(kn[j], q3[...], preferred_element_type=f32)
+            same = jnp.concatenate([kcol[j]] * (heads * own // 128), axis=1) == qseg
+            s = jnp.where(same, s, masked_value)
+            s_scr[j] = s
+            return jnp.maximum(top, jnp.max(s, axis=0, keepdims=True))
+
+        top = lax.fori_loop(low, high, one, jnp.full((1, heads * own), masked_value, f32))
+        o_scr[...] = jnp.zeros_like(o_scr)
+
+        def two(j, total):
+            p = jnp.exp(s_scr[j] - top)
+            low_p = p.astype(bf16)
+            for h in range(heads):
+                rows = pl.ds(h * HD, HD)
+                v = kv_out[j // 2, j % 2, pl.ds(wide + h * HD, HD)]
+                o_scr[rows] += jnp.dot(v, low_p[:, h * own : (h + 1) * own], preferred_element_type=f32)
+            return total + jnp.sum(p, axis=0, keepdims=True)
+
+        total = lax.fori_loop(low, high, two, jnp.zeros((1, heads * own), f32))
+        for h in range(heads):
+            rows = pl.ds(h * HD, HD)
+            ctx_own[block, rows] = (o_scr[rows] / total[:, h * own : (h + 1) * own]).astype(bf16)
+        lse_ref[block] = top + jnp.log(total)
+
+    def back_copy(j):
+        return rcopy(ctx_own.at[c ^ j], ctx_out.at[c], vs.at[j], vr.at[j], (d, r, c ^ j))
+
+    def attend(j):
+        attend_block(c ^ j)
+        if j:
+            back_copy(j).start()
+        else:
+            ctx_out[c] = ctx_own[c]
 
     wide = q_src.shape[1]
     lag = 3
     ready = 2 * len(steps) + 2 * lag
+    rest = len(jobs) - ready - 1
     for i in range(len(jobs) + 2 * lag):
         if i == ready:
             prepare()
@@ -662,18 +781,27 @@
             settle(1)
         if ready <= i < ready + 4:
             project((3, 2, 1, 0)[i - ready])
-        if ready + 4 <= i < ready + 8:
-            spread_out(i - ready - 4)
-        if i < len(jobs):
+        if ready + 3 <= i < ready + 7:
+            spread_out(i - ready - 3)
+        if i == ready + 5:
+            unpack()
+        if i == ready + 7:
+            collect()
+        if ready + 8 <= i < ready + 12:
+            attend((3, 2, 1, 0)[i - ready - 8])
+        if i <= ready:
             first(*jobs[i])
+        elif i <= ready + 4:
+            for n in range(ready + 1 + (i - ready - 1) * 2, min(ready + 1 + (i - ready) * 2, len(jobs))):
+                first(*jobs[n])
+            if i == ready + 4:
+                for start, _ in late_moves:
+                    start()
         if 0 <= i - lag < len(jobs):
             second(*jobs[i - lag])
         if 0 <= i - 2 * lag < len(jobs):
             third(*jobs[i - 2 * lag])
 
-    for j in (1, 2, 3):
-        kv(j).wait_recv()
-        pair(j).start()
     for k in range(kinds):
         if k > 1:
             settle(k)
@@ -708,39 +836,56 @@
 
             guard(way, hop, body)
     for j in (1, 2, 3):
-        q(j).wait()
+        q(j).wait_send()
         kv(j).wait_send()
+        back_copy(j).wait()
     for j in range(4):
-        pair(j).wait()
-    pltpu.make_async_copy(ints, ints_out.at[d], il.at[0]).wait()
-    rcopy(ints, ints_out.at[1 - d], il.at[1], il.at[2], pn).wait()
+        pair(j).wait_send()
+    for _, wait in late_moves:
+        wait()
 
 
 VM = pl.BlockSpec(memory_space=pltpu.VMEM)
 
 
-def gather_fast(shards, tokens, ints, wide, cid):
-    kinds = len(shards)
+def head_fast(weights, tokens, cotangent, ints, vectors, scale, cid):
+    kinds = 4
     dma = pltpu.SemaphoreType.DMA
     _, feats, cols = tokens.shape
     own = cols // 2
-    piece = jax.ShapeDtypeStruct((4, wide, own), bf16)
+    width = 4 * feats
+    part = feats // 2
+    wide = weights[0].shape[1] // 3
+    full = 4 * wide
+    heads = wide // HD
+    shape = jax.ShapeDtypeStruct
+    piece = shape((4, wide, own), bf16)
+    taken = shape((4, feats, own), bf16)
+    weight = shape((4, 4, 2, part, weights[2].shape[1]), bf16)
+    hidden = weights[2].shape[1]
+    student_width = vectors[2].shape[1]
     return pl.pallas_call(
-        functools.partial(gather_kernel, kinds),
-        out_shape=[jax.ShapeDtypeStruct((4, 4, 2) + s.shape, s.dtype) for s in shards]
-        + [
-            jax.ShapeDtypeStruct((4, feats, own), tokens.dtype),
-            jax.ShapeDtypeStruct((2,) + ints.shape, ints.dtype),
-            piece,
-            jax.ShapeDtypeStruct((4, 2, 2 * wide, own), bf16),
-            jax.ShapeDtypeStruct((4 * wide, 4 * feats), bf16),
+        functools.partial(head_kernel, scale),
+        out_shape=[
+            shape((4, 4, 2, part, full), bf16), weight, weight, taken, taken, shape((2,) + ints.shape, ints.dtype),
+            piece, shape((4, 2, 2 * wide, own), bf16), shape((4 * wide, width), bf16), shape((8, width), f32),
+            shape((4, hidden), f32), shape((width, student_width), bf16), piece,
+            shape((4, 1, heads * own), f32), piece,
         ],
-        in_specs=[HBM] * (kinds + 2),
-        out_specs=[VM, VM] + [HBM] * (kinds - 2) + [VM, HBM, VM, VM, VM],
+        in_specs=[VM, VM] + [HBM] * 5 + [VM] * len(vectors),
+        out_specs=[VM, HBM, HBM] + [VM] * 12,
         scratch_shapes=[
-            pltpu.VMEM((own, 4 * feats), bf16),
+            pltpu.VMEM((feats, full), bf16),
+            pltpu.VMEM((96, 128), f32),
+            pltpu.VMEM((4, 4, 2, 48, 128), f32),
+            pltpu.VMEM((own, width), bf16),
             pltpu.VMEM((4, wide, own), bf16),
             pltpu.VMEM((4, 2 * wide, own), bf16),
+            pltpu.VMEM((8, own, wide), bf16),
+            pltpu.VMEM((wide, heads * own), bf16),
+            pltpu.VMEM((8, own, heads * own), f32),
+            pltpu.VMEM((wide, own), f32),
+            pltpu.VMEM((8, own, 128), f32),
             dma((kinds,)),
             dma((kinds, 2, 3)), dma((kinds, 2, 3)),
             dma((kinds, 4)), dma((kinds, 4)),
@@ -749,12 +894,13 @@
             dma((kinds, 4, 4)), dma((kinds, 4, 4)),
             dma, dma((4,)), dma((4,)), dma((3,)),
             dma((2, 4)), dma((2, 4)), dma((4,)), dma((4,)),
+            dma, dma((4,)), dma((4,)), dma((4,)), dma((4,)),
         ],
         compiler_params=pltpu.CompilerParams(
-            collective_id=cid, has_side_effects=True, vmem_limit_bytes=40 * 1024 * 1024
+            collective_id=cid, has_side_effects=True, vmem_limit_bytes=56 * 1024 * 1024
         ),
         name="head",
-    )(*shards, tokens, ints)
+    )(*weights, tokens, cotangent, ints, *vectors)
 
 
 def scatter_core(grads, outs, scratch, begin, during, late=0, gap=0):
@@ -999,42 +1145,6 @@
 def line_peers():
     d, r, c = place()
     return [(d ^ (j // 4), r, c ^ (j % 4)) for j in range(1, 8)]
-
-
-def swap_kernel(src, cot, out, cot_out, send, recv, tl, ts, tr):
-    d, r, c = place()
-    greet(plane_peers() + [(d, r, c ^ j) for j in (1, 2, 3)])
-
-    def move(j):
-        return rcopy(src.at[c ^ j], out.at[c], send.at[j], recv.at[j], (d, r, c ^ j))
-
-    for j in (3, 2, 1):
-        move(j).start()
-    moves = take_copies(cot, cot_out, tl, ts, tr)
-    for start, _ in moves:
-        start()
-    out[c] = src[c]
-    for j in (1, 2, 3):
-        move(j).wait()
-    for _, wait in moves:
-        wait()
-
-
-def swap_fast(values, cotangent, cid):
-    dma = pltpu.SemaphoreType.DMA
-    _, feats, cols = cotangent.shape
-    return pl.pallas_call(
-        swap_kernel,
-        out_shape=[
-            jax.ShapeDtypeStruct(values.shape, values.dtype),
-            jax.ShapeDtypeStruct((4, feats, cols // 2), cotangent.dtype),
-        ],
-        in_specs=[VM, HBM],
-        out_specs=[VM, VM],
-        scratch_shapes=[dma((4,)), dma((4,)), dma, dma((4,)), dma((4,))],
-        compiler_params=pltpu.CompilerParams(collective_id=cid, has_side_effects=True),
-        name="swap",
-    )(values, cotangent)
 
 
 def sum_steps(src, total, parts, sems):
@@ -1190,14 +1300,14 @@
 def tail_kernel(docs, classes, scale, *refs):
     kinds = 2
     grads, refs = refs[:kinds], refs[kinds:]
-    (q_ref, kv_ref, lse_ref, ctx_ref, dctx_ref, qseg_ref, kseg_ref), refs = refs[:7], refs[7:]
+    (q_ref, kv_ref, lse_ref, ctx_ref, dctx_ref, ints_ref), refs = refs[:6], refs[6:]
     (out_ref, seg_ref, label_ref, proj_ref, svec_ref, mid_ref, cls_ref), refs = refs[:7], refs[7:]
     vec_refs, refs = refs[:7], refs[7:]
     (x_ref, ctx_all_ref, resid_ref, out_t_ref, w_ref), refs = refs[:5], refs[5:]
     outs, refs = refs[: kinds + 1], refs[kinds + 1 :]
     (give_out, out_out, small_out), refs = refs[:3], refs[3:]
     (total, theirs, dqkv, own_grads, dpad, weights, resid_t, give_src), refs = refs[:8], refs[8:]
-    (dctx, dq, dkv, kn, vn, q3, dc3, dq_scr, dkv_scr, bias_scr), refs = refs[:10], refs[10:]
+    (dctx, dq, dkv, kn, vn, q3, dc3, dq_scr, dkv_scr, bias_scr, landed, kcol), refs = refs[:12], refs[12:]
     (hidden, logit, stats, stats_all, small), refs = refs[:5], refs[5:]
     parts, refs = refs[:10], refs[10:]
     (send, recv, psend, precv), sems, (wl, gl, gs, gr), refs = refs[:4], refs[4:8], refs[8:12], refs[12:]
@@ -1263,6 +1373,9 @@
             stats_all, small,
         )
 
+    def segment(at):
+        return ints_ref[r // 2, r % 2, pl.ds(at, 1)].astype(f32)
+
     def prepare(_):
         @pl.loop(0, tiles)
         def _(j):
@@ -1270,6 +1383,8 @@
             vn[j] = kv_ref[j, pl.ds(wide, wide)].astype(f32).T.astype(bf16)
             dkv_scr[j] = jnp.zeros((deep, tile), f32)
 
+        for j in range(tiles):
+            kcol[j] = jnp.broadcast_to(segment(j), (128, own)).T
         bias_scr[...] = jnp.zeros_like(bias_scr)
         for j in (1, 2, 3):
             to_heads(j).wait_recv()
@@ -1281,7 +1396,7 @@
         q_at, dc_at = q_ref.at[pl.ds(block, 1)], dctx.at[pl.ds(block, 1)]
         block_rows(q_at, heads, scale, q3)
         block_rows(dc_at, heads, 1.0, dc3)
-        qseg = jnp.concatenate([qseg_ref[block]] * heads, axis=1)
+        qseg = jnp.concatenate([segment(2 * block + d)] * heads, axis=1)
         lse = lse_ref[block]
         product = ctx_ref[block].astype(f32) * dctx[block].astype(f32)
         delta = jnp.concatenate(
@@ -1293,8 +1408,8 @@
         @pl.loop(jnp.maximum(here - 4, 0), jnp.minimum(here + 5, tiles))
         def _(j):
             s = jnp.dot(kn[j], q3[...], preferred_element_type=f32)
-            s = jnp.where(kseg_ref[j] == qseg, s, masked_value)
-            p = jnp.exp(s - lse)
+            same = jnp.concatenate([kcol[j]] * (heads * own // 128), axis=1) == qseg
+            p = jnp.exp(jnp.where(same, s, masked_value) - lse)
             d_p = jnp.dot(vn[j], dc3[...], preferred_element_type=f32)
             d_s = (p * (d_p - delta)).astype(bf16)
             p = p.astype(bf16)
@@ -1313,10 +1428,10 @@
         return rcopy(dkv.at[c ^ j, 1 - d], theirs.at[c ^ j], psend.at[j], precv.at[j], pn)
 
     def kv(j):
-        return rcopy(total.at[c ^ j], dqkv.at[c, kv_rows], send.at[0, j], recv.at[0, j], (d, r, c ^ j))
+        return rcopy(total.at[c ^ j], landed.at[c, kv_rows], send.at[0, j], recv.at[0, j], (d, r, c ^ j))
 
     def q(j):
-        return rcopy(dq.at[c ^ j], dqkv.at[c, q_rows], send.at[1, j], recv.at[1, j], (d, r, c ^ j))
+        return rcopy(dq.at[c ^ j], landed.at[c, q_rows], send.at[1, j], recv.at[1, j], (d, r, c ^ j))
 
     def leave(_):
         for j in (3, 2, 1, 0):
@@ -1326,13 +1441,13 @@
             pair(j).start()
             if j:
                 q(j).start()
-        dqkv[c, q_rows] = dq[c]
+        landed[c, q_rows] = dq[c]
         for j in (3, 2, 1):
             pair(j).wait_recv()
             total[c ^ j] = dkv[c ^ j, d] + theirs[c ^ j]
             kv(j).start()
         pair(0).wait_recv()
-        dqkv[c, kv_rows] = dkv[c, d] + theirs[c]
+        landed[c, kv_rows] = dkv[c, d] + theirs[c]
 
         @pl.loop(0, 4)
         def _(at):
@@ -1359,6 +1474,13 @@
             for far in (1, 2, 3):
                 q(far).wait_recv()
                 kv(far).wait_recv()
+
+            @pl.loop(0, 4)
+            def _(at):
+                for h in range(heads):
+                    for slot, spot in enumerate((deep, 0, wide)):
+                        dqkv[at, pl.ds((3 * h + slot) * HD, HD)] = landed[at, pl.ds(spot + h * HD, HD)]
+
         make((0, 3, 1, 2)[j])
         launch(kinds * 4 + j)
 
@@ -1444,6 +1566,8 @@
             pltpu.VMEM((wide, own), f32),
             pltpu.VMEM((tiles, deep, own), f32),
             pltpu.VMEM((8, deep), f32),
+            pltpu.VMEM((cols, deep + wide, own), bf16),
+            pltpu.VMEM((tiles, own, 128), f32),
             pltpu.VMEM((own, student_width), f32),
             pltpu.VMEM((own, student_width), f32),
             pltpu.VMEM((24, student_width), f32),
@@ -1462,6 +1586,69 @@
     )(*grads, *attention, *student, *vectors, *rest, out_t.reshape(4, feats, own), w_attn)
 
 
+def finish_kernel(docs, classes, in_ref, back_ref, attn_ref, grad_ref, small_ref, *outs):
+    d, r, c = place()
+    w_qkv, w_out, w_in, w_back, tokens, proj, logits, b_qkv, b_in, singles = outs[:9] + (outs[9:],)
+    rows = in_ref.shape[0] * in_ref.shape[1]
+    w_in[...] = in_ref[...].reshape(rows, -1).astype(f32)
+    w_back[...] = back_ref[...].reshape(rows, -1).astype(f32)
+    columns = w_qkv.shape[1]
+    w_qkv[...] = attn_ref[:, :, :columns].reshape(rows, -1).astype(f32)
+    w_out[...] = attn_ref[:, :, columns:].reshape(rows, -1).astype(f32)
+    tokens[...] = grad_ref[...].astype(f32)
+    feats = proj.shape[0]
+    proj[...] = small_ref[pl.ds(pl.multiple_of(r * feats, 8), feats)]
+    for i in range(2):
+        some = small_ref[pl.ds(pl.multiple_of(920 + 8 * (2 * d + i), 8), 8)]
+        logits[i] = some[:docs, :classes]
+    line = [small_ref[pl.ds(1012 + 3 * c + i, 1)] for i in range(3)]
+    line = jnp.concatenate(line, axis=1)
+    wide = b_qkv.shape[1]
+    b_qkv[0:1] = line[:, :wide]
+    b_qkv[1:2] = line[:, wide:]
+    for i in range(b_in.shape[1] // 128):
+        b_in[:, i * 128 : (i + 1) * 128] = small_ref[pl.ds(952 + 6 * c + i, 1)]
+    for i in range(6):
+        line = [small_ref[976 + 6 * i + j : 977 + 6 * i + j] for j in range(6)]
+        line = jnp.concatenate(line, axis=1)
+        for row in range(4):
+
+            @pl.when(r == row)
+            def _():
+                singles[i][...] = line[:, row * feats : (row + 1) * feats]
+
+    s_mid, s_cls, s_mid_bias, s_cls_bias, s_bias, s_query = singles[6:]
+    s_mid[...] = small_ref[768:896]
+    s_cls[...] = jnp.concatenate([small_ref[896:912]] + [jnp.zeros((112, 128), f32)], axis=0).T[:, :classes]
+    s_mid_bias[...] = small_ref[912:913]
+    s_cls_bias[...] = small_ref[913:914, :classes]
+    s_bias[...] = small_ref[914:915]
+    s_query[...] = small_ref[915:916]
+
+
+def finish_fast(docs, classes, w_in, w_back, w_attn, grad, small, columns):
+    _, part, hidden = w_in.shape
+    feats = 2 * part
+    width = small.shape[1]
+
+    def shape(*dims):
+        return jax.ShapeDtypeStruct(dims, f32)
+
+    shapes = [
+        shape(feats, columns), shape(w_attn.shape[2] - columns, feats), shape(feats, hidden), shape(feats, hidden),
+        shape(*grad.shape), shape(feats, width), shape(2, docs, classes), shape(2, columns // 3), shape(1, hidden),
+    ]
+    shapes += [shape(1, feats)] * 6
+    shapes += [shape(width, width), shape(width, classes), shape(1, width), shape(1, classes)] + [shape(1, width)] * 2
+    return pl.pallas_call(
+        functools.partial(finish_kernel, docs, classes),
+        out_shape=shapes,
+        in_specs=[VM] * 5,
+        out_specs=[VM] * len(shapes),
+        name="finish",
+    )(w_in, w_back, w_attn, grad, small)
+
+
 def dot(a, b, contract=((1,), (0,))):
     return lax.dot_general(a, b, (contract, ((), ())), preferred_element_type=f32)
 
@@ -1475,84 +1662,6 @@
                 out[spot] = ref[0, pl.ds(h * HD, HD)] * jnp.asarray(scale, out.dtype)
             else:
                 out[spot] = jnp.zeros((HD, own), out.dtype)
-
-
-def attn_fwd_kernel(heads, scale, bounds, q_ref, kv_ref, qseg_ref, kseg_ref, ctx_ref, lse_ref, kn, q3, s_scr, o_scr):
-    step = pl.program_id(0)
-    tiles, _, tile = kv_ref.shape
-    wide = heads * HD
-    own = q_ref.shape[-1]
-
-    @pl.when(step == 0)
-    def _():
-        @pl.loop(0, tiles)
-        def _(j):
-            kn[j] = kv_ref[j, pl.ds(0, wide)].astype(f32).T.astype(bf16)
-
-    block_rows(q_ref, heads, scale, q3)
-    low, high = bounds[step, 0], bounds[step, 1]
-    qseg = jnp.concatenate([qseg_ref[0]] * heads, axis=1)
-
-    def one(j, top):
-        s = dot(kn[j], q3[...])
-        s = jnp.where(kseg_ref[j] == qseg, s, masked_value)
-        s_scr[j] = s
-        return jnp.maximum(top, jnp.max(s, axis=0, keepdims=True))
-
-    top = lax.fori_loop(low, high, one, jnp.full((1, heads * own), masked_value, f32))
-    o_scr[...] = jnp.zeros_like(o_scr)
-
-    def two(j, total):
-        p = jnp.exp(s_scr[j] - top)
-        low_p = p.astype(bf16)
-        for h in range(heads):
-            rows = pl.ds(h * HD, HD)
-            v = kv_ref[j, pl.ds(wide + h * HD, HD)]
-            o_scr[rows] += dot(v, low_p[:, h * own : (h + 1) * own])
-        return total + jnp.sum(p, axis=0, keepdims=True)
-
-    total = lax.fori_loop(low, high, two, jnp.zeros((1, heads * own), f32))
-    for h in range(heads):
-        rows = pl.ds(h * HD, HD)
-        ctx_ref[0, rows] = (o_scr[rows] / total[:, h * own : (h + 1) * own]).astype(bf16)
-    lse_ref[0] = top + jnp.log(total)
-
-
-def attn_fwd(bounds, q, kv, qseg, kseg, scale):
-    blocks, wide, own = q.shape
-    tiles, _, tile = kv.shape
-    heads = wide // HD
-    return pl.pallas_call(
-        functools.partial(attn_fwd_kernel, heads, scale),
-        out_shape=[
-            jax.ShapeDtypeStruct(q.shape, bf16),
-            jax.ShapeDtypeStruct((blocks, 1, heads * own), f32),
-        ],
-        grid_spec=pltpu.PrefetchScalarGridSpec(
-            num_scalar_prefetch=1,
-            grid=(blocks,),
-            in_specs=[
-                pl.BlockSpec((1, wide, own), lambda i, b: (i, 0, 0)),
-                pl.BlockSpec(kv.shape, lambda i, b: (0, 0, 0)),
-                pl.BlockSpec((1, 1, own), lambda i, b: (i, 0, 0)),
-                pl.BlockSpec(kseg.shape, lambda i, b: (0, 0, 0)),
-            ],
-            out_specs=[
-                pl.BlockSpec((1, wide, own), lambda i, b: (i, 0, 0)),
-                pl.BlockSpec((1, 1, heads * own), lambda i, b: (i, 0, 0)),
-            ],
-            scratch_shapes=[
-                pltpu.VMEM((tiles, tile, wide), bf16),
-                pltpu.VMEM((wide, heads * own), bf16),
-                pltpu.VMEM((tiles, tile, heads * own), f32),
-                pltpu.VMEM((wide, own), f32),
-            ],
-        ),
-        compiler_params=pltpu.CompilerParams(
-            dimension_semantics=("arbitrary",), vmem_limit_bytes=48 * 1024 * 1024
-        ),
-        name="attn_fwd",
-    )(bounds, q, kv, qseg, kseg)
 
 
 def fast_local(
@@ -1600,50 +1709,30 @@
     doc_ids = jnp.arange(docs_count, dtype=jnp.int32)
     class_ids = jnp.arange(class_count, dtype=jnp.int32)
 
-    w_three = w_qkv.reshape(width_row, heads_dev, 3, HD).transpose(0, 2, 1, 3)
-    w_three = jnp.concatenate([w_three[:, 1], w_three[:, 2], w_three[:, 0]], axis=1)
-    shard_attn = own_half(jnp.concatenate([w_three.reshape(width_row, -1), w_out], axis=1))
-    proj_rows = width_row // cols
-    lanes = -(-3 * width_col // 128) * 128
-    offsets = jnp.concatenate([jnp.zeros_like(b_qkv[0]), b_qkv[1], b_qkv[0]])
-    offsets = jnp.pad(offsets, (0, lanes - 3 * width_col))
-    vectors = [offsets, b_out, ln1_gain, ln1_bias, b_back, ln2_gain, ln2_bias, b_in]
-    vectors.append(lax.dynamic_slice_in_dim(s_proj, col_index * proj_rows, proj_rows).astype(f32).reshape(-1))
-    flat = jnp.concatenate(vectors)
-    flat = jnp.pad(flat, (0, 96 * 128 - flat.shape[0])).reshape(96, 128)
-    w_attn, vec, w_in_all, w_back_all, x_parts, ints, queries, kv, w_out_all = gather_fast(
-        [shard_attn, own_half(flat), own_half(w_in), own_half(w_back)],
+    ints = jnp.pad(labels, ((0, 0), (0, own - docs_count)))[:, None]
+    ints = jnp.concatenate([segments.reshape(-1, seq_len // own, own), ints], axis=1)
+    ints = jnp.pad(ints, ((0, 0), (0, 16 - ints.shape[1]), (0, 0)))
+    row_vectors = [b_out, ln1_gain, ln1_bias, b_back, ln2_gain, ln2_bias]
+    (
+        w_attn, w_in_all, w_back_all, x_parts, c_parts, ints, queries, kv, w_out_all, row_vectors, b_in_all,
+        s_proj_all, context, lse, ctx_parts,
+    ) = head_fast(
+        [w_qkv, w_out, w_in, w_back],
         tokens,
-        jnp.concatenate([segments, labels], axis=1),
-        width_col,
+        cotangent,
+        ints,
+        [b_qkv, b_in[None], s_proj] + [v[None] for v in row_vectors],
+        score_scale,
         1,
     )
     w_in_all = w_in_all.reshape(cols, width, hidden_col)
     w_back_all = w_back_all.reshape(cols, width, hidden_col)
-    vec = vec.reshape(cols, rows, -1)
-    at = lanes + 6 * width_row
-    row_vectors = vec[0, :, lanes:at].reshape(rows, 6, width_row).transpose(1, 0, 2).reshape(6, width)
     b_out_a, gain_one, bias_one, b_back_a, gain_two, bias_two = [row_vectors[i] for i in range(6)]
-    b_in_all = vec[:, 0, at : at + hidden_col]
-    at += hidden_col
-    s_proj_all = vec[:, :, at : at + proj_rows * student_width].astype(bf16)
-    s_proj_all = s_proj_all.reshape(cols, rows, proj_rows, student_width).transpose(1, 0, 2, 3)
-    s_proj_all = s_proj_all.reshape(width, student_width)
-    x_t = x_parts.reshape(width, own)
-    ints = lax.dynamic_index_in_dim(ints.reshape(seqs, -1), row_index, 0, False)
-    seg_all, label_seq = ints[:seq_len], ints[seq_len:]
-    seg_blocks = seg_all.reshape(cols, parts, own)
-    seg_q = lax.dynamic_index_in_dim(seg_blocks, dp_index, 1, False)
-    seg_own = lax.dynamic_index_in_dim(seg_q, col_index, 0, False)
-    lows = jnp.sum(seg_all[None, :] < seg_q[:, :1], axis=1) // own
-    highs = (jnp.sum(seg_all[None, :] <= seg_q[:, -1:], axis=1) + own - 1) // own
-    bounds = jnp.stack([lows, highs], axis=1).astype(jnp.int32)
-
+    x_t, ctx_t = x_parts.reshape(width, own), ctx_parts.reshape(width, own)
     kv = kv.reshape(cols * parts, 2 * width_col, own)
-    q_rows, k_rows = seg_q[:, None, :], seg_all.reshape(cols * parts, own, 1)
-    context, lse = attn_fwd(bounds, queries, kv, q_rows, k_rows, score_scale)
-    ctx_t, c_parts = swap_fast(context, cotangent, 3)
-    ctx_parts, ctx_t = ctx_t, ctx_t.reshape(width, own)
+    own_ints = lax.dynamic_index_in_dim(ints.reshape(seqs, 16, own), row_index, 0, False)
+    seg_own = lax.dynamic_index_in_dim(own_ints, 2 * col_index + dp_index, 0, False)
+    label_seq = own_ints[seq_len // own, :docs_count]
 
     x = x_t.T
     attn_out = mm(ctx_t, w_out_all, ((0,), (0,))) + b_out_a
@@ -1687,7 +1776,7 @@
         class_count,
         score_scale,
         [g_in.astype(bf16).reshape(blocked), g_back.astype(bf16).reshape(blocked)],
-        [queries, kv, lse, context, d_ctx.reshape(cols, width_col, own), q_rows, k_rows],
+        [queries, kv, lse, context, d_ctx.reshape(cols, width_col, own), ints],
         [
             layer_out,
             seg_own[:, None],
@@ -1704,47 +1793,33 @@
         w_attn,
         4,
     )
-    g_in, g_back, g_attn = [part.reshape(width_row, -1).astype(f32) for part in (g_in, g_back, g_attn)]
-    g_qkv = g_attn[:, : 3 * width_col].reshape(width_row, 3, heads_dev, HD)
-    g_qkv = jnp.stack([g_qkv[:, 2], g_qkv[:, 0], g_qkv[:, 1]], axis=2).reshape(width_row, -1)
-
-    def at_col(part):
-        return lax.dynamic_index_in_dim(part, col_index, 0, False)
-
-    def at_row(part):
-        return lax.dynamic_slice_in_dim(part, row_index * width_row, width_row)
-
-    g_sproj, g_mid, g_cls = small[:width], small[width : width + 128], small[width + 128 : width + 144].T
-    g_mid_bias, g_cls_bias, g_sbias, g_query = [small[width + 144 + i] for i in range(4)]
-    logits = small[width + 152 : width + 184].reshape(seqs, 8, 128)[:, :docs_count, :class_count]
-    g_in_bias = small[width + 184 : width + 208].reshape(cols, hidden_col)
-    vector_sums = small[width + 208 : width + 244].reshape(6, width)
-    g_out_bias, g_ln1_gain, g_ln1_bias, g_back_bias, g_ln2_gain, g_ln2_bias = [vector_sums[i] for i in range(6)]
-    g_qkv_bias = small[width + 244 :].reshape(cols, 2, width_col)
-    logits = lax.dynamic_slice_in_dim(logits, dp_index * (seqs // parts), seqs // parts)
+    (
+        g_qkv, g_out, g_in, g_back, grad_tokens, g_sproj, logits, g_qkv_bias, g_in_bias, g_out_bias, g_ln1_gain,
+        g_ln1_bias, g_back_bias, g_ln2_gain, g_ln2_bias, g_mid, g_cls, g_mid_bias, g_cls_bias, g_sbias, g_query,
+    ) = finish_fast(docs_count, class_count, g_in, g_back, g_attn, grad_tokens, small, 3 * width_col)
     return (
         out,
         logits,
-        grad_tokens.astype(f32),
+        grad_tokens,
         g_qkv,
-        at_col(g_qkv_bias),
-        g_attn[:, 3 * width_col :],
-        at_row(g_out_bias),
-        at_row(g_ln1_gain),
-        at_row(g_ln1_bias),
+        g_qkv_bias,
+        g_out,
+        g_out_bias[0],
+        g_ln1_gain[0],
+        g_ln1_bias[0],
         g_in,
-        at_col(g_in_bias),
+        g_in_bias[0],
         g_back,
-        at_row(g_back_bias),
-        at_row(g_ln2_gain),
-        at_row(g_ln2_bias),
-        at_row(g_sproj),
-        g_sbias,
-        g_query,
+        g_back_bias[0],
+        g_ln2_gain[0],
+        g_ln2_bias[0],
+        g_sproj,
+        g_sbias[0],
+        g_query[0],
         g_mid,
-        g_mid_bias,
-        g_cls[:, :class_count],
-        g_cls_bias[:class_count],
+        g_mid_bias[0],
+        g_cls,
+        g_cls_bias[0],
     )
 
 

time: 354 us -> 314 us (0.89)
  local copies, waits for them, and re-layouts: 52.1 us -> 21.1 us
  other arithmetic: 14.7 us -> 8.3 us
    slice x15 -> x0, local copies, waits for them, and re-layouts: 11.5 us -> none  [the longest x3 2.09 us: fast_local(): seg_all, label_seq = (ints[:seq_len], ints[seq_len:])]
    dynamic_slice x13 -> x0, local copies, waits for them, and re-layouts: 7.35 us -> none  [the longest x7 4.46 us: at_row(): return lax.dynamic_slice_in_dim(part, row_index * width_row, width_row)]
    unnamed x70 -> x55, local copies, waits for them, and re-layouts: 12.9 us -> 6.47 us
    reshape x11 -> x0, local copies, waits for them, and re-layouts: 3.94 us -> none  [the longest x1 1.22 us: fast_local(): vec = vec.reshape(cols, rows, -1)]
    convert_element_type x4 -> x0, other arithmetic: 3.72 us -> none  [the longest x3 2.75 us: fast_local(): part.reshape(width_row, -1).astype(f32)]
    pallas_call x3 -> x2, Pallas kernels: 116 us -> 116 us  [the longest x1 113 us: head_fast(): pl.pallas_call(functools.partial(head_kernel, scale), out_shape=[shape((4...]
where the time goes in v2:
time: 314 us
  Pallas kernels  253 us (81%)
  matrix products  30 us (10%)
  local copies, waits for them, and re-layouts  21.1 us (7%)
  other arithmetic  8.3 us (3%)
    pallas_call x1, Pallas kernels, tail_fast(): pl.pallas_call(functools.partial(tail_kernel, docs, classes, scale), out_...  137 us
    pallas_call x1, Pallas kernels, head_fast(): pl.pallas_call(functools.partial(head_kernel, scale), out_shape=[shape((4...  113 us
    dot_general x1, matrix products, fast_local(): jnp.einsum('td,cdn->ctn', hidden_low, w_in_all, preferred_element_type=f32)  10.1 us
    unnamed x55, local copies, waits for them, and re-layouts  6.47 us

profile of v2, /device:TPU:0, one launch (start us, length us, event | category | flops | bytes accessed | tf_op | source)
XLA Modules:
  0.0 313.7 jit_solution(16736585344480445392)
XLA Ops:
  0.7 0.7 copy.71
  1.4 0.7 pad.24
  2.1 0.6 pad.25.refs_6_
  2.7 1.3 broadcast_in_dim.58.refs_8_
  4.0 113.1 %head.1 = (bf16[4,4,2,96,768]{4,3,2,1,0:T(8,128)(2,1)}, bf16[4,4,2,96,768]{4,3,2,1,0:T(8,128)(2,1)}, bf16[4,4,2,96,768]{4,3,2,1,0:T(8,128)(2,1)}, bf16[4,192,256...) custom-call(bf16[192,576]{1,0:T(8,128)(2,1)} %refs_0_.1, ...), custom_call_target="tpu_custom_call" | custom-call | tf_op jit(solution)/shard_map/head/pallas_call | solution.py:867
  117.1 1.6 slice_reduce_fusion
  118.7 1.0 bitcast_convert_fusion
  119.7 0.3 copy.54
  120.0 0.0 slice-start.2
  120.0 1.7 fusion.49
  121.8 0.0 copy-start.5
  121.8 0.2 multiply_reduce_fusion.4
  122.0 0.0 copy-start.8
  122.0 0.4 copy-done.16
  122.5 10.1 %fusion.9 = (bf16[4,256,768]{2,1,0:T(8,128)(2,1)S(1)}, f32[4,256,768]{2,1,0:T(8,128)}, f32[4,768,256]{1,2,0:T(8,128)}) fusion(f32[4,768]{1,0:T(4,128)S(1)} %copy-done.17, bf16[4,768,768]{2,1,0:T(8,128)(2,1)S(1)} %bitcast.224, f32[256,768]{1,0:T(8,128)S(1)} %get-tuple-element.172, f32[768]{0:T(1024)S(1)} %get-tuple-element.160, ...), kind=kOutput, calls=%fused_computation.17 | convolution fusion | flops 1260847104 | bytes 13389824 | tf_op jit(solution)/shard_map/td,cdn->ctn/dot_general | solution.py:1742
  132.6 0.0 slice-done.2
  132.6 1.5 fusion.46
  134.2 0.0 copy-start.7
  134.2 0.2 multiply_reduce_fusion.3
  134.4 0.0 copy-start.10
  134.4 0.0 copy-done.5
  134.4 0.0 copy-done.8
  134.4 0.3 copy-done.7
  134.7 0.2 copy-done.10
  135.0 1.2 fusion.28
  136.2 1.9 copy.60
  138.1 1.2 copy.55
  139.3 2.0 fusion.33
  141.3 1.1 convert_reduce_fusion.1
  142.5 0.0 copy-start.6
  142.5 0.0 copy-start.9
  142.5 0.0 slice-start.1
  142.5 6.2 %convert_reduce_fusion = (f32[4,768]{1,0:T(4,128)}, bf16[4,256,768]{2,1,0:T(8,128)(2,1)S(1)}) fusion(f32[4,256,768]{2,1,0:T(8,128)S(1)} %copy-done.20, bf16[4,768,768]{2,1,0:T(8,128)(2,1)} %bitcast.228, f32[256,768]{1,0:T(8,128)S(1)} %get-tuple-element.164, f32[4,768,256]{1,2,0:T(8,128)} %get-tuple-element.175, f32[4,768]{1,0:T(4,128)S(1)} %copy-done.18), kind=kOutput, calls=%fused_computation.18 | convolution fusion | flops 1221522432 | bytes 13393920 | tf_op jit(solution)/shard_map/td,cdn->ctn/dot_general | solution.py:1756
  148.7 0.0 copy-done.6
  148.7 0.0 slice-done.1
  148.8 1.7 multiply_reduce_fusion
  150.5 0.3 convert_reduce_fusion.2
  150.8 0.0 copy-start
  150.8 1.3 convolution_convert_fusion.2
  152.0 0.6 broadcast_in_dim.67.refs_16_
  152.6 0.6 broadcast_in_dim.68.refs_17_
  153.2 0.6 broadcast_in_dim.69.refs_18_
  153.8 3.7 %convolution_convert_fusion = bf16[4,768,768]{1,2,0:T(8,128)(2,1)} fusion(bf16[4,256,768]{2,1,0:T(8,128)(2,1)S(1)} %copy-done.3, f32[256,768]{1,0:T(8,128)S(1)} %get-tuple-element.164), kind=kOutput, calls=%fused_computation.32 | convolution fusion | flops 1210515456 | bytes 7077888 | tf_op jit(solution)/shard_map/td,ctn->cdn/dot_general | solution.py:1755
  157.5 0.0 copy-start.13
  157.5 0.0 copy-start.14
  157.5 0.0 copy-start.15
  157.5 3.8 %convolution_convert_fusion.1 = bf16[4,768,768]{1,2,0:T(8,128)(2,1)} fusion(bf16[4,256,768]{2,1,0:T(8,128)(2,1)S(1)} %get-tuple-element.179, f32[256,768]{1,0:T(8,128)S(1)} %get-tuple-element.172, f32[768]{0:T(1024)S(1)} %get-tuple-element.160, f32[768]{0:T(1024)S(1)} %get-tuple-element.161, f32[256]{0:T(256)S(1)} %copy-done.9, f32[256]{0:T(256)S(1)} %copy-done.6), kind=kOutput, calls=%fused_computation.33 | convolution fusion | flops 1211301888 | bytes 7086080 | tf_op jit(solution)/shard_map/td,ctn->cdn/dot_general | solution.py:1760
  161.3 0.6 broadcast_in_dim.70.refs_19_
  161.9 0.6 broadcast_in_dim.71.refs_20_
  162.5 0.7 dynamic-slice_bitcast_fusion.1
  163.2 0.8 copy.61.refs_9_
  164.0 0.7 dynamic-slice_bitcast_fusion
  164.7 0.7 copy.62.refs_10_
  165.4 0.2 convert_reduce_fusion.3
  165.6 0.7 broadcast_in_dim.72.refs_21_
  166.3 0.1 copy.58
  166.4 0.6 pad.29.refs_14_
  167.1 0.6 select_maximum_fusion.refs_12_
  167.7 136.7 %tail.1 = (bf16[2,96,768]{2,1,0:T(8,128)(2,1)}, bf16[2,96,768]{2,1,0:T(8,128)(2,1)}, bf16[2,96,768]{2,1,0:T(8,128)(2,1)}, bf16[2,192,512]{2,1,0:T(8,128)(2,1)}, ...) custom-call(bf16[4,4,2,96,768]{4,3,2,1,0:T(8,128)(2,1)} %bitcast.205, bf16[4,4,2,96,768]{4,3,2,1,0:T(8,128)(2,1)} %bitcast.204, ...), custom_call_target="tpu_custom_call" | custom-call | tf_op jit(solution)/shard_map/tail/pallas_call | solution.py:1545
  304.4 3.4 %finish.1 = (f32[192,576]{1,0:T(8,128)}, f32[192,192]{1,0:T(8,128)}, f32[192,768]{1,0:T(8,128)}, f32[192,768]{1,0:T(8,128)}, f32[2,192,512]{2,1,0:T(8,128)}, /*i...) custom-call(bf16[2,96,768]{2,1,0:T(8,128)(2,1)} %get-tuple-element.8, ...), custom_call_target="tpu_custom_call" | custom-call | tf_op jit(solution)/shard_map/finish/pallas_call | solution.py:1643
  307.8 1.5 copy.64
  309.3 1.3 copy.63
  310.6 1.3 reduce.8
  311.9 1.8 copy.73
  (44 shorter events, 0.1 us)
Async XLA Ops:
  117.0 3.0 copy-start.1
  119.7 2.3 copy-start.17
  120.0 2.5 copy-start.16
  120.0 12.6 %slice-start.2 = ((s8[4718592]{0:T(1024)(128)(4,1)}), s8[4194304]{0:T(1024)(128)(4,1)S(1)}, s32[]{:S(2)}) async-start(s8[4718592]{0:T(1024)(128)(4,1)} %bitcast.229), calls=%async_computation.2 | async-start | bytes 8388608
  121.8 12.7 %copy-start.5 = (f32[256]{0:T(256)}, f32[256]{0:T(256)S(1)}, u32[]{:S(2)}) copy-start(f32[256]{0:T(256)S(1)} %broadcast_multiply_fusion.5) | copy-start | bytes 3076
  122.0 12.4 %copy-start.8 = (f32[256]{0:T(256)}, f32[256]{0:T(256)S(1)}, u32[]{:S(2)}) copy-start(f32[256]{0:T(256)S(1)} %add_rsqrt_fusion.1) | copy-start | bytes 3076
  122.5 10.1 %copy-start.12 = (f32[768]{0:T(1024)S(1)}, f32[768]{0:T(1024)}, u32[]{:S(2)}) copy-start(f32[768]{0:T(1024)} %get-tuple-element.159) | copy-start | bytes 9220
  122.5 10.1 %slice-start.3 = ((s8[4718592]{0:T(1024)(128)(4,1)}), s8[524288]{0:T(1024)(128)(4,1)S(1)}, s32[]{:S(2)}) async-start(s8[4718592]{0:T(1024)(128)(4,1)} %bitcast.229), calls=%async_computation.3 | async-start | bytes 1048576
  132.6 1.6 copy-start.2
  134.2 0.6 copy-start.7
  134.4 0.6 copy-start.10
  139.3 3.2 %copy-start.18 = (f32[4,768]{1,0:T(4,128)S(1)}, f32[4,768]{1,0:T(4,128)}, u32[]{:S(2)}) copy-start(f32[4,768]{1,0:T(4,128)} %get-tuple-element.69) | copy-start | bytes 36868
  139.3 3.2 %copy-start.20 = (f32[4,256,768]{2,1,0:T(8,128)S(1)}, f32[4,256,768]{2,1,0:T(8,128)}, u32[]{:S(2)}) copy-start(f32[4,256,768]{2,1,0:T(8,128)} %get-tuple-element.170) | copy-start | bytes 9437188
  141.3 7.4 %slice-start = ((s8[4718592]{0:T(1024)(128)(4,1)}), s8[4194304]{0:T(1024)(128)(4,1)S(1)}, s32[]{:S(2)}) async-start(s8[4718592]{0:T(1024)(128)(4,1)} %bitcast.225), calls=%async_computation | async-start | bytes 8388608
  142.5 6.2 %copy-start.6 = (f32[256]{0:T(256)S(1)}, f32[256]{0:T(256)}, u32[]{:S(2)}) copy-start(f32[256]{0:T(256)} %copy-done.5) | copy-start | bytes 3076
  142.5 6.2 %copy-start.9 = (f32[256]{0:T(256)S(1)}, f32[256]{0:T(256)}, u32[]{:S(2)}) copy-start(f32[256]{0:T(256)} %copy-done.8) | copy-start | bytes 3076
  142.5 6.2 %slice-start.1 = ((s8[4718592]{0:T(1024)(128)(4,1)}), s8[524288]{0:T(1024)(128)(4,1)S(1)}, s32[]{:S(2)}) async-start(s8[4718592]{0:T(1024)(128)(4,1)} %bitcast.225), calls=%async_computation.1 | async-start | bytes 1048576
  150.4 3.4 %copy-start.3 = (bf16[4,256,768]{2,1,0:T(8,128)(2,1)S(1)}, bf16[4,256,768]{2,1,0:T(8,128)(2,1)}, u32[]{:S(2)}) copy-start(bf16[4,256,768]{2,1,0:T(8,128)(2,1)} %copy-done.2) | copy-start | bytes 4718596
  150.8 6.7 %copy-start = (f32[256,768]{1,0:T(8,128)}, f32[256,768]{1,0:T(8,128)S(1)}, u32[]{:S(2)}) copy-start(f32[256,768]{1,0:T(8,128)S(1)} %get-tuple-element.166.refs_24_) | copy-start | bytes 2359300
  157.5 7.9 %copy-start.4 = (bf16[4,192,256]{2,1,0:T(8,128)(2,1)S(1)}, bf16[4,192,256]{2,1,0:T(8,128)(2,1)}, u32[]{:S(2)}) copy-start(bf16[4,192,256]{2,1,0:T(8,128)(2,1)} %get-tuple-element.71) | copy-start | bytes 1179652
  157.5 8.8 %copy-start.11 = (f32[128,14]{0,1:T(8,128)S(1)}, f32[128,14]{0,1:T(8,128)}, u32[]{:S(2)}) copy-start(f32[128,14]{0,1:T(8,128)} %param.44) | copy-start | bytes 21508
  157.5 9.5 %copy-start.19 = (f32[14]{0:T(128)S(1)}, f32[14]{0:T(128)}, u32[]{:S(2)}) copy-start(f32[14]{0:T(128)} %param.45) | copy-start | bytes 172
  157.5 9.5 %copy-start.13 = (f32[128]{0:T(128)S(1)}, f32[128]{0:T(128)}, u32[]{:S(2)}) copy-start(f32[128]{0:T(128)} %param.43) | copy-start | bytes 1540
  157.5 9.5 %copy-start.14 = (f32[128]{0:T(128)S(1)}, f32[128]{0:T(128)}, u32[]{:S(2)}) copy-start(f32[128]{0:T(128)} %param.41) | copy-start | bytes 1540
  157.5 9.5 %copy-start.15 = (f32[128]{0:T(128)S(1)}, f32[128]{0:T(128)}, u32[]{:S(2)}) copy-start(f32[128]{0:T(128)} %param.40) | copy-start | bytes 1540

commit v3 on v2

--- a/solution.py
+++ b/solution.py
@@ -571,9 +571,7 @@
         ref = outs[k].at[at, r ^ bit, 1 - d]
         rcopy(ref, ref, ps.at[k, at, bit], pr.at[k, at, bit], pn).wait_recv()
 
-    for k in range(kinds):
-        pltpu.make_async_copy(shards[k], outs[k].at[c, r, d], own_sem.at[k]).start()
-
+    def set_out(k):
         @pl.when(has_up)
         def _():
             z_send(k, c, 0, 1).start()
@@ -581,6 +579,11 @@
         @pl.when(has_down)
         def _():
             z_send(k, c, 1, 1).start()
+
+    for k in range(kinds):
+        pltpu.make_async_copy(shards[k], outs[k].at[c, r, d], own_sem.at[k]).start()
+        if k < kinds - 1:
+            set_out(k)
 
     def spread(k, at, own):
         to_x(k, at, own).start()
@@ -773,34 +776,45 @@
     wide = q_src.shape[1]
     lag = 3
     ready = 2 * len(steps) + 2 * lag
-    rest = len(jobs) - ready - 1
-    for i in range(len(jobs) + 2 * lag):
-        if i == ready:
-            prepare()
-            settle(0)
-            settle(1)
-        if ready <= i < ready + 4:
-            project((3, 2, 1, 0)[i - ready])
-        if ready + 3 <= i < ready + 7:
-            spread_out(i - ready - 3)
-        if i == ready + 5:
-            unpack()
-        if i == ready + 7:
-            collect()
-        if ready + 8 <= i < ready + 12:
-            attend((3, 2, 1, 0)[i - ready - 8])
-        if i <= ready:
-            first(*jobs[i])
-        elif i <= ready + 4:
-            for n in range(ready + 1 + (i - ready - 1) * 2, min(ready + 1 + (i - ready) * 2, len(jobs))):
-                first(*jobs[n])
-            if i == ready + 4:
-                for start, _ in late_moves:
-                    start()
-        if 0 <= i - lag < len(jobs):
-            second(*jobs[i - lag])
-        if 0 <= i - 2 * lag < len(jobs):
-            third(*jobs[i - 2 * lag])
+
+    def do(**stages):
+        for stage, numbers in stages.items():
+            for n in numbers:
+                {"f": first, "s": second, "t": third}[stage](*jobs[n])
+
+    for i in range(ready):
+        do(f=[i], s=[i - lag] if i >= lag else [], t=[i - 2 * lag] if i >= 2 * lag else [])
+    prepare()
+    settle(0)
+    settle(1)
+    project(3)
+    do(f=[20], s=[17], t=[14])
+    project(2)
+    do(f=[21], s=[18], t=[15])
+    project(1)
+    do(s=[19], t=[16])
+    project(0)
+    set_out(kinds - 1)
+    do(s=[20], t=[17])
+    for start, _ in late_moves:
+        start()
+    for at in range(3):
+        spread_out(at)
+        do(t=[18 + at])
+    spread_out(3)
+    do(s=[21])
+    unpack()
+    collect()
+    attend(3)
+    do(f=[22, 23])
+    attend(2)
+    do(f=[24, 25], s=[22])
+    attend(1)
+    do(f=[26, 27], s=[23], t=[21])
+    attend(0)
+    for n in (24, 25, 26, 27):
+        do(s=[n], t=[n - 2])
+    do(t=[26, 27])
 
     for k in range(kinds):
         if k > 1:
@@ -1307,7 +1321,7 @@
     outs, refs = refs[: kinds + 1], refs[kinds + 1 :]
     (give_out, out_out, small_out), refs = refs[:3], refs[3:]
     (total, theirs, dqkv, own_grads, dpad, weights, resid_t, give_src), refs = refs[:8], refs[8:]
-    (dctx, dq, dkv, kn, vn, q3, dc3, dq_scr, dkv_scr, bias_scr, landed, kcol), refs = refs[:12], refs[12:]
+    (dctx, dq, dkv, kn, vn, q3, dc3, dq_scr, dkv_scr, bias_scr, landed, kcol, qsegs, deltas), refs = refs[:14], refs[14:]
     (hidden, logit, stats, stats_all, small), refs = refs[:5], refs[5:]
     parts, refs = refs[:10], refs[10:]
     (send, recv, psend, precv), sems, (wl, gl, gs, gr), refs = refs[:4], refs[4:8], refs[8:12], refs[12:]
@@ -1381,48 +1395,64 @@
         def _(j):
             kn[j] = kv_ref[j, pl.ds(0, wide)].astype(f32).T.astype(bf16)
             vn[j] = kv_ref[j, pl.ds(wide, wide)].astype(f32).T.astype(bf16)
-            dkv_scr[j] = jnp.zeros((deep, tile), f32)
 
         for j in range(tiles):
             kcol[j] = jnp.broadcast_to(segment(j), (128, own)).T
         bias_scr[...] = jnp.zeros_like(bias_scr)
+        dq_scr[...] = jnp.zeros_like(dq_scr)
+        for block in range(4):
+            block_rows(q_ref.at[pl.ds(block, 1)], heads, scale, q3.at[block])
+            qsegs[block] = jnp.concatenate([segment(2 * block + d)] * heads, axis=1)
         for j in (1, 2, 3):
             to_heads(j).wait_recv()
+        for block in range(4):
+            block_rows(dctx.at[pl.ds(block, 1)], heads, 1.0, dc3.at[block])
+            product = ctx_ref[block].astype(f32) * dctx[block].astype(f32)
+            deltas[block] = jnp.concatenate(
+                [jnp.sum(product[h * HD : (h + 1) * HD], axis=0, keepdims=True) for h in range(heads)], axis=1
+            )
 
     ones = jnp.ones((8, own), bf16)
     across = (((1,), (1,)), ((), ()))
 
-    def attend_block(block, _):
-        q_at, dc_at = q_ref.at[pl.ds(block, 1)], dctx.at[pl.ds(block, 1)]
-        block_rows(q_at, heads, scale, q3)
-        block_rows(dc_at, heads, 1.0, dc3)
-        qseg = jnp.concatenate([segment(2 * block + d)] * heads, axis=1)
-        lse = lse_ref[block]
-        product = ctx_ref[block].astype(f32) * dctx[block].astype(f32)
-        delta = jnp.concatenate(
-            [jnp.sum(product[h * HD : (h + 1) * HD], axis=0, keepdims=True) for h in range(heads)], axis=1
-        )
-        dq_scr[...] = jnp.zeros_like(dq_scr)
-        here = 2 * block + d
-
-        @pl.loop(jnp.maximum(here - 4, 0), jnp.minimum(here + 5, tiles))
-        def _(j):
-            s = jnp.dot(kn[j], q3[...], preferred_element_type=f32)
-            same = jnp.concatenate([kcol[j]] * (heads * own // 128), axis=1) == qseg
-            p = jnp.exp(jnp.where(same, s, masked_value) - lse)
-            d_p = jnp.dot(vn[j], dc3[...], preferred_element_type=f32)
-            d_s = (p * (d_p - delta)).astype(bf16)
-            p = p.astype(bf16)
-            for h in range(heads):
-                rows, lanes = pl.ds(h * HD, HD), slice(h * own, (h + 1) * own)
-                dq_scr[rows] += jnp.dot(kv_ref[j, rows], d_s[:, lanes], preferred_element_type=f32)
-                dkv_scr[j, rows] += lax.dot_general(q3[rows, lanes], d_s[:, lanes], across, preferred_element_type=f32)
-                low = pl.ds(wide + h * HD, HD)
-                dkv_scr[j, low] += lax.dot_general(dctx[block, rows], p[:, lanes], across, preferred_element_type=f32)
-
-        made = (dq_scr[...] * scale).astype(bf16)
-        dq[block] = made
-        bias_scr[:, :wide] += lax.dot_general(ones, made, across, preferred_element_type=f32)
+    def attend(j, _):
+        if j < 3:
+            settle(j + 1)
+        for core in range(2):
+            tile_at = 2 * (c ^ j) + core
+            k_nat, v_nat = kn.at[tile_at], vn.at[tile_at]
+            k_t = kv_ref.at[tile_at]
+            seen = jnp.concatenate([kcol[tile_at]] * (heads * own // 128), axis=1)
+            dkv_scr[...] = jnp.zeros_like(dkv_scr)
+
+            @pl.loop(jnp.maximum(tile_at - 3 - d, 0) // 2, jnp.minimum((tile_at + 4 - d) // 2 + 1, 4))
+            def _(block):
+                s = jnp.dot(k_nat[...], q3[block], preferred_element_type=f32)
+                p = jnp.exp(jnp.where(seen == qsegs[block], s, masked_value) - lse_ref[block])
+                d_p = jnp.dot(v_nat[...], dc3[block], preferred_element_type=f32)
+                d_s = (p * (d_p - deltas[block])).astype(bf16)
+                p = p.astype(bf16)
+                for h in range(heads):
+                    rows, lanes = pl.ds(h * HD, HD), slice(h * own, (h + 1) * own)
+                    low = pl.ds(wide + h * HD, HD)
+                    dq_scr[block, rows] += jnp.dot(k_t[rows], d_s[:, lanes], preferred_element_type=f32)
+                    dkv_scr[rows] += lax.dot_general(
+                        q3[block, rows, lanes], d_s[:, lanes], across, preferred_element_type=f32
+                    )
+                    dkv_scr[low] += lax.dot_general(dctx[block, rows], p[:, lanes], across, preferred_element_type=f32)
+
+            made = dkv_scr[...].astype(bf16)
+            dkv[c ^ j, core] = made
+            bias_scr[:, wide:] += lax.dot_general(ones, made[wide:], across, preferred_element_type=f32)
+        pair(j).start()
+
+    def settle(j):
+        pair(j).wait_recv()
+        if j:
+            total[c ^ j] = dkv[c ^ j, d] + theirs[c ^ j]
+            kv(j).start()
+        else:
+            landed[c, kv_rows] = dkv[c, d] + theirs[c]
 
     def pair(j):
         return rcopy(dkv.at[c ^ j, 1 - d], theirs.at[c ^ j], psend.at[j], precv.at[j], pn)
@@ -1435,26 +1465,13 @@
 
     def leave(_):
         for j in (3, 2, 1, 0):
-            for core in range(2):
-                tile_at = 2 * (c ^ j) + core
-                dkv[c ^ j, core] = dkv_scr[tile_at].astype(bf16)
-            pair(j).start()
+            made = (dq_scr[c ^ j] * scale).astype(bf16)
+            dq[c ^ j] = made
+            bias_scr[:, :wide] += lax.dot_general(ones, made, across, preferred_element_type=f32)
             if j:
                 q(j).start()
         landed[c, q_rows] = dq[c]
-        for j in (3, 2, 1):
-            pair(j).wait_recv()
-            total[c ^ j] = dkv[c ^ j, d] + theirs[c ^ j]
-            kv(j).start()
-        pair(0).wait_recv()
-        landed[c, kv_rows] = dkv[c, d] + theirs[c]
-
-        @pl.loop(0, 4)
-        def _(at):
-            for core in range(2):
-                some = dkv[at, core, pl.ds(wide, wide)]
-                bias_scr[:, wide:] += lax.dot_general(ones, some, across, preferred_element_type=f32)
-
+        settle(0)
         for i in range(3):
             small[pl.ds(1012 + 3 * c + i, 1)] = bias_scr[0:1, i * 128 : (i + 1) * 128]
 
@@ -1498,13 +1515,13 @@
 
         start()
 
-    gap = 6
-    hooks = [[] for _ in range(8 + gap + 5)]
-    hooks[1].append(student)
-    hooks[2].append(prepare)
-    for block in range(4):
-        hooks[3 + block].append(functools.partial(attend_block, block))
-    hooks[7].append(leave)
+    gap = 3
+    hooks = [[] for _ in range(max(8 + gap + 5, 8 + len(steps)))]
+    hooks[0].append(prepare)
+    for i, j in enumerate((3, 2, 1, 0)):
+        hooks[1 + i].append(functools.partial(attend, j))
+    hooks[5].append(leave)
+    hooks[6].append(student)
     for i, step in enumerate(steps):
         hooks[8 + i].append(lambda launch, step=step: step())
     for j in range(4):
@@ -1561,13 +1578,15 @@
             pltpu.VMEM((cols, 2, deep, own), bf16),
             pltpu.VMEM((tiles, own, wide), bf16),
             pltpu.VMEM((tiles, own, wide), bf16),
-            pltpu.VMEM((wide, wide // HD * own), bf16),
-            pltpu.VMEM((wide, wide // HD * own), bf16),
-            pltpu.VMEM((wide, own), f32),
-            pltpu.VMEM((tiles, deep, own), f32),
+            pltpu.VMEM((4, wide, wide // HD * own), bf16),
+            pltpu.VMEM((4, wide, wide // HD * own), bf16),
+            pltpu.VMEM((4, wide, own), f32),
+            pltpu.VMEM((deep, own), f32),
             pltpu.VMEM((8, deep), f32),
             pltpu.VMEM((cols, deep + wide, own), bf16),
             pltpu.VMEM((tiles, own, 128), f32),
+            pltpu.VMEM((4, 1, wide // HD * own), f32),
+            pltpu.VMEM((4, 1, wide // HD * own), f32),
             pltpu.VMEM((own, student_width), f32),
             pltpu.VMEM((own, student_width), f32),
             pltpu.VMEM((24, student_width), f32),

time: 314 us -> 291 us (0.927)
  Pallas kernels: 253 us -> 229 us
    pallas_call x1, Pallas kernels: 137 us -> 118 us  [tail_fast(): pl.pallas_call(functools.partial(tail_kernel, docs, classes, scale), out_...]
    pallas_call x1, Pallas kernels: 113 us -> 108 us  [head_fast(): pl.pallas_call(functools.partial(head_kernel, scale), out_shape=[shape((4...]
where the time goes in v3:
time: 291 us; the launch traced here: 290 us
  Pallas kernels  229 us (79%)
  matrix products  30 us (10%)
  local copies, waits for them, and re-layouts  21.1 us (7%)
  other arithmetic  8.3 us (3%)
    pallas_call x1, Pallas kernels, tail_fast(): pl.pallas_call(functools.partial(tail_kernel, docs, classes, scale), out_...  118 us
    pallas_call x1, Pallas kernels, head_fast(): pl.pallas_call(functools.partial(head_kernel, scale), out_shape=[shape((4...  108 us
    dot_general x1, matrix products, fast_local(): jnp.einsum('td,cdn->ctn', hidden_low, w_in_all, preferred_element_type=f32)  10.1 us
    unnamed x55, local copies, waits for them, and re-layouts  6.47 us
    dot_general x1, matrix products, fast_local(): jnp.einsum('td,cdn->ctn', d_ffn, w_back_all, preferred_element_type=f32)  6.21 us

profile of v3, /device:TPU:0, one launch (start us, length us, event | category | flops | bytes accessed | tf_op | source)
XLA Modules:
  0.0 290.0 jit_solution(3780762326887109766)
XLA Ops:
  0.7 0.7 copy.71
  1.4 0.7 pad.24
  2.1 0.6 pad.25.refs_6_
  2.7 1.3 broadcast_in_dim.58.refs_8_
  4.0 108.3 %head.1 = (bf16[4,4,2,96,768]{4,3,2,1,0:T(8,128)(2,1)}, bf16[4,4,2,96,768]{4,3,2,1,0:T(8,128)(2,1)}, bf16[4,4,2,96,768]{4,3,2,1,0:T(8,128)(2,1)}, bf16[4,192,256...) custom-call(bf16[192,576]{1,0:T(8,128)(2,1)} %refs_0_.1, ...), custom_call_target="tpu_custom_call" | custom-call | tf_op jit(solution)/shard_map/head/pallas_call | solution.py:881
  112.2 1.6 slice_reduce_fusion
  113.8 1.0 bitcast_convert_fusion
  114.9 0.3 copy.54
  115.2 0.0 slice-start.2
  115.2 1.7 fusion.49
  117.0 0.0 copy-start.5
  117.0 0.2 multiply_reduce_fusion.4
  117.2 0.0 copy-start.8
  117.2 0.4 copy-done.16
  117.6 10.1 %fusion.9 = (bf16[4,256,768]{2,1,0:T(8,128)(2,1)S(1)}, f32[4,256,768]{2,1,0:T(8,128)}, f32[4,768,256]{1,2,0:T(8,128)}) fusion(f32[4,768]{1,0:T(4,128)S(1)} %copy-done.17, bf16[4,768,768]{2,1,0:T(8,128)(2,1)S(1)} %bitcast.224, f32[256,768]{1,0:T(8,128)S(1)} %get-tuple-element.172, f32[768]{0:T(1024)S(1)} %get-tuple-element.160, ...), kind=kOutput, calls=%fused_computation.17 | convolution fusion | flops 1260847104 | bytes 13389824 | tf_op jit(solution)/shard_map/td,cdn->ctn/dot_general | solution.py:1761
  127.8 0.0 slice-done.2
  127.8 1.5 fusion.46
  129.3 0.0 copy-start.7
  129.4 0.2 multiply_reduce_fusion.3
  129.6 0.0 copy-start.10
  129.6 0.0 copy-done.5
  129.6 0.0 copy-done.8
  129.6 0.3 copy-done.7
  129.9 0.2 copy-done.10
  130.2 1.2 fusion.28
  131.4 1.9 copy.60
  133.3 1.2 copy.55
  134.5 2.0 fusion.33
  136.5 1.1 convert_reduce_fusion.1
  137.7 0.0 copy-done.18
  137.7 0.0 copy-done.20
  137.7 0.0 copy-start.6
  137.7 0.0 copy-start.9
  137.7 0.0 slice-start.1
  137.7 6.2 %convert_reduce_fusion = (f32[4,768]{1,0:T(4,128)}, bf16[4,256,768]{2,1,0:T(8,128)(2,1)S(1)}) fusion(f32[4,256,768]{2,1,0:T(8,128)S(1)} %copy-done.20, bf16[4,768,768]{2,1,0:T(8,128)(2,1)} %bitcast.228, f32[256,768]{1,0:T(8,128)S(1)} %get-tuple-element.164, f32[4,768,256]{1,2,0:T(8,128)} %get-tuple-element.175, f32[4,768]{1,0:T(4,128)S(1)} %copy-done.18), kind=kOutput, calls=%fused_computation.18 | convolution fusion | flops 1221522432 | bytes 13393920 | tf_op jit(solution)/shard_map/td,cdn->ctn/dot_general | solution.py:1775
  143.9 1.7 multiply_reduce_fusion
  145.7 0.3 convert_reduce_fusion.2
  146.0 0.0 copy-start
  146.0 1.3 convolution_convert_fusion.2
  147.2 0.6 broadcast_in_dim.67.refs_16_
  147.8 0.6 broadcast_in_dim.68.refs_17_
  148.4 0.6 broadcast_in_dim.69.refs_18_
  149.0 3.7 %convolution_convert_fusion = bf16[4,768,768]{1,2,0:T(8,128)(2,1)} fusion(bf16[4,256,768]{2,1,0:T(8,128)(2,1)S(1)} %copy-done.3, f32[256,768]{1,0:T(8,128)S(1)} %get-tuple-element.164), kind=kOutput, calls=%fused_computation.32 | convolution fusion | flops 1210515456 | bytes 7077888 | tf_op jit(solution)/shard_map/td,ctn->cdn/dot_general | solution.py:1774
  152.7 0.0 copy-start.13
  152.7 0.0 copy-start.14
  152.7 0.0 copy-start.15
  152.7 3.8 %convolution_convert_fusion.1 = bf16[4,768,768]{1,2,0:T(8,128)(2,1)} fusion(bf16[4,256,768]{2,1,0:T(8,128)(2,1)S(1)} %get-tuple-element.179, f32[256,768]{1,0:T(8,128)S(1)} %get-tuple-element.172, f32[768]{0:T(1024)S(1)} %get-tuple-element.160, f32[768]{0:T(1024)S(1)} %get-tuple-element.161, f32[256]{0:T(256)S(1)} %copy-done.9, f32[256]{0:T(256)S(1)} %copy-done.6), kind=kOutput, calls=%fused_computation.33 | convolution fusion | flops 1211301888 | bytes 7086080 | tf_op jit(solution)/shard_map/td,ctn->cdn/dot_general | solution.py:1779
  156.5 0.6 broadcast_in_dim.70.refs_19_
  157.1 0.6 broadcast_in_dim.71.refs_20_
  157.7 0.7 dynamic-slice_bitcast_fusion.1
  158.4 0.8 copy.61.refs_9_
  159.2 0.7 dynamic-slice_bitcast_fusion
  159.9 0.7 copy.62.refs_10_
  160.6 0.2 convert_reduce_fusion.3
  160.8 0.7 broadcast_in_dim.72.refs_21_
  161.5 0.1 copy.58
  161.6 0.6 pad.29.refs_14_
  162.3 0.6 select_maximum_fusion.refs_12_
  162.9 117.8 %tail.1 = (bf16[2,96,768]{2,1,0:T(8,128)(2,1)}, bf16[2,96,768]{2,1,0:T(8,128)(2,1)}, bf16[2,96,768]{2,1,0:T(8,128)(2,1)}, bf16[2,192,512]{2,1,0:T(8,128)(2,1)}, ...) custom-call(bf16[4,4,2,96,768]{4,3,2,1,0:T(8,128)(2,1)} %bitcast.205, bf16[4,4,2,96,768]{4,3,2,1,0:T(8,128)(2,1)} %bitcast.204, ...), custom_call_target="tpu_custom_call" | custom-call | tf_op jit(solution)/shard_map/tail/pallas_call | solution.py:1562
  280.7 3.4 %finish.1 = (f32[192,576]{1,0:T(8,128)}, f32[192,192]{1,0:T(8,128)}, f32[192,768]{1,0:T(8,128)}, f32[192,768]{1,0:T(8,128)}, f32[2,192,512]{2,1,0:T(8,128)}, /*i...) custom-call(bf16[2,96,768]{2,1,0:T(8,128)(2,1)} %get-tuple-element.8, ...), custom_call_target="tpu_custom_call" | custom-call | tf_op jit(solution)/shard_map/finish/pallas_call | solution.py:1662
  284.1 1.5 copy.64
  285.6 1.3 copy.63
  286.9 1.3 reduce.8
  288.2 1.8 copy.73
  (44 shorter events, 0.1 us)
Async XLA Ops:
  112.2 3.0 %copy-start.1 = (bf16[768,768]{1,0:T(8,128)(2,1)S(1)}, bf16[768,768]{1,0:T(8,128)(2,1)}, u32[]{:S(2)}) copy-start(bf16[768,768]{1,0:T(8,128)(2,1)} %get-tuple-element.67) | copy-start | bytes 3538948
  114.9 2.3 copy-start.17
  115.2 2.5 copy-start.16
  115.2 12.6 %slice-start.2 = ((s8[4718592]{0:T(1024)(128)(4,1)}), s8[4194304]{0:T(1024)(128)(4,1)S(1)}, s32[]{:S(2)}) async-start(s8[4718592]{0:T(1024)(128)(4,1)} %bitcast.229), calls=%async_computation.2 | async-start | bytes 8388608
  117.0 12.7 %copy-start.5 = (f32[256]{0:T(256)}, f32[256]{0:T(256)S(1)}, u32[]{:S(2)}) copy-start(f32[256]{0:T(256)S(1)} %broadcast_multiply_fusion.5) | copy-start | bytes 3076
  117.2 12.4 %copy-start.8 = (f32[256]{0:T(256)}, f32[256]{0:T(256)S(1)}, u32[]{:S(2)}) copy-start(f32[256]{0:T(256)S(1)} %add_rsqrt_fusion.1) | copy-start | bytes 3076
  117.6 10.1 %copy-start.12 = (f32[768]{0:T(1024)S(1)}, f32[768]{0:T(1024)}, u32[]{:S(2)}) copy-start(f32[768]{0:T(1024)} %get-tuple-element.159) | copy-start | bytes 9220
  117.6 10.1 %slice-start.3 = ((s8[4718592]{0:T(1024)(128)(4,1)}), s8[524288]{0:T(1024)(128)(4,1)S(1)}, s32[]{:S(2)}) async-start(s8[4718592]{0:T(1024)(128)(4,1)} %bitcast.229), calls=%async_computation.3 | async-start | bytes 1048576
  127.8 1.6 copy-start.2
  129.3 0.6 copy-start.7
  129.6 0.6 copy-start.10
  134.5 3.2 %copy-start.18 = (f32[4,768]{1,0:T(4,128)S(1)}, f32[4,768]{1,0:T(4,128)}, u32[]{:S(2)}) copy-start(f32[4,768]{1,0:T(4,128)} %get-tuple-element.69) | copy-start | bytes 36868
  134.5 3.2 %copy-start.20 = (f32[4,256,768]{2,1,0:T(8,128)S(1)}, f32[4,256,768]{2,1,0:T(8,128)}, u32[]{:S(2)}) copy-start(f32[4,256,768]{2,1,0:T(8,128)} %get-tuple-element.170) | copy-start | bytes 9437188
  136.5 7.4 %slice-start = ((s8[4718592]{0:T(1024)(128)(4,1)}), s8[4194304]{0:T(1024)(128)(4,1)S(1)}, s32[]{:S(2)}) async-start(s8[4718592]{0:T(1024)(128)(4,1)} %bitcast.225), calls=%async_computation | async-start | bytes 8388608
  137.7 6.2 %copy-start.6 = (f32[256]{0:T(256)S(1)}, f32[256]{0:T(256)}, u32[]{:S(2)}) copy-start(f32[256]{0:T(256)} %copy-done.5) | copy-start | bytes 3076
  137.7 6.2 %copy-start.9 = (f32[256]{0:T(256)S(1)}, f32[256]{0:T(256)}, u32[]{:S(2)}) copy-start(f32[256]{0:T(256)} %copy-done.8) | copy-start | bytes 3076
  137.7 6.2 %slice-start.1 = ((s8[4718592]{0:T(1024)(128)(4,1)}), s8[524288]{0:T(1024)(128)(4,1)S(1)}, s32[]{:S(2)}) async-start(s8[4718592]{0:T(1024)(128)(4,1)} %bitcast.225), calls=%async_computation.1 | async-start | bytes 1048576
  145.6 3.4 %copy-start.3 = (bf16[4,256,768]{2,1,0:T(8,128)(2,1)S(1)}, bf16[4,256,768]{2,1,0:T(8,128)(2,1)}, u32[]{:S(2)}) copy-start(bf16[4,256,768]{2,1,0:T(8,128)(2,1)} %copy-done.2) | copy-start | bytes 4718596
  146.0 6.7 %copy-start = (f32[256,768]{1,0:T(8,128)}, f32[256,768]{1,0:T(8,128)S(1)}, u32[]{:S(2)}) copy-start(f32[256,768]{1,0:T(8,128)S(1)} %get-tuple-element.166.refs_24_) | copy-start | bytes 2359300
  152.7 7.9 %copy-start.4 = (bf16[4,192,256]{2,1,0:T(8,128)(2,1)S(1)}, bf16[4,192,256]{2,1,0:T(8,128)(2,1)}, u32[]{:S(2)}) copy-start(bf16[4,192,256]{2,1,0:T(8,128)(2,1)} %get-tuple-element.71) | copy-start | bytes 1179652
  152.7 8.8 %copy-start.11 = (f32[128,14]{0,1:T(8,128)S(1)}, f32[128,14]{0,1:T(8,128)}, u32[]{:S(2)}) copy-start(f32[128,14]{0,1:T(8,128)} %param.44) | copy-start | bytes 21508
  152.7 9.5 %copy-start.19 = (f32[14]{0:T(128)S(1)}, f32[14]{0:T(128)}, u32[]{:S(2)}) copy-start(f32[14]{0:T(128)} %param.45) | copy-start | bytes 172
  152.7 9.5 %copy-start.13 = (f32[128]{0:T(128)S(1)}, f32[128]{0:T(128)}, u32[]{:S(2)}) copy-start(f32[128]{0:T(128)} %param.43) | copy-start | bytes 1540
  152.7 9.5 %copy-start.14 = (f32[128]{0:T(128)S(1)}, f32[128]{0:T(128)}, u32[]{:S(2)}) copy-start(f32[128]{0:T(128)} %param.41) | copy-start | bytes 1540
  152.7 9.5 %copy-start.15 = (f32[128]{0:T(128)S(1)}, f32[128]{0:T(128)}, u32[]{:S(2)}) copy-start(f32[128]{0:T(128)} %param.40) | copy-start | bytes 1540

commit v4 on v3

--- a/solution.py
+++ b/solution.py
@@ -1,4 +1,5 @@
 import functools
+import math
 import jax
 import jax.numpy as jnp
 from jax import lax
@@ -1683,6 +1684,146 @@
                 out[spot] = jnp.zeros((HD, own), out.dtype)
 
 
+def spread_of(values):
+    mean_v = jnp.mean(values, axis=1, keepdims=True)
+    center = values - mean_v
+    inv_std = lax.rsqrt(jnp.mean(center * center, axis=1, keepdims=True) + norm_eps)
+    return center * inv_std, inv_std
+
+
+def spread_back(grad_hat, normed, inv_std):
+    return inv_std * (
+        grad_hat
+        - jnp.mean(grad_hat, axis=1, keepdims=True)
+        - normed * jnp.mean(grad_hat * normed, axis=1, keepdims=True)
+    )
+
+
+def dense_kernel(
+    ctx_ref, x_ref, cot_ref, wo_ref, vec_ref, b_in_ref, w_in_hbm, w_back_hbm,
+    g_in_hbm, g_back_hbm, dctx_ref, out_ref, out_t_ref, resid_ref, gb_in_ref, gb_out_ref, g1_ref, b1_ref, gb_back_ref,
+    g2_ref, b2_ref,
+    w_in, w_back, g_in, g_back, slope, act, total, hidden, hat, low, low_t, in_sem, back_sem, gi_sem, gb_sem,
+):
+    cols = w_in.shape[0]
+    across = (((1,), (1,)), ((), ()))
+
+    def fetch(c):
+        return (
+            pltpu.make_async_copy(w_in_hbm.at[c], w_in.at[c], in_sem.at[c]),
+            pltpu.make_async_copy(w_back_hbm.at[c], w_back.at[c], back_sem.at[c]),
+        )
+
+    def store(c):
+        return (
+            pltpu.make_async_copy(g_in.at[c], g_in_hbm.at[c], gi_sem.at[c]),
+            pltpu.make_async_copy(g_back.at[c], g_back_hbm.at[c], gb_sem.at[c]),
+        )
+
+    for c in range(cols):
+        for copy in fetch(c):
+            copy.start()
+
+    def natural(ref):
+        return ref[...].reshape(-1, ref.shape[2]).astype(f32).T
+
+    b_out, gain_one, bias_one, b_back, gain_two, bias_two = [vec_ref[i : i + 1] for i in range(6)]
+    attn_out = jnp.dot(natural(ctx_ref).astype(bf16), wo_ref[...], preferred_element_type=f32) + b_out
+    hat_one, inv_one = spread_of(natural(x_ref) + attn_out)
+    hidden_one = hat_one * gain_one + bias_one
+    hat[...] = hat_one
+    hidden[...] = hidden_one
+    low[...] = hidden_one.astype(bf16)
+    low_t[...] = hidden_one.T.astype(bf16)
+    total[...] = jnp.zeros_like(total)
+
+    @pl.loop(0, cols)
+    def _(c):
+        into, out = fetch(c)
+        into.wait()
+        pre = jnp.dot(low[...], w_in[c], preferred_element_type=f32) + b_in_ref[pl.ds(c, 1)]
+        share = 0.5 + 0.5 * lax.erf(pre * (0.5**0.5))
+        slope[c] = share + pre * (jnp.exp(-0.5 * pre * pre) * (0.5 / math.pi) ** 0.5)
+        made = (pre * share).astype(bf16)
+        act[c] = made
+        out.wait()
+        total[...] += lax.dot_general(made, w_back[c], across, preferred_element_type=f32)
+
+    hat_two, inv_two = spread_of(hidden[...] + total[...] + b_back)
+    layer_out = hat_two * gain_two + bias_two
+    out_ref[...] = layer_out.astype(bf16)
+    out_t_ref[...] = layer_out.T.astype(bf16).reshape(out_t_ref.shape)
+    cot = natural(cot_ref)
+    g2_ref[...] = jnp.sum(cot * hat_two, axis=0, keepdims=True)
+    b2_ref[...] = jnp.sum(cot, axis=0, keepdims=True)
+    d_two = spread_back(cot * gain_two, hat_two, inv_two)
+    d_ffn = d_two.astype(bf16)
+    gb_back_ref[...] = jnp.sum(d_ffn.astype(f32), axis=0, keepdims=True)
+    d_ffn_t = d_two.T.astype(bf16)
+    total[...] = d_two
+
+    @pl.loop(0, cols)
+    def _(c):
+        to_in, to_back = store(c)
+        g_back[c] = jnp.dot(d_ffn_t, act[c], preferred_element_type=f32).astype(bf16)
+        to_back.start()
+        d_pre = (slope[c] * jnp.dot(d_ffn, w_back[c], preferred_element_type=f32)).astype(bf16)
+        gb_in_ref[pl.ds(c, 1)] = jnp.sum(d_pre.astype(f32), axis=0, keepdims=True)
+        total[...] += lax.dot_general(d_pre, w_in[c], across, preferred_element_type=f32)
+        g_in[c] = jnp.dot(low_t[...], d_pre, preferred_element_type=f32).astype(bf16)
+        to_in.start()
+
+    d_hidden, hat_one = total[...], hat[...]
+    g1_ref[...] = jnp.sum(d_hidden * hat_one, axis=0, keepdims=True)
+    b1_ref[...] = jnp.sum(d_hidden, axis=0, keepdims=True)
+    d_one = spread_back(d_hidden * gain_one, hat_one, inv_one)
+    resid_ref[...] = d_one
+    d_attn = d_one.astype(bf16)
+    gb_out_ref[...] = jnp.sum(d_attn.astype(f32), axis=0, keepdims=True)
+    d_ctx = lax.dot_general(wo_ref[...], d_attn, across, preferred_element_type=f32)
+    dctx_ref[...] = d_ctx.astype(bf16).reshape(dctx_ref.shape)
+
+    @pl.loop(0, cols)
+    def _(c):
+        for copy in store(c):
+            copy.wait()
+
+
+def dense_fast(ctx, x, cot, wo, vec, b_in, w_in, w_back):
+    cols, width, hidden = w_in.shape
+    own = x.shape[2]
+    dma = pltpu.SemaphoreType.DMA
+    shape = jax.ShapeDtypeStruct
+    line = shape((1, width), f32)
+    weight = shape(w_in.shape, bf16)
+    return pl.pallas_call(
+        dense_kernel,
+        out_shape=[
+            weight, weight, shape(ctx.shape, bf16), shape((own, width), bf16), shape(x.shape, bf16),
+            shape((own, width), f32), shape((cols, hidden), f32),
+        ]
+        + [line] * 6,
+        in_specs=[VM] * 6 + [HBM] * 2,
+        out_specs=[HBM] * 2 + [VM] * 11,
+        scratch_shapes=[
+            pltpu.VMEM((cols, width, hidden), bf16),
+            pltpu.VMEM((cols, width, hidden), bf16),
+            pltpu.VMEM((cols, width, hidden), bf16),
+            pltpu.VMEM((cols, width, hidden), bf16),
+            pltpu.VMEM((cols, own, hidden), f32),
+            pltpu.VMEM((cols, own, hidden), bf16),
+            pltpu.VMEM((own, width), f32),
+            pltpu.VMEM((own, width), f32),
+            pltpu.VMEM((own, width), f32),
+            pltpu.VMEM((own, width), bf16),
+            pltpu.VMEM((width, own), bf16),
+            dma((cols,)), dma((cols,)), dma((cols,)), dma((cols,)),
+        ],
+        compiler_params=pltpu.CompilerParams(vmem_limit_bytes=56 * 1024 * 1024),
+        name="dense",
+    )(ctx, x, cot, wo, vec, b_in, w_in, w_back)
+
+
 def fast_local(
     tokens,
     segments,
@@ -1746,46 +1887,16 @@
     )
     w_in_all = w_in_all.reshape(cols, width, hidden_col)
     w_back_all = w_back_all.reshape(cols, width, hidden_col)
-    b_out_a, gain_one, bias_one, b_back_a, gain_two, bias_two = [row_vectors[i] for i in range(6)]
-    x_t, ctx_t = x_parts.reshape(width, own), ctx_parts.reshape(width, own)
     kv = kv.reshape(cols * parts, 2 * width_col, own)
     own_ints = lax.dynamic_index_in_dim(ints.reshape(seqs, 16, own), row_index, 0, False)
     seg_own = lax.dynamic_index_in_dim(own_ints, 2 * col_index + dp_index, 0, False)
     label_seq = own_ints[seq_len // own, :docs_count]
 
-    x = x_t.T
-    attn_out = mm(ctx_t, w_out_all, ((0,), (0,))) + b_out_a
-    normed_one, inv_one = normalize(x.astype(f32) + attn_out)
-    hidden_one = normed_one * gain_one + bias_one
-    hidden_low = hidden_one.astype(bf16)
-    pre_act = jnp.einsum("td,cdn->ctn", hidden_low, w_in_all, preferred_element_type=f32)
-    pre_act = pre_act + b_in_all[:, None, :]
-    act = gelu_exact(pre_act).astype(bf16)
-    ffn_out = jnp.einsum("ctn,cdn->td", act, w_back_all, preferred_element_type=f32) + b_back_a
-    normed_two, inv_two = normalize(hidden_one + ffn_out)
-    layer_out = (normed_two * gain_two + bias_two).astype(bf16)
-
-    d_out = c_parts.reshape(width, own).T.astype(f32)
-    g_ln2_gain = jnp.sum(d_out * normed_two, axis=0)
-    g_ln2_bias = jnp.sum(d_out, axis=0)
-    d_resid_two = normalize_back(d_out * gain_two, normed_two, inv_two)
-    d_ffn = d_resid_two.astype(bf16)
-    g_back_bias = jnp.sum(d_ffn.astype(f32), axis=0)
-    g_back = jnp.einsum("td,ctn->cdn", d_ffn, act, preferred_element_type=f32)
-    d_act = jnp.einsum("td,cdn->ctn", d_ffn, w_back_all, preferred_element_type=f32)
-    _, gelu_fn = jax.vjp(gelu_exact, pre_act)
-    d_pre = gelu_fn(d_act)[0].astype(bf16)
-    g_in_bias = jnp.sum(d_pre.astype(f32), axis=1)
-    g_in = jnp.einsum("td,ctn->cdn", hidden_low, d_pre, preferred_element_type=f32)
-    d_hidden_one = d_resid_two + jnp.einsum(
-        "ctn,cdn->td", d_pre, w_in_all, preferred_element_type=f32
-    )
-    g_ln1_gain = jnp.sum(d_hidden_one * normed_one, axis=0)
-    g_ln1_bias = jnp.sum(d_hidden_one, axis=0)
-    d_resid_one = normalize_back(d_hidden_one * gain_one, normed_one, inv_one)
-    d_attn = d_resid_one.astype(bf16)
-    g_out_bias = jnp.sum(d_attn.astype(f32), axis=0)
-    d_ctx = mm(w_out_all, d_attn, ((1,), (1,))).astype(bf16)
+    (
+        g_in, g_back, d_ctx, layer_out, out_t, d_resid_one, g_in_bias, g_out_bias, g_ln1_gain, g_ln1_bias, g_back_bias,
+        g_ln2_gain, g_ln2_bias,
+    ) = dense_fast(ctx_parts, x_parts, c_parts, w_out_all, row_vectors, b_in_all, w_in_all, w_back_all)
+
     blocked = (cols, rows, parts, width_row // parts, -1)
     lane_pad = ((0, 0), (0, 128 - class_count))
     student_vectors = jnp.stack([s_bias, s_query, s_mid_bias, jnp.pad(s_cls_bias, (0, 128 - class_count))])
@@ -1794,8 +1905,8 @@
         docs_count,
         class_count,
         score_scale,
-        [g_in.astype(bf16).reshape(blocked), g_back.astype(bf16).reshape(blocked)],
-        [queries, kv, lse, context, d_ctx.reshape(cols, width_col, own), ints],
+        [g_in.reshape(blocked), g_back.reshape(blocked)],
+        [queries, kv, lse, context, d_ctx, ints],
         [
             layer_out,
             seg_own[:, None],
@@ -1805,10 +1916,9 @@
             s_mid,
             jnp.pad(s_cls, lane_pad),
         ],
-        [g_in_bias]
-        + [v[None] for v in (g_out_bias, g_ln1_gain, g_ln1_bias, g_back_bias, g_ln2_gain, g_ln2_bias)],
+        [g_in_bias, g_out_bias, g_ln1_gain, g_ln1_bias, g_back_bias, g_ln2_gain, g_ln2_bias],
         [x_parts, ctx_parts, d_resid_one],
-        layer_out.T,
+        out_t.reshape(width, own),
         w_attn,
         4,
     )

time: 291 us -> 262 us (0.900)
  matrix products: 30 us -> 0 us
  Pallas kernels: 229 us -> 247 us
  local copies, waits for them, and re-layouts: 21.1 us -> 11.6 us
  other arithmetic: 8.3 us -> 1.88 us
    dot_general x8 -> x0, matrix products: 30 us -> none  [the longest x1 10.1 us: fast_local(): jnp.einsum('td,cdn->ctn', hidden_low, w_in_all, preferred_element_type=f32)]
    pallas_call x0 -> x1, Pallas kernels: none -> 17.1 us  [dense_fast(): pl.pallas_call(dense_kernel, out_shape=[weight, weight, shape(ctx.shape,...]
    reduce_sum x6 -> x0, other arithmetic: 4.08 us -> none  [the longest x1 2.01 us: fast_local(): g_ln2_gain = jnp.sum(d_out * normed_two, axis=0)]
    broadcast_in_dim x6 -> x0, local copies, waits for them, and re-layouts: 3.59 us -> none  [fast_local(): v[None]]
    convert_element_type x3 -> x0, local copies, waits for them, and re-layouts: 3.34 us -> none  [the longest x1 1.91 us: fast_local(): layer_out = (normed_two * gain_two + bias_two).astype(bf16)]
    unnamed x55 -> x15, local copies, waits for them, and re-layouts: 6.47 us -> 5.43 us
where the time goes in v4:
time: 262 us; the launch traced here: 261 us
  Pallas kernels  247 us (94%)
  local copies, waits for them, and re-layouts  11.6 us (4%)
    pallas_call x1, Pallas kernels, tail_fast(): pl.pallas_call(functools.partial(tail_kernel, docs, classes, scale), out_...  118 us
    pallas_call x1, Pallas kernels, head_fast(): pl.pallas_call(functools.partial(head_kernel, scale), out_shape=[shape((4...  109 us
    pallas_call x1, Pallas kernels, dense_fast(): pl.pallas_call(dense_kernel, out_shape=[weight, weight, shape(ctx.shape,...  17.1 us
    unnamed x15, local copies, waits for them, and re-layouts  5.43 us

profile of v4, /device:TPU:0, one launch (start us, length us, event | category | flops | bytes accessed | tf_op | source)
XLA Modules:
  0.0 261.3 jit_solution(14641445725451164054)
XLA Ops:
  0.7 0.7 copy.56
  1.4 0.7 pad.24
  2.1 0.6 pad.25.refs_6_
  2.7 1.3 broadcast_in_dim.31.refs_8_
  4.0 108.6 %head.1 = (bf16[4,4,2,96,768]{4,3,2,1,0:T(8,128)(2,1)}, bf16[4,4,2,96,768]{4,3,2,1,0:T(8,128)(2,1)}, bf16[4,4,2,96,768]{4,3,2,1,0:T(8,128)(2,1)}, bf16[4,192,256...) custom-call(bf16[192,576]{1,0:T(8,128)(2,1)} %refs_0_.1, ...), custom_call_target="tpu_custom_call" | custom-call | tf_op jit(solution)/shard_map/head/pallas_call | solution.py:882
  112.6 0.0 copy-start
  112.6 0.0 copy-start.4
  112.6 0.0 copy-start.1
  112.6 0.0 copy-start.2
  112.6 0.0 copy-start.3
  112.6 17.1 %dense.1 = (bf16[4,768,768]{2,1,0:T(8,128)(2,1)}, bf16[4,768,768]{2,1,0:T(8,128)(2,1)}, bf16[4,192,256]{2,1,0:T(8,128)(2,1)}, bf16[256,768]{1,0:T(8,128)(2,1)}, ...) custom-call(bf16[4,192,256]{2,1,0:T(8,128)(2,1)} %get-tuple-element., ...), custom_call_target="tpu_custom_call" | custom-call | tf_op jit(solution)/shard_map/dense/pallas_call | solution.py:1799
  129.8 0.7 dynamic-slice_bitcast_fusion.1
  130.5 0.8 copy.50.refs_9_
  131.3 0.7 dynamic-slice_bitcast_fusion
  132.0 0.7 copy.51.refs_10_
  132.7 0.0 copy-done
  132.7 0.1 copy.49
  132.8 0.6 pad.29.refs_14_
  133.4 0.0 copy-done.4
  133.4 0.0 copy-done.1
  133.4 0.0 copy-done.2
  133.4 0.0 copy-done.3
  133.5 0.6 select_maximum_fusion.refs_12_
  134.1 117.9 %tail.1 = (bf16[2,96,768]{2,1,0:T(8,128)(2,1)}, bf16[2,96,768]{2,1,0:T(8,128)(2,1)}, bf16[2,96,768]{2,1,0:T(8,128)(2,1)}, bf16[2,192,512]{2,1,0:T(8,128)(2,1)}, ...) custom-call(bf16[4,4,2,96,768]{4,3,2,1,0:T(8,128)(2,1)} %bitcast.41, bf16[4,4,2,96,768]{4,3,2,1,0:T(8,128)(2,1)} %bitcast.42, ...), custom_call_target="tpu_custom_call" | custom-call | tf_op jit(solution)/shard_map/tail/pallas_call | solution.py:1563
  252.0 3.4 %finish.1 = (f32[192,576]{1,0:T(8,128)}, f32[192,192]{1,0:T(8,128)}, f32[192,768]{1,0:T(8,128)}, f32[192,768]{1,0:T(8,128)}, f32[2,192,512]{2,1,0:T(8,128)}, /*i...) custom-call(bf16[2,96,768]{2,1,0:T(8,128)(2,1)} %get-tuple-element.1, ...), custom_call_target="tpu_custom_call" | custom-call | tf_op jit(solution)/shard_map/finish/pallas_call | solution.py:1663
  255.4 1.5 copy.53
  256.9 1.3 copy.52
  258.2 1.3 reduce
  259.5 1.8 copy.58
  (5 shorter events, 0.0 us)
Async XLA Ops:
  112.6 20.1 %copy-start = (f32[128,14]{0,1:T(8,128)S(1)}, f32[128,14]{0,1:T(8,128)}, u32[]{:S(2)}) copy-start(f32[128,14]{0,1:T(8,128)} %param.44) | copy-start | bytes 21508
  112.6 20.9 %copy-start.4 = (f32[14]{0:T(128)S(1)}, f32[14]{0:T(128)}, u32[]{:S(2)}) copy-start(f32[14]{0:T(128)} %param.45) | copy-start | bytes 172
  112.6 20.8 %copy-start.1 = (f32[128]{0:T(128)S(1)}, f32[128]{0:T(128)}, u32[]{:S(2)}) copy-start(f32[128]{0:T(128)} %param.43) | copy-start | bytes 1540
  112.6 20.8 %copy-start.2 = (f32[128]{0:T(128)S(1)}, f32[128]{0:T(128)}, u32[]{:S(2)}) copy-start(f32[128]{0:T(128)} %param.41) | copy-start | bytes 1540
  112.6 20.8 %copy-start.3 = (f32[128]{0:T(128)S(1)}, f32[128]{0:T(128)}, u32[]{:S(2)}) copy-start(f32[128]{0:T(128)} %param.40) | copy-start | bytes 1540

commit v5 on v4

--- a/solution.py
+++ b/solution.py
@@ -600,7 +600,7 @@
         pass_p(k, at, 2).start()
 
     steps = [(0, 0)] + [(way, hop) for hop in (1, 2, 3) for way in (0, 1)]
-    jobs = [(k, way, hop) for k in range(kinds) for way, hop in steps]
+    jobs = [(group, way, hop) for group in ((0, 1), (2,), (3,)) for way, hop in steps]
 
     def at_of(way, hop):
         return c - hop if way == 0 else c + hop
@@ -614,30 +614,36 @@
         else:
             pl.when(valid(way, hop))(body)
 
-    def first(k, way, hop):
+    def first(group, way, hop):
         def body():
             at = at_of(way, hop)
-            if hop:
-                z_send(k, at, way, hop).wait_recv()
-                if hop < 3:
-                    can = has_up if way == 0 else has_down
-
-                    @pl.when(can)
-                    def _():
-                        z_send(k, at, way, hop + 1).start()
-
-            spread(k, at, hop == 0)
+            for k in group:
+                if hop:
+                    z_send(k, at, way, hop).wait_recv()
+                    if hop < 3:
+                        can = has_up if way == 0 else has_down
+
+                        @pl.when(can)
+                        def _():
+                            z_send(k, at, way, hop + 1).start()
+
+                spread(k, at, hop == 0)
 
         guard(way, hop, body)
 
-    def second(k, way, hop):
-        guard(way, hop, lambda: onward(k, at_of(way, hop)))
-
-    def third(k, way, hop):
+    def second(group, way, hop):
+        def body():
+            for k in group:
+                onward(k, at_of(way, hop))
+
+        guard(way, hop, body)
+
+    def third(group, way, hop):
         def body():
             at = at_of(way, hop)
-            got_corner(k, at)
-            pass_p(k, at, 3).start()
+            for k in group:
+                got_corner(k, at)
+                pass_p(k, at, 3).start()
 
         guard(way, hop, body)
 
@@ -776,7 +782,7 @@
 
     wide = q_src.shape[1]
     lag = 3
-    ready = 2 * len(steps) + 2 * lag
+    ready = len(steps) + 2 * lag
 
     def do(**stages):
         for stage, numbers in stages.items():
@@ -784,38 +790,39 @@
                 {"f": first, "s": second, "t": third}[stage](*jobs[n])
 
     for i in range(ready):
+        if i == ready - 4:
+            set_out(kinds - 1)
         do(f=[i], s=[i - lag] if i >= lag else [], t=[i - 2 * lag] if i >= 2 * lag else [])
     prepare()
     settle(0)
     settle(1)
     project(3)
-    do(f=[20], s=[17], t=[14])
+    do(f=[13], s=[10], t=[7])
     project(2)
-    do(f=[21], s=[18], t=[15])
+    do(f=[14], s=[11], t=[8])
     project(1)
-    do(s=[19], t=[16])
+    do(s=[12], t=[9])
     project(0)
-    set_out(kinds - 1)
-    do(s=[20], t=[17])
+    do(s=[13], t=[10])
     for start, _ in late_moves:
         start()
     for at in range(3):
         spread_out(at)
-        do(t=[18 + at])
+        do(t=[11 + at])
     spread_out(3)
-    do(s=[21])
+    do(s=[14])
     unpack()
     collect()
     attend(3)
-    do(f=[22, 23])
+    do(f=[15, 16])
     attend(2)
-    do(f=[24, 25], s=[22])
+    do(f=[17, 18], s=[15])
     attend(1)
-    do(f=[26, 27], s=[23], t=[21])
+    do(f=[19, 20], s=[16], t=[14])
     attend(0)
-    for n in (24, 25, 26, 27):
+    for n in (17, 18, 19, 20):
         do(s=[n], t=[n - 2])
-    do(t=[26, 27])
+    do(t=[19, 20])
 
     for k in range(kinds):
         if k > 1:
@@ -1516,7 +1523,7 @@
 
         start()
 
-    gap = 3
+    gap = 1
     hooks = [[] for _ in range(max(8 + gap + 5, 8 + len(steps)))]
     hooks[0].append(prepare)
     for i, j in enumerate((3, 2, 1, 0)):

time: 262 us -> 250 us (0.954)
  Pallas kernels: 247 us -> 233 us
    pallas_call x1, Pallas kernels: 118 us -> 108 us  [tail_fast(): pl.pallas_call(functools.partial(tail_kernel, docs, classes, scale), out_...]
    pallas_call x1, Pallas kernels: 109 us -> 105 us  [head_fast(): pl.pallas_call(functools.partial(head_kernel, scale), out_shape=[shape((4...]
where the time goes in v5:
time: 250 us; the launch traced here: 248 us
  Pallas kernels  233 us (93%)
  local copies, waits for them, and re-layouts  11.6 us (5%)
    pallas_call x1, Pallas kernels, tail_fast(): pl.pallas_call(functools.partial(tail_kernel, docs, classes, scale), out_...  108 us
    pallas_call x1, Pallas kernels, head_fast(): pl.pallas_call(functools.partial(head_kernel, scale), out_shape=[shape((4...  105 us
    pallas_call x1, Pallas kernels, dense_fast(): pl.pallas_call(dense_kernel, out_shape=[weight, weight, shape(ctx.shape,...  17.1 us
    unnamed x15, local copies, waits for them, and re-layouts  5.43 us

profile of v5, /device:TPU:0, one launch (start us, length us, event | category | flops | bytes accessed | tf_op | source)
XLA Modules:
  0.0 247.6 jit_solution(1933937855553868853)
XLA Ops:
  0.7 0.7 copy.56
  1.4 0.7 pad.24
  2.1 0.6 pad.25.refs_6_
  2.7 1.3 broadcast_in_dim.31.refs_8_
  4.0 105.2 %head.1 = (bf16[4,4,2,96,768]{4,3,2,1,0:T(8,128)(2,1)}, bf16[4,4,2,96,768]{4,3,2,1,0:T(8,128)(2,1)}, bf16[4,4,2,96,768]{4,3,2,1,0:T(8,128)(2,1)}, bf16[4,192,256...) custom-call(bf16[192,576]{1,0:T(8,128)(2,1)} %refs_0_.1, ...), custom_call_target="tpu_custom_call" | custom-call | tf_op jit(solution)/shard_map/head/pallas_call | solution.py:889
  109.1 0.0 copy-start
  109.1 0.0 copy-start.4
  109.2 0.0 copy-start.1
  109.2 0.0 copy-start.2
  109.2 0.0 copy-start.3
  109.2 17.1 %dense.1 = (bf16[4,768,768]{2,1,0:T(8,128)(2,1)}, bf16[4,768,768]{2,1,0:T(8,128)(2,1)}, bf16[4,192,256]{2,1,0:T(8,128)(2,1)}, bf16[256,768]{1,0:T(8,128)(2,1)}, ...) custom-call(bf16[4,192,256]{2,1,0:T(8,128)(2,1)} %get-tuple-element., ...), custom_call_target="tpu_custom_call" | custom-call | tf_op jit(solution)/shard_map/dense/pallas_call | solution.py:1806
  126.3 0.7 dynamic-slice_bitcast_fusion.1
  127.0 0.8 copy.50.refs_9_
  127.8 0.7 dynamic-slice_bitcast_fusion
  128.6 0.7 copy.51.refs_10_
  129.2 0.0 copy-done
  129.2 0.1 copy.49
  129.4 0.6 pad.29.refs_14_
  130.0 0.0 copy-done.4
  130.0 0.0 copy-done.1
  130.0 0.0 copy-done.2
  130.0 0.0 copy-done.3
  130.0 0.6 select_maximum_fusion.refs_12_
  130.6 107.7 %tail.1 = (bf16[2,96,768]{2,1,0:T(8,128)(2,1)}, bf16[2,96,768]{2,1,0:T(8,128)(2,1)}, bf16[2,96,768]{2,1,0:T(8,128)(2,1)}, bf16[2,192,512]{2,1,0:T(8,128)(2,1)}, ...) custom-call(bf16[4,4,2,96,768]{4,3,2,1,0:T(8,128)(2,1)} %bitcast.41, bf16[4,4,2,96,768]{4,3,2,1,0:T(8,128)(2,1)} %bitcast.42, ...), custom_call_target="tpu_custom_call" | custom-call | tf_op jit(solution)/shard_map/tail/pallas_call | solution.py:1570
  238.3 3.4 %finish.1 = (f32[192,576]{1,0:T(8,128)}, f32[192,192]{1,0:T(8,128)}, f32[192,768]{1,0:T(8,128)}, f32[192,768]{1,0:T(8,128)}, f32[2,192,512]{2,1,0:T(8,128)}, /*i...) custom-call(bf16[2,96,768]{2,1,0:T(8,128)(2,1)} %get-tuple-element.1, ...), custom_call_target="tpu_custom_call" | custom-call | tf_op jit(solution)/shard_map/finish/pallas_call | solution.py:1670
  241.8 1.5 copy.53
  243.3 1.3 copy.52
  244.6 1.3 reduce
  245.8 1.8 copy.58
  (5 shorter events, 0.0 us)
Async XLA Ops:
  109.1 20.1 %copy-start = (f32[128,14]{0,1:T(8,128)S(1)}, f32[128,14]{0,1:T(8,128)}, u32[]{:S(2)}) copy-start(f32[128,14]{0,1:T(8,128)} %param.44) | copy-start | bytes 21508
  109.1 20.8 %copy-start.4 = (f32[14]{0:T(128)S(1)}, f32[14]{0:T(128)}, u32[]{:S(2)}) copy-start(f32[14]{0:T(128)} %param.45) | copy-start | bytes 172
  109.2 20.8 %copy-start.1 = (f32[128]{0:T(128)S(1)}, f32[128]{0:T(128)}, u32[]{:S(2)}) copy-start(f32[128]{0:T(128)} %param.43) | copy-start | bytes 1540
  109.2 20.8 %copy-start.2 = (f32[128]{0:T(128)S(1)}, f32[128]{0:T(128)}, u32[]{:S(2)}) copy-start(f32[128]{0:T(128)} %param.41) | copy-start | bytes 1540
  109.2 20.8 %copy-start.3 = (f32[128]{0:T(128)S(1)}, f32[128]{0:T(128)}, u32[]{:S(2)}) copy-start(f32[128]{0:T(128)} %param.40) | copy-start | bytes 1540
